TPU v7x, 32 devices: a whole 2x2x4 slice. The times are simulated.
32 devices in a mesh: fsdp: 8 (over y, x, core), tp: 4 (over z).
Axes of the slice: x: 2, y: 2, z: 4, core: 2. Of those that a mesh axis runs over, the one named last changes fastest.
Arguments:
- tokens: bfloat16 [8192, 1536], P(('fsdp', 'tp')), may hold values from -6 to 6
- cotangent: bfloat16 [8192, 1536], P(('fsdp', 'tp')), may hold values from -6 to 6
- seq_start: int32 [32], P('fsdp'), may hold values from 0 to 1, as said below
- token_valid: int32 [8192], P('fsdp'), may hold values from 0 to 1, as said below
- norm_gain: float32 [1536], replicated, may hold values from 0.5 to 1.5
- proj_z: bfloat16 [1536, 3072], P('fsdp', 'tp'), may hold values from -0.15625 to 0.15625
- proj_x: bfloat16 [1536, 3072], P('fsdp', 'tp'), may hold values from -0.15625 to 0.15625
- proj_bc: bfloat16 [1536, 256], P('fsdp'), may hold values from -0.15625 to 0.15625
- proj_dt: bfloat16 [1536, 48], P('fsdp', 'tp'), may hold values from -0.15625 to 0.15625
- conv_chan: float32 [4, 3072], P(None, 'tp'), may hold values from -3 to 3
- bias_chan: float32 [3072], P('tp'), may hold values from -0.5 to 0.5
- conv_shared: float32 [4, 256], replicated, may hold values from -3 to 3
- bias_shared: float32 [256], replicated, may hold values from -0.5 to 0.5
- a_log: float32 [48], P('tp'), may hold values from -1 to 1.5
- dt_bias: float32 [48], P('tp'), may hold values from -8 to -2
- skip_gain: float32 [48], P('tp'), may hold values from 0.5 to 1.5
- gate_gain: float32 [3072], P('tp'), may hold values from 0.5 to 1.5
- proj_out: bfloat16 [3072, 1536], P('tp', 'fsdp'), may hold values from -0.109375 to 0.109375
Outputs:
- output: bfloat16 [8192, 1536], P(('fsdp', 'tp'))
- grad_tokens: bfloat16 [8192, 1536], P(('fsdp', 'tp'))
- grad_norm_gain: float32 [1536], replicated
- grad_proj_z: float32 [1536, 3072], P('fsdp', 'tp')
- grad_proj_x: float32 [1536, 3072], P('fsdp', 'tp')
- grad_proj_bc: float32 [1536, 256], P('fsdp')
- grad_proj_dt: float32 [1536, 48], P('fsdp', 'tp')
- grad_conv_chan: float32 [4, 3072], P(None, 'tp')
- grad_bias_chan: float32 [3072], P('tp')
- grad_conv_shared: float32 [4, 256], replicated
- grad_bias_shared: float32 [256], replicated
- grad_a_log: float32 [48], P('tp')
- grad_dt_bias: float32 [48], P('tp')
- grad_skip_gain: float32 [48], P('tp')
- grad_gate_gain: float32 [3072], P('tp')
- grad_proj_out: float32 [3072, 1536], P('tp', 'fsdp')
Inputs may be any that keep to these rules, and one draw needn't show every extreme that they name: `seq_start`: each buffer of 4 blocks has 1 at its first block; a sequence spans 4 to min(15, 4) blocks and no sequence crosses a buffer; after a buffer's last sequence the flags are 0; some buffer is filled with sequences to its end. `token_valid`: within a sequence all tokens are 1 except between 0 and 127 tokens at the end of its last block; every token of the blocks after a buffer's last sequence is 0.
All inputs are finite; a program needn't handle non-finite values.
Results may differ from a plain program's by a relative error of at most 0.02.
Values may be sent and summed in bfloat16 or wider, within the bound.
A program may use at most 192 MiB of HBM per device.

v0:
```python
import jax
import jax.numpy as jnp
from jax import lax
from jax.sharding import PartitionSpec as P

HEAD = 64
STATE = 128
STRETCH = 256
INNER = 3072


EPSILON = 1e-05
PRECISE = lax.Precision.HIGHEST


def causal_conv(signal, kernel, offset_bias, openings):
    length = signal.shape[0]
    tap_count = kernel.shape[0]
    padded = jnp.concatenate(
        [jnp.zeros((tap_count - 1, signal.shape[1]), jnp.float32), signal], axis=0
    )
    within = jnp.arange(length) % STRETCH
    opening = jnp.repeat(openings, STRETCH)
    result = jnp.zeros_like(signal) + offset_bias[None, :]
    for tap_index in range(tap_count):
        reach_back = tap_count - 1 - tap_index
        allowed = 1.0 - opening * (within < reach_back).astype(jnp.float32)
        result = (
            result
            + allowed[:, None] * padded[tap_index : tap_index + length] * kernel[tap_index][None, :]
        )
    return jax.nn.silu(result)


def state_scan(inputs, step_rates, decay_a, shared_b, shared_c, openings):
    seq_len, head_count, head_size = inputs.shape
    block_count = seq_len // STRETCH
    blocks_x = inputs.reshape(block_count, STRETCH, head_count, head_size)
    blocks_dt = step_rates.reshape(block_count, STRETCH, head_count)
    blocks_b = shared_b.reshape(block_count, STRETCH, shared_b.shape[1])
    blocks_c = shared_c.reshape(block_count, STRETCH, shared_c.shape[1])
    log_decay = blocks_dt * decay_a[None, None, :]
    lower = (jnp.arange(STRETCH)[:, None] >= jnp.arange(STRETCH)[None, :]).astype(jnp.float32)
    cumulative = jnp.einsum("ts,csh->cth", lower, log_decay, precision=PRECISE)
    spread = cumulative[:, :, None, :] - cumulative[:, None, :, :]
    weights = jnp.exp(jnp.where(lower[None, :, :, None] > 0, spread, -1e30))
    intersection = jnp.einsum("ctn,csn->cts", blocks_c, blocks_b, precision=PRECISE)
    scaled_x = blocks_x * blocks_dt[..., None]
    within_block = jnp.einsum(
        "ctsh,cshp->cthp", weights * intersection[..., None], scaled_x, precision=PRECISE
    )
    to_end = jnp.exp(cumulative[:, -1:, :] - cumulative)
    block_states = jnp.einsum(
        "cshp,csn->chpn", scaled_x * to_end[..., None], blocks_b, precision=PRECISE
    )
    carry_decay = jnp.exp(cumulative[:, -1, :])

    def advance(carried, block_item):
        opening, factor, fresh_state = block_item
        entering = carried * (1.0 - opening)
        return (entering * factor[:, None, None] + fresh_state, entering)

    initial = jnp.zeros((head_count, head_size, blocks_b.shape[-1]), jnp.float32)
    _, entering = lax.scan(advance, initial, (openings, carry_decay, block_states))
    across_block = (
        jnp.einsum("ctn,chpn->cthp", blocks_c, entering, precision=PRECISE)
        * jnp.exp(cumulative)[..., None]
    )
    return (within_block + across_block).reshape(seq_len, head_count, head_size)


def gated_branch(
    pre_z,
    pre_x,
    pre_bc,
    pre_dt,
    conv_chan,
    bias_chan,
    conv_shared,
    bias_shared,
    a_log,
    dt_bias,
    skip_gain,
    validity,
    openings,
):
    length = pre_x.shape[0]
    head_count = pre_dt.shape[1]
    features = causal_conv(pre_x, conv_chan, bias_chan, openings)
    shared = causal_conv(pre_bc, conv_shared, bias_shared, openings)
    step_rates = jax.nn.softplus(pre_dt + dt_bias[None, :]) * validity[:, None]
    decay_a = -jnp.exp(a_log)
    heads_x = features.reshape(length, head_count, HEAD)
    mixed_out = state_scan(
        heads_x, step_rates, decay_a, shared[:, :STATE], shared[:, STATE:], openings
    )
    mixed_out = mixed_out + skip_gain[None, :, None] * heads_x
    return mixed_out.reshape(length, head_count * HEAD) * jax.nn.silu(pre_z) * validity[:, None]


def shards(
    tokens,
    cotangent,
    seq_start,
    token_valid,
    norm_gain,
    proj_z,
    proj_x,
    proj_bc,
    proj_dt,
    conv_chan,
    bias_chan,
    conv_shared,
    bias_shared,
    a_log,
    dt_bias,
    skip_gain,
    gate_gain,
    proj_out,
):
    validity = token_valid.astype(jnp.float32)
    openings = seq_start.astype(jnp.float32)
    whole_z, whole_x, whole_bc, whole_dt, whole_out = (
        lax.all_gather(proj_z, "fsdp", axis=0, tiled=True),
        lax.all_gather(proj_x, "fsdp", axis=0, tiled=True),
        lax.all_gather(proj_bc, "fsdp", axis=0, tiled=True),
        lax.all_gather(proj_dt, "fsdp", axis=0, tiled=True),
        lax.all_gather(proj_out, "fsdp", axis=1, tiled=True),
    )
    resid = tokens.astype(jnp.float32)
    rstd = lax.rsqrt(jnp.mean(resid * resid, axis=1, keepdims=True) + EPSILON)
    normed = (resid * rstd * norm_gain[None, :]).astype(jnp.bfloat16)
    normed_all = lax.all_gather(normed, "tp", axis=0, tiled=True)
    pre_z = jnp.dot(normed_all, whole_z, preferred_element_type=jnp.float32)
    pre_x = jnp.dot(normed_all, whole_x, preferred_element_type=jnp.float32)
    pre_bc = jnp.dot(normed_all, whole_bc, preferred_element_type=jnp.float32)
    pre_dt = jnp.dot(normed_all, whole_dt, preferred_element_type=jnp.float32)

    def mixer(
        in_z,
        in_x,
        in_bc,
        in_dt,
        taps_chan,
        offset_chan,
        taps_shared,
        offset_shared,
        log_rate,
        step_bias,
        direct_gain,
    ):
        return gated_branch(
            in_z,
            in_x,
            in_bc,
            in_dt,
            taps_chan,
            offset_chan,
            taps_shared,
            offset_shared,
            log_rate,
            step_bias,
            direct_gain,
            validity,
            openings,
        )

    gated, mixer_back = jax.vjp(
        mixer,
        pre_z,
        pre_x,
        pre_bc,
        pre_dt,
        conv_chan,
        bias_chan,
        conv_shared,
        bias_shared,
        a_log,
        dt_bias,
        skip_gain,
    )
    squares = lax.psum(jnp.sum(gated * gated, axis=1), "tp")
    gate_rstd = lax.rsqrt(squares / INNER + EPSILON)[:, None]
    gnormed = (gated * gate_rstd * gate_gain[None, :]).astype(jnp.bfloat16)
    mixed = lax.psum_scatter(
        jnp.dot(gnormed, whole_out, preferred_element_type=jnp.float32).astype(jnp.bfloat16),
        "tp",
        scatter_dimension=0,
        tiled=True,
    ).astype(jnp.float32)
    cot_all = lax.all_gather(cotangent, "tp", axis=0, tiled=True)
    d_gnormed = jnp.einsum("td,cd->tc", cot_all, whole_out, preferred_element_type=jnp.float32)
    grad_out_rows = jnp.einsum("tc,td->cd", gnormed, cot_all, preferred_element_type=jnp.float32)
    output = (resid + mixed).astype(jnp.bfloat16)
    scaled = gate_gain[None, :] * d_gnormed
    d_gate_gain = jnp.sum(d_gnormed * gated * gate_rstd, axis=0)
    cross = lax.psum(jnp.sum(scaled * gated, axis=1), "tp")
    d_gated = (
        gate_rstd * scaled - gated * (gate_rstd * gate_rstd * gate_rstd) * (cross / INNER)[:, None]
    )
    grads = mixer_back(d_gated)
    grad_z = grads[0].astype(jnp.bfloat16)
    grad_x = grads[1].astype(jnp.bfloat16)
    grad_bc = grads[2].astype(jnp.bfloat16)
    grad_dt = grads[3].astype(jnp.bfloat16)
    weight_z = jnp.einsum("td,tc->dc", normed_all, grad_z, preferred_element_type=jnp.float32)
    weight_x = jnp.einsum("td,tc->dc", normed_all, grad_x, preferred_element_type=jnp.float32)
    weight_bc = jnp.einsum("td,tc->dc", normed_all, grad_bc, preferred_element_type=jnp.float32)
    weight_dt = jnp.einsum("td,tc->dc", normed_all, grad_dt, preferred_element_type=jnp.float32)

    def partial_term(grad_rows, weight_full):
        return jnp.einsum("tc,dc->td", grad_rows, weight_full, preferred_element_type=jnp.float32)

    d_normed = lax.psum_scatter(
        (
            partial_term(grad_z, whole_z)
            + partial_term(grad_x, whole_x)
            + partial_term(grad_bc, whole_bc)
            + partial_term(grad_dt, whole_dt)
        ).astype(jnp.bfloat16),
        "tp",
        scatter_dimension=0,
        tiled=True,
    ).astype(jnp.float32)
    owned_z, owned_x, owned_bc, owned_dt, owned_out = (
        lax.psum_scatter(
            weight_z.astype(jnp.bfloat16), "fsdp", scatter_dimension=0, tiled=True
        ).astype(jnp.float32),
        lax.psum_scatter(
            weight_x.astype(jnp.bfloat16), "fsdp", scatter_dimension=0, tiled=True
        ).astype(jnp.float32),
        lax.psum_scatter(
            weight_bc.astype(jnp.bfloat16), "fsdp", scatter_dimension=0, tiled=True
        ).astype(jnp.float32),
        lax.psum_scatter(
            weight_dt.astype(jnp.bfloat16), "fsdp", scatter_dimension=0, tiled=True
        ).astype(jnp.float32),
        lax.psum_scatter(
            grad_out_rows.astype(jnp.bfloat16), "fsdp", scatter_dimension=1, tiled=True
        ).astype(jnp.float32),
    )
    d_norm_gain = jnp.sum(d_normed * resid * rstd, axis=0)
    scaled_in = d_normed * norm_gain[None, :]
    d_resid = rstd * scaled_in - resid * (rstd * rstd * rstd) * jnp.mean(
        scaled_in * resid, axis=1, keepdims=True
    )
    grad_tokens = (d_resid + cotangent.astype(jnp.float32)).astype(jnp.bfloat16)
    summed = lax.psum(
        (
            grads[4],
            grads[5],
            grads[6],
            grads[7],
            grads[8],
            grads[9],
            grads[10],
            d_gate_gain,
            d_norm_gain,
        ),
        "fsdp",
    )
    shared_sums = (
        lax.psum(owned_bc.astype(jnp.bfloat16), "tp").astype(jnp.float32),
        lax.psum(summed[2].astype(jnp.bfloat16), "tp").astype(jnp.float32),
        lax.psum(summed[3].astype(jnp.bfloat16), "tp").astype(jnp.float32),
        lax.psum(summed[8].astype(jnp.bfloat16), "tp").astype(jnp.float32),
    )
    return (
        output,
        grad_tokens,
        shared_sums[3],
        owned_z,
        owned_x,
        shared_sums[0],
        owned_dt,
        summed[0],
        summed[1],
        shared_sums[1],
        shared_sums[2],
        summed[4],
        summed[5],
        summed[6],
        summed[7],
        owned_out,
    )


def solution(mesh):
    in_specs = (
        P(("fsdp", "tp"), None),
        P(("fsdp", "tp"), None),
        P("fsdp"),
        P("fsdp"),
        P(),
        P("fsdp", "tp"),
        P("fsdp", "tp"),
        P("fsdp", None),
        P("fsdp", "tp"),
        P(None, "tp"),
        P("tp"),
        P(),
        P(),
        P("tp"),
        P("tp"),
        P("tp"),
        P("tp"),
        P("tp", "fsdp"),
    )
    out_specs = (
        P(("fsdp", "tp"), None),
        P(("fsdp", "tp"), None),
        P(),
        P("fsdp", "tp"),
        P("fsdp", "tp"),
        P("fsdp", None),
        P("fsdp", "tp"),
        P(None, "tp"),
        P("tp"),
        P(),
        P(),
        P("tp"),
        P("tp"),
        P("tp"),
        P("tp"),
        P("tp", "fsdp"),
    )
    return jax.shard_map(shards, mesh=mesh, in_specs=in_specs, out_specs=out_specs, check_vma=False)
```

profile of v0, /device:TPU:9, one launch (start us, length us, event | category | flops | bytes accessed | tf_op | source)
XLA Modules:
  0.0 747.8 jit_solution(2506165639398660441)
XLA Ops:
  16.0 9.8 %all-gather = bf16[8,192,12]{1,2,0:T(8,128)(2,1)S(1)} all-gather(bf16[1,192,12]{1,2,0:T(8,128)(2,1)S(1)} %bitcast.207), channel_id=1, replica_groups=mesh['fsdp'=8,'tp'=4] {'fsdp'}, dimensions={0}, use_global_device_ids=true | all-gather | bytes 41472 | tf_op jit(solution)/shard_map/all_gather | solution.py:127
  25.9 10.4 %all_gather.24 = bf16[1536,256]{1,0:T(8,128)(2,1)S(1)} all-gather(bf16[192,256]{1,0:T(8,128)(2,1)S(1)} %copy-done.48), channel_id=1, replica_groups=mesh['fsdp'=8,'tp'=4] {'fsdp'}, dimensions={0}, use_global_device_ids=true | all-gather | bytes 884736 | tf_op jit(solution)/shard_map/all_gather | solution.py:126
  36.3 38.1 %all-gather.7.cloned.1.call-done = bf16[1024,1536]{1,0:T(8,128)(2,1)} async-done(((bf16[256,1536]{1,0:T(8,128)(2,1)}), bf16[1024,1536]{1,0:T(8,128)(2,1)}) %all-gather.7.cloned.1.call-update) | async-done | bytes 3145744 | tf_op jit(solution)/shard_map/all_gather | solution.py:133
  74.4 3.4 fusion.95
  78.5 2.9 fusion.121
  83.5 23.2 %all-gather.9.cloned.1.call-done = bf16[1536,768]{1,0:T(8,128)(2,1)} async-done(((bf16[192,768]{1,0:T(8,128)(2,1)}), bf16[1536,768]{1,0:T(8,128)(2,1)}) %all-gather.9.cloned.1.call-update) | async-done | bytes 2359312 | tf_op jit(solution)/shard_map/all_gather | solution.py:125
  106.7 5.2 fusion.120
  112.0 4.7 fusion.32
  116.7 3.6 copy.88
  120.3 5.1 reshape.258
  127.4 6.3 fusion.38
  133.9 15.0 %while.36 = (s32[]{:T(128)}, f32[12,64,128]{2,1,0:T(8,128)S(1)}, f32[4,12,64,128]{3,2,1,0:T(8,128)S(1)}, f32[4]{0:T(128)S(1)}, f32[4,12,1,1]{1,3,2,0:T(1,128)}, ...) while((s32[]{:T(128)}, f32[12,64,128]{2,1,0:T(8,128)S(1)}, ...), condition=%wide.region_2.3_spmd.clone, body=%wide.region_1.2_spmd.clone.sunk | while | flops 589828 | bytes 1967464 | solution.py:64
  151.7 14.0 %bitcast_add_fusion.3 = f32[4,256,12,64]{1,3,2,0:T(8,128)S(1)} fusion(f32[4,256,12,64]{1,3,2,0:T(8,128)S(1)} %fusion.123, f32[4,256,256]{2,1,0:T(8,128)S(1)} %copy-done.31, f32[4,256,12]{1,2,0:T(8,128)S(1)} %convolution_bitcast_fusion.1, pred[256,256]{1,0:T(8,128)(4,1)S(1)} %convert_compare_fusion, f32[4,256,12,64]{1,0,3,2:T(4,128)S(1)} %copy-done.6, ...), kind=kOutput, calls=%fused_computation.59 | convolution fusion | flops 2427715584 | bytes 10698752 | tf_op jit(solution)/shard_map/jvp(ctsh,cshp->cthp)/dot_general | solution.py:49
  170.2 3.7 copy.94
  173.8 8.9 %multiply_reduce_fusion.10 = (f32[1024]{0:T(1024)}, f32[1024,768]{1,0:T(8,128)}, f32[1024,768]{1,0:T(8,128)}) fusion(f32[1024]{0:T(1024)S(1)} %convert_element_type.114, f32[1024,768]{1,0:T(8,128)} %copy.94, f32[1024,768]{1,0:T(8,128)} %get-tuple-element.356, f32[768]{0:T(1024)} %mul.780, bf16[1024,1536]{1,0:T(8,128)(2,1)S(1)} %copy-done.1, ...), kind=kOutput, calls=%fused_computation.76 | convolution fusion | flops 2426928128 | bytes 18099200 | tf_op jit(solution)/shard_map/dot_general | solution.py:134
  182.8 7.9 %psum.105 = f32[1024]{0:T(1024)S(1)} all-reduce(f32[1024]{0:T(1024)} %get-tuple-element.353), channel_id=1, replica_groups=mesh['fsdp'=8,'tp'=4] {'tp'}, use_global_device_ids=true, to_apply=%region_4.5 | all-reduce | flops 1024 | bytes 8192 | tf_op jit(solution)/shard_map/psum | solution.py:182
  191.3 39.1 %all-gather.15.cloned.1.call-done = bf16[1024,1536]{1,0:T(8,128)(2,1)} async-done(((bf16[256,1536]{1,0:T(8,128)(2,1)}), bf16[1024,1536]{1,0:T(8,128)(2,1)}) %all-gather.15.cloned.1.call-update) | async-done | bytes 3145744 | tf_op jit(solution)/shard_map/all_gather | solution.py:191
  230.4 8.7 %multiply_reduce_fusion = (f32[768]{0:T(1024)}, f32[1024]{0:T(1024)}, f32[1024,768]{1,0:T(8,128)}) fusion(f32[1024,768]{1,0:T(8,128)} %get-tuple-element.354, f32[1024]{0:T(1024)} %get-tuple-element.382, f32[768]{0:T(1024)} %param.38, bf16[1024,1536]{1,0:T(8,128)(2,1)} %all-gather.15.cloned.1.call-done, bf16[768,1536]{0,1:T(8,128)(2,1)} %all-gather.13.cloned.1.call-done), kind=kOutput, calls=%fused_computation.60 | convolution fusion | flops 2420635904 | bytes 11810816 | tf_op jit(solution)/shard_map/td,cd->tc/dot_general | solution.py:192
  239.1 10.1 %psum.106 = f32[1024]{0:T(1024)} all-reduce(f32[1024]{0:T(1024)} %get-tuple-element.284), channel_id=1, replica_groups=mesh['fsdp'=8,'tp'=4] {'tp'}, use_global_device_ids=true, to_apply=%region_7.8 | all-reduce | flops 1024 | bytes 8192 | tf_op jit(solution)/shard_map/psum | solution.py:197
  249.9 8.4 %multiply_reduce_fusion.1 = (f32[768]{0:T(1024)}, f32[1024,768]{1,0:T(8,128)}, bf16[1024,768]{1,0:T(8,128)(2,1)}) fusion(f32[1024,768]{1,0:T(8,128)S(1)} %copy-done.5, f32[1024,768]{1,0:T(8,128)} %get-tuple-element.395, f32[1024]{0:T(1024)S(1)} %convert_element_type.114, f32[1024]{0:T(1024)S(1)} %broadcast_multiply_fusion.1, ...), kind=kLoop, calls=%fused_computation.61 | loop fusion | flops 21232896 | bytes 20472832 | tf_op jit(solution)/shard_map/transpose(jvp())/reduce_sum | solution.py:97
  258.2 3.6 copy.95
  261.8 3.4 reshape.262
  265.3 7.5 %fusion.69 = f32[4,256,128]{2,1,0:T(8,128)} fusion(f32[4,12,64,128]{3,2,1,0:T(8,128)} %copy-done, f32[4,256,12,64]{1,0,3,2:T(4,128)S(1)} %reshape.262, f32[4,256,12]{1,2,0:T(8,128)} %copy-done.38), kind=kOutput, calls=%fused_computation.126 | convolution fusion | flops 1208745984 | bytes 5292032 | tf_op jit(solution)/shard_map/transpose(jvp(ctn,chpn->cthp))/dot_general | solution.py:66
  272.8 4.3 fusion.41
  279.1 26.1 %while.37 = (s32[]{:T(128)}, f32[12,64,128]{2,1,0:T(8,128)S(1)}, f32[4,12]{1,0:T(4,128)}, f32[4,12,64,128]{3,2,1,0:T(8,128)}, f32[4,12,64,128]{3,2,1,0:T(8,128)}...) while((s32[]{:T(128)}, f32[12,64,128]{2,1,0:T(8,128)S(1)}, ...), condition=%wide.region_10.11_spmd.clone, body=%wide.region_8.10_spmd.clone.sunk | while | flops 688120 | bytes 2359756 | solution.py:64
  305.2 8.6 %fusion.70 = f32[4,256,128]{2,1,0:T(8,128)} fusion(f32[4,12,64,128]{3,2,1,0:T(8,128)} %get-tuple-element.224, f32[4,256,12,64]{1,0,3,2:T(4,128)} %reshape.258, f32[4,256,12]{1,2,0:T(8,128)} %copy-done.24, f32[4,256,12]{1,2,0:T(8,128)} %copy-done.36), kind=kOutput, calls=%fused_computation.127 | convolution fusion | flops 1209532416 | bytes 5341184 | tf_op jit(solution)/shard_map/transpose(jvp(cshp,csn->chpn))/dot_general | solution.py:53
  313.8 4.4 fusion.125
  318.2 18.6 %fusion.14 = (f32[4,256,12]{1,2,0:T(8,128)}, f32[4,256,12]{1,2,0:T(8,128)}, f32[4,256,256]{2,1,0:T(8,128)}) fusion(f32[4,256,256]{2,1,0:T(8,128)S(1)} %copy-done.32, f32[4,256,12]{1,2,0:T(8,128)S(1)} %copy-done.35, pred[256,256]{1,0:T(8,128)(4,1)S(1)} %copy-done.54, f32[4,256,12,64]{1,0,3,2:T(4,128)S(1)} %copy-done.7, f32[4,256,12]{1,2,0:T(8,128)S(1)} %copy-done.37, ...), kind=kOutput, calls=%fused_computation.25 | convolution fusion | flops 2444730368 | bytes 8650752 | tf_op jit(solution)/shard_map/transpose(jvp(ctsh,cshp->cthp))/dot_general | solution.py:49
  340.4 3.4 convolution_add_fusion
  343.8 14.3 %multiply_reduce_fusion.6 = (f32[4,256,12]{1,2,0:T(8,128)S(1)}, f32[4,256,12]{1,2,0:T(8,128)}, f32[4,256,12,64]{1,3,2,0:T(8,128)}) fusion(f32[4,256,12,64]{1,3,2,0:T(8,128)} %fusion.125, f32[4,256,12,64]{1,0,3,2:T(4,128)S(1)} %copy-done.8, f32[4,256,12]{1,2,0:T(8,128)S(1)} %copy-done.37, f32[4,256,256]{2,1,0:T(8,128)S(1)} %copy-done.33, ...), kind=kOutput, calls=%fused_computation.66 | convolution fusion | flops 2431623168 | bytes 13942784 | tf_op jit(solution)/shard_map/transpose(jvp(ctsh,cshp->cthp))/dot_general | solution.py:49
  366.0 2.9 multiply_reduce_fusion.7
  371.2 29.7 %reduce-scatter.18.cloned.1.call-done = bf16[192,256]{1,0:T(8,128)(2,1)} async-done(((bf16[1536,256]{1,0:T(8,128)(2,1)}), bf16[192,256]{1,0:T(8,128)(2,1)}) %reduce-scatter.18.cloned.1.call-update) | async-done | bytes 98320 | tf_op jit(solution)/shard_map/reduce_scatter | solution.py:232
  401.2 7.2 convolution_convert_fusion.1
  408.5 5.4 convolution_convert_fusion.3
  414.0 4.0 copy.98
  420.4 3.5 copy.99
  424.0 10.0 %multiply_reduce_fusion.5 = (f32[768]{0:T(1024)S(1)}, f32[768]{0:T(1024)S(1)}, f32[768]{0:T(1024)S(1)}, f32[768]{0:T(1024)S(1)}, f32[768]{0:T(1024)S(1)}, /*index=5*/f32[1024,768]{1,0:T(8,128)S(1)}) fusion(f32[1024,768]{1,0:T(8,128)} %copy-done.14, f32[1024]{0:T(1024)S(1)} %get-tuple-element.384, f32[1024]{0:T(1024)S(1)} %get-tuple-element.383, ...), kind=kLoop, calls=%fused_computation.65 | loop fusion | flops 18870528 | bytes 15763456 | tf_op jit(solution)/shard_map/transpose(jvp())/reduce_sum | solution.py:30
  437.4 4.0 convolution_convert_fusion.2
  454.1 5.9 convolution_convert_fusion
  462.6 11.1 %all-reduce.26.cloned.1.call-done = bf16[192,256]{1,0:T(8,128)(2,1)} async-done(((bf16[192,256]{1,0:T(8,128)(2,1)}), bf16[192,256]{1,0:T(8,128)(2,1)}) %all-reduce.26.cloned.1.call-update) | async-done | bytes 98320 | tf_op jit(solution)/shard_map/psum | solution.py:263
  475.2 45.8 %reduce-scatter.20.cloned.1.call-done = bf16[768,192]{0,1:T(8,128)(2,1)} async-done(((bf16[768,1536]{0,1:T(8,128)(2,1)}), bf16[768,192]{0,1:T(8,128)(2,1)}) %reduce-scatter.20.cloned.1.call-update) | async-done | bytes 294928 | tf_op jit(solution)/shard_map/reduce_scatter | solution.py:238
  522.9 43.8 %reduce-scatter.14.cloned.1.call-done = bf16[192,768]{1,0:T(8,128)(2,1)} async-done(((bf16[1536,768]{1,0:T(8,128)(2,1)}), bf16[192,768]{1,0:T(8,128)(2,1)}) %reduce-scatter.14.cloned.1.call-update) | async-done | bytes 294928 | tf_op jit(solution)/shard_map/reduce_scatter | solution.py:226
  568.5 43.9 %reduce-scatter.16.cloned.1.call-done = bf16[192,768]{1,0:T(8,128)(2,1)} async-done(((bf16[1536,768]{1,0:T(8,128)(2,1)}), bf16[192,768]{1,0:T(8,128)(2,1)}) %reduce-scatter.16.cloned.1.call-update) | async-done | bytes 294928 | tf_op jit(solution)/shard_map/reduce_scatter | solution.py:229
  614.2 60.2 %reduce-scatter.12.cloned.1.call-done = bf16[256,1536]{1,0:T(8,128)(2,1)} async-done(((bf16[1024,1536]{1,0:T(8,128)(2,1)}), bf16[256,1536]{1,0:T(8,128)(2,1)}) %reduce-scatter.12.cloned.1.call-update) | async-done | bytes 786448 | tf_op jit(solution)/shard_map/reduce_scatter | solution.py:214
  676.1 22.6 %all-reduce.22 = (bf16[1536]{0:T(1024)(128)(2,1)S(1)}, f32[4,768]{1,0:T(4,128)}, f32[768]{0:T(1024)}, bf16[4,256]{1,0:T(4,128)(2,1)S(1)}, bf16[256]{0:T(256)(128...) all-reduce(f32[1536]{0:T(1024)S(1)} %get-tuple-element.296, ...), channel_id=1, replica_groups=mesh['fsdp'=8,'tp'=4] {'fsdp'}, use_global_device_ids=true, to_apply=%region_21.22 | all-reduce | flops 7460 | bytes 54048 | tf_op jit(solution)/shard_map/psum | solution.py:248
  698.7 9.0 %all-reduce.23 = (bf16[1536]{0:T(1024)(128)(2,1)S(1)}, bf16[4,256]{1,0:T(4,128)(2,1)S(1)}, bf16[256]{0:T(256)(128)(2,1)S(1)}) all-reduce(bf16[1536]{0:T(1024)(128)(2,1)S(1)} %get-tuple-element.335, bf16[4,256]{1,0:T(4,128)(2,1)S(1)} %get-tuple-element.338, ...), channel_id=1, replica_groups=mesh['fsdp'=8,'tp'=4] {'tp'}, use_global_device_ids=true, to_apply=%region_22.23 | all-reduce | flops 2816 | bytes 11264 | tf_op jit(solution)/shard_map/psum | solution.py:266
  709.4 28.3 %reduce-scatter.10.cloned.1.call-done = bf16[256,1536]{1,0:T(8,128)(2,1)} async-done(((bf16[1024,1536]{1,0:T(8,128)(2,1)}), bf16[256,1536]{1,0:T(8,128)(2,1)}) %reduce-scatter.10.cloned.1.call-update) | async-done | bytes 786448 | tf_op jit(solution)/shard_map/reduce_scatter | solution.py:185
  737.7 3.2 fusion.51
  (355 shorter events, 108.8 us)
Async XLA Ops:
  7.3 18.6 %copy-start.48 = (bf16[192,256]{1,0:T(8,128)(2,1)S(1)}, bf16[192,256]{1,0:T(8,128)(2,1)}, u32[]{:S(2)}) copy-start(bf16[192,256]{1,0:T(8,128)(2,1)} %param.29) | copy-start | bytes 294916
  7.3 67.1 %copy-start.94 = (f32[12]{0:T(128)S(1)}, f32[12]{0:T(128)}, u32[]{:S(2)}) copy-start(f32[12]{0:T(128)} %param.36) | copy-start | bytes 148
  7.3 67.1 %all-gather.7.cloned.1.call-start = ((), (), s32[]{:S(2)}) async-start(), calls=%async_computation.7 | async-start | bytes 3932160 | tf_op jit(solution)/shard_map/all_gather | solution.py:133
  12.1 94.6 %all-gather.9.cloned.1.call-start = ((), (), s32[]{:S(2)}) async-start(), calls=%async_computation.8 | async-start | bytes 2654208 | tf_op jit(solution)/shard_map/all_gather | solution.py:125
  12.9 161.0 %all-gather.11.cloned.1.call-start = ((), (), s32[]{:S(2)}) async-start(), calls=%async_computation.9 | async-start | bytes 2654208 | tf_op jit(solution)/shard_map/all_gather | solution.py:124
  13.6 177.7 %all-gather.13.cloned.1.call-start = ((), (), s32[]{:S(2)}) async-start(), calls=%async_computation.10 | async-start | bytes 2654208 | tf_op jit(solution)/shard_map/all_gather | solution.py:128
  14.2 216.2 %all-gather.15.cloned.1.call-start = ((), (), s32[]{:S(2)}) async-start(), calls=%async_computation.12 | async-start | bytes 3932160 | tf_op jit(solution)/shard_map/all_gather | solution.py:191
  14.8 386.1 %reduce-scatter.18.cloned.1.call-start = ((), (), s32[]{:S(2)}) async-start(), calls=%async_computation.16 | async-start | bytes 884736 | tf_op jit(solution)/shard_map/reduce_scatter | solution.py:232
  14.9 136.7 %copy-start.53 = (pred[256,256]{1,0:T(8,128)(4,1)}, pred[256,256]{1,0:T(8,128)(4,1)S(1)}, u32[]{:S(2)}) copy-start(pred[256,256]{1,0:T(8,128)(4,1)S(1)} %convert_compare_fusion) | copy-start | bytes 196612
  15.0 62.9 %copy-start.92 = (f32[12]{0:T(128)}, f32[12]{0:T(128)S(1)}, u32[]{:S(2)}) copy-start(f32[12]{0:T(128)S(1)} %exponential_negate_fusion) | copy-start | bytes 148
  15.1 66.4 %copy-start.71 = (f32[1,256]{1,0:T(1,128)}, f32[1,256]{1,0:T(1,128)S(1)}, u32[]{:S(2)}) copy-start(f32[1,256]{1,0:T(1,128)S(1)} %get-tuple-element.387) | copy-start | bytes 3076
  15.1 66.4 %copy-start.73 = (f32[1,256]{1,0:T(1,128)}, f32[1,256]{1,0:T(1,128)S(1)}, u32[]{:S(2)}) copy-start(f32[1,256]{1,0:T(1,128)S(1)} %get-tuple-element.388) | copy-start | bytes 3076
  15.1 66.4 %copy-start.75 = (f32[1,256]{1,0:T(1,128)}, f32[1,256]{1,0:T(1,128)S(1)}, u32[]{:S(2)}) copy-start(f32[1,256]{1,0:T(1,128)S(1)} %get-tuple-element.389) | copy-start | bytes 3076
  15.1 66.4 %copy-start.77 = (f32[1,256]{1,0:T(1,128)}, f32[1,256]{1,0:T(1,128)S(1)}, u32[]{:S(2)}) copy-start(f32[1,256]{1,0:T(1,128)S(1)} %get-tuple-element.390) | copy-start | bytes 3076
  15.9 96.1 %copy-start.43 = (f32[1024]{0:T(1024)}, f32[1024]{0:T(1024)S(1)}, u32[]{:S(2)}) copy-start(f32[1024]{0:T(1024)S(1)} %get-tuple-element.386) | copy-start | bytes 12292
  15.9 96.0 %copy-start.56 = (f32[768]{0:T(1024)}, f32[768]{0:T(1024)S(1)}, u32[]{:S(2)}) copy-start(f32[768]{0:T(1024)S(1)} %get-tuple-element.299) | copy-start | bytes 9220
  15.9 96.0 %copy-start.58 = (f32[768]{0:T(1024)}, f32[768]{0:T(1024)S(1)}, u32[]{:S(2)}) copy-start(f32[768]{0:T(1024)S(1)} %get-tuple-element.300) | copy-start | bytes 9220
  16.0 96.0 %copy-start.60 = (f32[768]{0:T(1024)}, f32[768]{0:T(1024)S(1)}, u32[]{:S(2)}) copy-start(f32[768]{0:T(1024)S(1)} %get-tuple-element.301) | copy-start | bytes 9220
  16.0 96.0 %copy-start.62 = (f32[768]{0:T(1024)}, f32[768]{0:T(1024)S(1)}, u32[]{:S(2)}) copy-start(f32[768]{0:T(1024)S(1)} %get-tuple-element.302) | copy-start | bytes 9220
  25.9 51.9 %copy-start.40 = (bf16[1536,12]{0,1:T(8,128)(2,1)}, bf16[1536,12]{0,1:T(8,128)(2,1)S(1)}, u32[]{:S(2)}) copy-start(bf16[1536,12]{0,1:T(8,128)(2,1)S(1)} %reshape.277) | copy-start | bytes 110596
  36.3 45.1 %copy-start.23 = (bf16[1536,256]{1,0:T(8,128)(2,1)}, bf16[1536,256]{1,0:T(8,128)(2,1)S(1)}, u32[]{:S(2)}) copy-start(bf16[1536,256]{1,0:T(8,128)(2,1)S(1)} %all_gather.24) | copy-start | bytes 2359300
  77.9 73.7 %copy-start.36 = (f32[4,256,12]{1,2,0:T(8,128)}, f32[4,256,12]{1,2,0:T(8,128)S(1)}, u32[]{:S(2)}) copy-start(f32[4,256,12]{1,2,0:T(8,128)S(1)} %copy.90) | copy-start | bytes 147460
  78.2 73.4 %copy-start.34 = (f32[4,256,12]{1,2,0:T(8,128)}, f32[4,256,12]{1,2,0:T(8,128)S(1)}, u32[]{:S(2)}) copy-start(f32[4,256,12]{1,2,0:T(8,128)S(1)} %convolution_bitcast_fusion.1) | copy-start | bytes 147460
  78.5 48.9 %copy-start.24 = (f32[4,256,12]{1,2,0:T(8,128)}, f32[4,256,12]{1,2,0:T(8,128)S(1)}, u32[]{:S(2)}) copy-start(f32[4,256,12]{1,2,0:T(8,128)S(1)} %get-tuple-element.380) | copy-start | bytes 147460
  78.5 73.2 %copy-start.38 = (f32[4,256,12]{1,2,0:T(8,128)}, f32[4,256,12]{1,2,0:T(8,128)S(1)}, u32[]{:S(2)}) copy-start(f32[4,256,12]{1,2,0:T(8,128)S(1)} %get-tuple-element.379) | copy-start | bytes 147460
  83.5 43.9 %copy-start.12 = (f32[1024,128]{1,0:T(8,128)}, f32[1024,128]{1,0:T(8,128)S(1)}, u32[]{:S(2)}) copy-start(f32[1024,128]{1,0:T(8,128)S(1)} %get-tuple-element.373) | copy-start | bytes 1572868
  83.5 65.5 %copy-start.10 = (f32[1024,128]{1,0:T(8,128)}, f32[1024,128]{1,0:T(8,128)S(1)}, u32[]{:S(2)}) copy-start(f32[1024,128]{1,0:T(8,128)S(1)} %get-tuple-element.374) | copy-start | bytes 1572868
  83.5 28.5 %copy-start.81 = (f32[768]{0:T(1024)S(1)}, f32[768]{0:T(1024)}, u32[]{:S(2)}) copy-start(f32[768]{0:T(1024)} %param.32) | copy-start | bytes 9220
  148.9 16.8 %copy-start = (f32[4,12,64,128]{3,2,1,0:T(8,128)}, f32[4,12,64,128]{3,2,1,0:T(8,128)S(1)}, u32[]{:S(2)}) copy-start(f32[4,12,64,128]{3,2,1,0:T(8,128)S(1)} %get-tuple-element.542) | copy-start | bytes 4718596
  230.4 19.4 %copy-start.5 = (f32[1024,768]{1,0:T(8,128)S(1)}, f32[1024,768]{1,0:T(8,128)}, u32[]{:S(2)}) copy-start(f32[1024,768]{1,0:T(8,128)} %get-tuple-element.356) | copy-start | bytes 9437188
  318.2 18.7 %copy-start.65 = (f32[4,12]{1,0:T(4,128)S(1)}, f32[4,12]{1,0:T(4,128)}, u32[]{:S(2)}) copy-start(f32[4,12]{1,0:T(4,128)} %copy-done.64) | copy-start | bytes 580
  318.2 18.7 %copy-start.80 = (f32[4,12]{1,0:T(4,128)S(1)}, f32[4,12]{1,0:T(4,128)}, u32[]{:S(2)}) copy-start(f32[4,12]{1,0:T(4,128)} %get-tuple-element.225) | copy-start | bytes 580
  365.0 96.1 %reduce-scatter.22.cloned.1.call-start = ((), (), s32[]{:S(2)}) async-start(), calls=%async_computation.19 | async-start | bytes 442368
  369.3 31.8 %copy-start.66 = (f32[1024]{0:T(1024)S(1)}, f32[1024]{0:T(1024)}, u32[]{:S(2)}) copy-start(f32[1024]{0:T(1024)} %get-tuple-element.382) | copy-start | bytes 12292
  369.3 31.8 %copy-start.82 = (f32[768]{0:T(1024)S(1)}, f32[768]{0:T(1024)}, u32[]{:S(2)}) copy-start(f32[768]{0:T(1024)} %param.38) | copy-start | bytes 9220
  371.2 102.5 %all-reduce.26.cloned.1.call-start = ((), (), s32[]{:S(2)}) async-start(), calls=%async_computation.17 | async-start | bytes 196608 | tf_op jit(solution)/shard_map/psum | solution.py:263
  400.9 120.2 %reduce-scatter.20.cloned.1.call-start = ((), (), s32[]{:S(2)}) async-start(), calls=%async_computation.18 | async-start | bytes 2654208 | tf_op jit(solution)/shard_map/reduce_scatter | solution.py:238
  408.4 158.2 %reduce-scatter.14.cloned.1.call-start = ((), (), s32[]{:S(2)}) async-start(), calls=%async_computation.14 | async-start | bytes 2654208 | tf_op jit(solution)/shard_map/reduce_scatter | solution.py:226
  413.9 198.5 %reduce-scatter.16.cloned.1.call-start = ((), (), s32[]{:S(2)}) async-start(), calls=%async_computation.15 | async-start | bytes 2654208 | tf_op jit(solution)/shard_map/reduce_scatter | solution.py:229
  441.4 233.0 %reduce-scatter.12.cloned.1.call-start = ((), (), s32[]{:S(2)}) async-start(), calls=%async_computation.13 | async-start | bytes 3932160 | tf_op jit(solution)/shard_map/reduce_scatter | solution.py:214
  452.3 285.4 %reduce-scatter.10.cloned.1.call-start = ((), (), s32[]{:S(2)}) async-start(), calls=%async_computation.11 | async-start | bytes 3932160 | tf_op jit(solution)/shard_map/reduce_scatter | solution.py:185
  460.1 214.4 %copy-start.16 = (bf16[256,1536]{1,0:T(8,128)(2,1)S(1)}, bf16[256,1536]{1,0:T(8,128)(2,1)}, u32[]{:S(2)}) copy-start(bf16[256,1536]{1,0:T(8,128)(2,1)} %param.22) | copy-start | bytes 2359300
  460.1 214.3 %copy-start.49 = (f32[1536]{0:T(1024)S(1)}, f32[1536]{0:T(1024)}, u32[]{:S(2)}) copy-start(f32[1536]{0:T(1024)} %param.26) | copy-start | bytes 18436
  460.1 214.3 %copy-start.69 = (f32[256]{0:T(256)S(1)}, f32[256]{0:T(256)}, u32[]{:S(2)}) copy-start(f32[256]{0:T(256)} %copy-done.68) | copy-start | bytes 3076
  460.2 215.9 %copy-start.84 = (f32[768]{0:T(1024)S(1)}, f32[768]{0:T(1024)}, u32[]{:S(2)}) copy-start(f32[768]{0:T(1024)} %get-tuple-element.283) | copy-start | bytes 9220
  460.2 215.9 %copy-start.87 = (f32[256]{0:T(256)S(1)}, f32[256]{0:T(256)}, u32[]{:S(2)}) copy-start(f32[256]{0:T(256)} %get-tuple-element.298) | copy-start | bytes 3076
  460.2 277.5 %copy-start.21 = (bf16[256,1536]{1,0:T(8,128)(2,1)S(1)}, bf16[256,1536]{1,0:T(8,128)(2,1)}, u32[]{:S(2)}) copy-start(bf16[256,1536]{1,0:T(8,128)(2,1)} %param.23) | copy-start | bytes 2359300
  460.2 277.5 %copy-start.83 = (f32[256]{0:T(256)S(1)}, f32[256]{0:T(256)}, u32[]{:S(2)}) copy-start(f32[256]{0:T(256)} %get-tuple-element.391) | copy-start | bytes 3076
  (68 other events, 345.8 us)
Sparse Core Ops, SparseCore 0:
  12.3 62.0 all-gather.6
  76.3 30.4 all-gather.8
  108.6 28.8 all-gather.10
  139.3 28.9 all-gather.12
  169.7 60.7 all-gather.14
  365.1 35.6 reduce-scatter.17
  404.5 33.8 reduce-scatter.21
  440.7 32.8 all-reduce.25
  477.0 44.0 reduce-scatter.19
  524.3 42.3 reduce-scatter.13
  570.0 42.3 reduce-scatter.15
  614.5 59.8 reduce-scatter.11
  676.7 60.8 reduce-scatter.9
where the time goes:
time: 761 us; the launch traced here: 748 us
  waiting for transfers between devices  366 us (48%)
  matrix products  154 us (20%)
  other arithmetic  78.7 us (10%)
  blocking collectives  69.7 us (9%)
  local copies, waits for them, and re-layouts  61.8 us (8%)
  between operations  15.9 us (2%)
    reduce_scatter x1, waiting for transfers between devices, shards(): lax.psum_scatter((partial_term(grad_z, whole_z) + partial_term(grad_x, wh...  60.2 us
    dot_general x3, matrix products, state_scan(): jnp.einsum('ctsh,cshp->cthp', weights * intersection[..., None], scaled_x...  47 us
    reduce_scatter x1, waiting for transfers between devices, shards(): lax.psum_scatter(grad_out_rows.astype(jnp.bfloat16), 'fsdp', scatter_dime...  45.8 us
    reduce_scatter x1, waiting for transfers between devices, shards(): lax.psum_scatter(weight_x.astype(jnp.bfloat16), 'fsdp', scatter_dimension...  43.9 us
    reduce_scatter x1, waiting for transfers between devices, shards(): lax.psum_scatter(weight_z.astype(jnp.bfloat16), 'fsdp', scatter_dimension...  43.8 us
    all_gather x1, waiting for transfers between devices, shards(): cot_all = lax.all_gather(cotangent, 'tp', axis=0, tiled=True)  39.1 us
    all_gather x1, waiting for transfers between devices, shards(): normed_all = lax.all_gather(normed, 'tp', axis=0, tiled=True)  38.1 us
    reduce_scatter x1, waiting for transfers between devices, shards(): lax.psum_scatter(weight_bc.astype(jnp.bfloat16), 'fsdp', scatter_dimensio...  29.7 us
  transfers between devices with their start and end apart: 13, of which 10 were waited for; matrix products, arithmetic and copies ran while one was open for 21% of the time, Pallas kernels for 0%

commit v1 on v0

v1 whole, which is shorter than its diff:
```python
import functools
import jax
import jax.numpy as jnp
from jax import lax
from jax.experimental import pallas as pl
from jax.experimental.pallas import tpu as pltpu
from jax.sharding import PartitionSpec as P

HEAD = 64
STATE = 128
STRETCH = 256
LANES = 128
EPSILON = 1e-05
F32 = jnp.float32
BF16 = jnp.bfloat16
NN = (((1,), (0,)), ((), ()))
NT = (((1,), (1,)), ((), ()))
TN = (((0,), (0,)), ((), ()))


def mm(a, b, dims=NN):
    return lax.dot_general(a, b, dims, preferred_element_type=F32)


def exact(a, b):
    return lax.dot_general(a, b, NN, precision=lax.Precision.HIGHEST, preferred_element_type=F32)


def halves(v):
    high = v.astype(BF16)
    return high, (v - high.astype(F32)).astype(BF16)


def iota(shape, dim):
    return lax.broadcasted_iota(jnp.int32, shape, dim)


def spread_heads(v, chan):
    high, rest = halves(v)
    rows = iota((2 * LANES, chan), 0) & (LANES - 1)
    pick = jnp.where(rows == (iota((2 * LANES, chan), 1) >> 6), 1.0, 0.0).astype(BF16)
    return mm(jnp.concatenate([high, rest], axis=1), pick)


def gather_heads(v):
    chan = v.shape[1]
    high, rest = halves(v)
    pick = jnp.where((iota((chan, LANES), 0) >> 6) == iota((chan, LANES), 1), 1.0, 0.0).astype(BF16)
    return mm(high, pick) + mm(rest, pick)


def softplus(v):
    return jnp.maximum(v, 0.0) + jnp.log1p(jnp.exp(-jnp.abs(v)))


def sigmoid(v):
    return 1.0 / (1.0 + jnp.exp(-v))


def lower_mask():
    return iota((STRETCH, STRETCH), 0) >= iota((STRETCH, STRETCH), 1)


def convolve(xs_ref, taps_ref, bias_ref):
    total = bias_ref[...] + taps_ref[0:1, :] * xs_ref[5:5 + STRETCH, :]
    for tap in range(1, 4):
        total = total + taps_ref[tap:tap + 1, :] * xs_ref[5 + tap:5 + tap + STRETCH, :]
    return total


def decays(pre_dt, head_ref, valid):
    rates = softplus(pre_dt + head_ref[0:1, :]) * valid
    log_decay = rates * head_ref[1:2, :]
    lower = lower_mask().astype(F32)
    cumulative = exact(lower, log_decay)
    last = cumulative[STRETCH - 1:STRETCH, :]
    return rates, cumulative, jnp.exp(cumulative), jnp.exp(last - cumulative)


def weights_of(cumulative, across, head):
    return jnp.exp(jnp.minimum(cumulative[:, head:head + 1] - across[head:head + 1, :], 0.0))


def forward_kernel(
    open_ref, tok_ref, valid_ref, gain_ref, w_ref, taps_ref, bias_ref, head_ref, skip_ref,
    normed_ref, pre_ref, y_ref, gated_ref, sq_ref, enter_ref,
    state, xs,
):
    chan = y_ref.shape[1]
    block = pl.program_id(0)
    opening = open_ref[block] == 1

    @pl.when(opening)
    def _():
        state[...] = jnp.zeros_like(state)
        xs[0:8, :] = jnp.zeros((8, xs.shape[1]), F32)

    @pl.when(jnp.logical_not(opening))
    def _():
        xs[0:8, :] = xs[STRETCH:STRETCH + 8, :]

    valid = valid_ref[...]
    resid = tok_ref[...].astype(F32)
    rstd = lax.rsqrt(jnp.mean(resid * resid, axis=1, keepdims=True) + EPSILON)
    normed = (resid * rstd * gain_ref[...]).astype(BF16)
    normed_ref[...] = normed
    pre = mm(normed, w_ref[...])
    pre_ref[...] = pre
    xs[8:8 + STRETCH, :] = pre[:, chan:2 * chan + 2 * STATE]
    conv = convolve(xs, taps_ref, bias_ref)
    feats = conv * sigmoid(conv)
    x = feats[:, :chan]
    bs = feats[:, chan:chan + STATE].astype(BF16)
    cs = feats[:, chan + STATE:].astype(BF16)
    rates, cumulative, grown, to_end = decays(pre[:, 2 * chan + 2 * STATE:], head_ref, valid)
    across = cumulative.T
    grown_e = spread_heads(grown, chan)
    scaled = x * spread_heads(rates, chan)
    entering = state[...]
    enter_ref[0] = entering
    y_ref[...] = mm(cs, entering.astype(BF16)) * grown_e
    state[...] = entering * grown_e[STRETCH - 1:STRETCH, :] + mm(
        bs, (scaled * spread_heads(to_end, chan)).astype(BF16), TN
    )
    overlap = jnp.where(lower_mask(), mm(cs, bs, NT), 0.0)
    scaled_b = scaled.astype(BF16)
    first = iota((STRETCH, LANES), 1) < HEAD
    for pair in range(chan // LANES):
        cols = slice(pair * LANES, (pair + 1) * LANES)
        both = scaled_b[:, cols]
        mats = [
            (weights_of(cumulative, across, 2 * pair + side) * overlap).astype(BF16) for side in range(2)
        ]
        zero = jnp.zeros_like(both)
        y_ref[:, cols] += mm(
            jnp.concatenate(mats, axis=1),
            jnp.concatenate([jnp.where(first, both, zero), jnp.where(first, zero, both)], axis=0),
        )
    pre_z = pre[:, :chan]
    gated = (y_ref[...] + skip_ref[...] * x) * (pre_z * sigmoid(pre_z)) * valid
    gated_ref[...] = gated
    sq_ref[...] = jnp.sum(gated * gated, axis=1, keepdims=True)


def backward_kernel(
    open_ref, tok_ref, valid_ref, w_ref, taps_ref, bias_ref, head_ref, skip_ref, gate_ref,
    pre_ref, halo_ref, y_ref, enter_ref, dgn_ref, stats_ref,
    dpre_ref, dnormed_ref, dtaps_ref, dbias_ref, dhead_ref, dchan_ref, dgain_ref,
    dstate, xs, dus,
    *, inner,
):
    chan = y_ref.shape[1]
    wide = chan + 2 * STATE
    step = pl.program_id(0)
    block = pl.num_programs(0) - 1 - step
    opening = open_ref[block] == 1
    keep = jnp.where(opening, 0.0, 1.0).astype(F32)

    @pl.when(step == 0)
    def _():
        dstate[...] = jnp.zeros_like(dstate)
        dus[...] = jnp.zeros_like(dus)
        dtaps_ref[...] = jnp.zeros_like(dtaps_ref)
        dbias_ref[...] = jnp.zeros_like(dbias_ref)
        dhead_ref[...] = jnp.zeros_like(dhead_ref)
        dchan_ref[...] = jnp.zeros_like(dchan_ref)
        dgain_ref[...] = jnp.zeros_like(dgain_ref)

    valid = valid_ref[...]
    xs[0:8, :] = halo_ref[:, chan:2 * chan + 2 * STATE] * keep
    xs[8:8 + STRETCH, :] = pre_ref[:, chan:2 * chan + 2 * STATE]
    conv = convolve(xs, taps_ref, bias_ref)
    gate_u = sigmoid(conv)
    feats = conv * gate_u
    slope = gate_u * (1.0 + conv * (1.0 - gate_u))
    x = feats[:, :chan]
    bs = feats[:, chan:chan + STATE].astype(BF16)
    cs = feats[:, chan + STATE:].astype(BF16)
    pre_dt = pre_ref[:, 2 * chan + 2 * STATE:]
    rates, cumulative, grown, to_end = decays(pre_dt, head_ref, valid)
    across = cumulative.T
    grown_e = spread_heads(grown, chan)
    rates_e = spread_heads(rates, chan)
    to_end_e = spread_heads(to_end, chan)
    leave_e = grown_e[STRETCH - 1:STRETCH, :]

    pre_z = pre_ref[:, :chan]
    gate_z = sigmoid(pre_z)
    silu_z = pre_z * gate_z * valid
    y = y_ref[...]
    mixed = y + skip_ref[...] * x
    gated = mixed * silu_z
    grstd, cross = row_stats(stats_ref, inner)
    dgn = dgn_ref[...]
    d_gated = grstd * (gate_ref[...] * dgn) - gated * (grstd * grstd * grstd * cross * (1.0 / inner))
    d_mixed = d_gated * silu_z
    dpre_ref[:, :chan] = (
        d_gated * mixed * (valid * (gate_z * (1.0 + pre_z * (1.0 - gate_z))))
    ).astype(BF16)
    dchan_ref[0:1, :] += jnp.sum(dgn * gated * grstd, axis=0, keepdims=True)
    dchan_ref[1:2, :] += jnp.sum(d_mixed * x, axis=0, keepdims=True)

    dy_b = d_mixed.astype(BF16)
    dy = dy_b.astype(F32)
    scaled = x * rates_e
    scaled_b = scaled.astype(BF16)
    entering = enter_ref[0]
    d_leaving = dstate[...]
    d_leaving_b = d_leaving.astype(BF16)
    tail = mm(bs, d_leaving_b) * to_end_e
    overlap = jnp.where(lower_mask(), mm(cs, bs, NT), 0.0)
    first = iota((STRETCH, LANES), 1) < HEAD
    d_overlap = jnp.zeros((STRETCH, STRETCH), F32)
    parts = []
    for pair in range(chan // LANES):
        cols = slice(pair * LANES, (pair + 1) * LANES)
        dy_pair = dy_b[:, cols]
        x_pair = scaled_b[:, cols]
        zero = jnp.zeros_like(dy_pair)
        sides = [jnp.where(first, dy_pair, zero), jnp.where(first, zero, dy_pair)]
        mats = []
        for side in range(2):
            weight = weights_of(cumulative, across, 2 * pair + side)
            mats.append((weight * overlap).astype(BF16))
            d_overlap = d_overlap + mm(sides[side], x_pair, NT) * weight
        parts.append(mm(jnp.concatenate(mats, axis=0), jnp.concatenate(sides, axis=0), TN))
    d_scaled = jnp.concatenate(parts, axis=1) + tail
    scaled_r = scaled_b.astype(F32)
    d_cum = gather_heads(dy * y - scaled_r * d_scaled)
    d_last = jnp.sum(scaled_r * tail, axis=0, keepdims=True) + leave_e * jnp.sum(
        d_leaving * entering, axis=0, keepdims=True
    )
    d_last = gather_heads(jnp.broadcast_to(d_last, (8, chan)))[0:1, :]
    upper = (iota((STRETCH, STRETCH), 0) <= iota((STRETCH, STRETCH), 1)).astype(F32)
    d_log = exact(upper, d_cum) + d_last
    decay = head_ref[1:2, :]
    d_rates = d_log * decay + gather_heads(x * d_scaled)
    d_dt = d_rates * valid * sigmoid(pre_dt + head_ref[0:1, :])
    dhead_ref[0:1, :] += jnp.sum(d_log * rates, axis=0, keepdims=True) * decay
    dhead_ref[1:2, :] += jnp.sum(d_dt, axis=0, keepdims=True)
    dpre_ref[:, 2 * chan + 2 * STATE:] = d_dt.astype(BF16)

    d_x = d_scaled * rates_e + skip_ref[...] * d_mixed
    d_overlap_b = jnp.where(lower_mask(), d_overlap, 0.0).astype(BF16)
    dy_grown = (dy * grown_e).astype(BF16)
    x_end = (scaled * to_end_e).astype(BF16)
    d_b = mm(d_overlap_b, cs, TN) + mm(x_end, d_leaving_b, NT)
    d_c = mm(d_overlap_b, bs) + mm(dy_grown, entering.astype(BF16), NT)
    dstate[...] = (d_leaving * leave_e + mm(cs, dy_grown, TN)) * keep

    dus[0:STRETCH, :chan] = d_x * slope[:, :chan]
    dus[0:STRETCH, chan:chan + STATE] = d_b * slope[:, chan:chan + STATE]
    dus[0:STRETCH, chan + STATE:] = d_c * slope[:, chan + STATE:]
    d_conv = dus[0:STRETCH, :]
    dbias_ref[...] += jnp.sum(d_conv, axis=0, keepdims=True)
    d_pre = jnp.zeros((STRETCH, wide), F32)
    for tap in range(4):
        dtaps_ref[tap:tap + 1, :] += jnp.sum(d_conv * xs[5 + tap:5 + tap + STRETCH, :], axis=0, keepdims=True)
        d_pre = d_pre + taps_ref[tap:tap + 1, :] * dus[3 - tap:3 - tap + STRETCH, :]
    dpre_ref[:, chan:2 * chan + 2 * STATE] = d_pre.astype(BF16)
    dus[STRETCH:STRETCH + 8, :] = d_conv[0:8, :] * keep

    d_normed = mm(dpre_ref[...], w_ref[...], NT)
    dnormed_ref[...] = d_normed.astype(BF16)
    resid = tok_ref[...].astype(F32)
    rstd = lax.rsqrt(jnp.mean(resid * resid, axis=1, keepdims=True) + EPSILON)
    dgain_ref[...] += jnp.sum(d_normed * (resid * rstd), axis=0, keepdims=True)


def whole(shape):
    return pl.BlockSpec(shape, lambda *_: (0,) * len(shape), pipeline_mode=pl.Buffered(1))


def mixer_forward(openings, tok, valid, gain, w_in, taps, bias, heads, skip):
    tokens, width = tok.shape
    cols = w_in.shape[1]
    chan = skip.shape[1]
    blocks = tokens // STRETCH
    wide = chan + 2 * STATE
    rows = lambda n: pl.BlockSpec((STRETCH, n), lambda i, *_: (i, 0))
    return pl.pallas_call(
        forward_kernel,
        name="mixer_forward",
        grid_spec=pltpu.PrefetchScalarGridSpec(
            num_scalar_prefetch=1,
            grid=(blocks,),
            in_specs=[
                rows(width), rows(1), whole((1, width)), whole((width, cols)), whole((4, wide)), whole((1, wide)),
                whole((8, LANES)), whole((1, chan)),
            ],
            out_specs=[
                rows(width), rows(cols), rows(chan), rows(chan), rows(1),
                pl.BlockSpec((1, STATE, chan), lambda i, *_: (i, 0, 0)),
            ],
            scratch_shapes=[
                pltpu.VMEM((STATE, chan), F32),
                pltpu.VMEM((STRETCH + 8, wide), F32),
            ],
        ),
        out_shape=[
            jax.ShapeDtypeStruct((tokens, width), BF16),
            jax.ShapeDtypeStruct((tokens, cols), F32),
            jax.ShapeDtypeStruct((tokens, chan), F32),
            jax.ShapeDtypeStruct((tokens, chan), F32),
            jax.ShapeDtypeStruct((tokens, 1), F32),
            jax.ShapeDtypeStruct((blocks, STATE, chan), F32),
        ],
        cost_estimate=pl.CostEstimate(
            flops=2 * tokens * width * cols, bytes_accessed=tokens * cols * 12, transcendentals=tokens * chan
        ),
        compiler_params=pltpu.CompilerParams(vmem_limit_bytes=60 << 20, dimension_semantics=("arbitrary",)),
    )(openings, tok, valid, gain, w_in, taps, bias, heads, skip)


def mixer_backward(
    openings, tok, valid, w_in, taps, bias, heads, skip, gate, pre, y, enter, dgn, stats, inner
):
    tokens, width = tok.shape
    cols = w_in.shape[1]
    chan = skip.shape[1]
    blocks = tokens // STRETCH
    wide = chan + 2 * STATE
    per = STRETCH // 8
    rows = lambda n: pl.BlockSpec((STRETCH, n), lambda i, *_: (blocks - 1 - i, 0))
    return pl.pallas_call(
        functools.partial(backward_kernel, inner=inner),
        name="mixer_backward",
        grid_spec=pltpu.PrefetchScalarGridSpec(
            num_scalar_prefetch=1,
            grid=(blocks,),
            in_specs=[
                rows(width), rows(1), whole((width, cols)), whole((4, wide)), whole((1, wide)),
                whole((8, LANES)), whole((1, chan)), whole((1, chan)),
                rows(cols),
                pl.BlockSpec((8, cols), lambda i, *_: (jnp.maximum((blocks - 1 - i) * per - 1, 0), 0)),
                rows(chan),
                pl.BlockSpec((1, STATE, chan), lambda i, *_: (blocks - 1 - i, 0, 0)),
                rows(chan),
                pl.BlockSpec((8, STRETCH), lambda i, *_: (0, blocks - 1 - i)),
            ],
            out_specs=[
                rows(cols), rows(width),
                pl.BlockSpec((8, wide), lambda i, *_: (0, 0)),
                pl.BlockSpec((1, wide), lambda i, *_: (0, 0)),
                pl.BlockSpec((8, LANES), lambda i, *_: (0, 0)),
                pl.BlockSpec((8, chan), lambda i, *_: (0, 0)),
                pl.BlockSpec((1, width), lambda i, *_: (0, 0)),
            ],
            scratch_shapes=[
                pltpu.VMEM((STATE, chan), F32),
                pltpu.VMEM((STRETCH + 8, wide), F32),
                pltpu.VMEM((STRETCH + 8, wide), F32),
            ],
        ),
        out_shape=[
            jax.ShapeDtypeStruct((tokens, cols), BF16),
            jax.ShapeDtypeStruct((tokens, width), BF16),
            jax.ShapeDtypeStruct((8, wide), F32),
            jax.ShapeDtypeStruct((1, wide), F32),
            jax.ShapeDtypeStruct((8, LANES), F32),
            jax.ShapeDtypeStruct((8, chan), F32),
            jax.ShapeDtypeStruct((1, width), F32),
        ],
        cost_estimate=pl.CostEstimate(
            flops=4 * tokens * width * cols, bytes_accessed=tokens * cols * 12, transcendentals=tokens * chan
        ),
        compiler_params=pltpu.CompilerParams(vmem_limit_bytes=60 << 20, dimension_semantics=("arbitrary",)),
    )(openings, tok, valid, w_in, taps, bias, heads, skip, gate, pre, pre, y, enter, dgn, stats)


def stats_kernel(cot_ref, wout_ref, gate_ref, gated_ref, sq_ref, dgn_ref, stats_ref):
    dgn = mm(cot_ref[...], wout_ref[...])
    dgn_ref[...] = dgn
    cross = jnp.sum(gate_ref[...] * dgn * gated_ref[...], axis=1, keepdims=True)
    lane = iota((STRETCH, LANES), 1)
    both = jnp.where(lane == 0, sq_ref[...], 0.0) + jnp.where(lane == 1, cross, 0.0)
    stats_ref[...] = both.T[0:8, :]


def row_stats(stats_ref, inner):
    filled = jnp.concatenate([stats_ref[...], jnp.zeros((LANES - 8, STRETCH), F32)], axis=0).T
    grstd = lax.rsqrt(filled[:, 0:1] * (1.0 / inner) + EPSILON)
    return grstd, filled[:, 1:2]


def output_kernel(gated_ref, stats_ref, gate_ref, wout_ref, gnormed_ref, out_ref, *, inner):
    grstd, _ = row_stats(stats_ref, inner)
    gnormed = (gated_ref[...] * grstd * gate_ref[...]).astype(BF16)
    gnormed_ref[...] = gnormed
    out_ref[...] = mm(gnormed, wout_ref[...], NT).astype(BF16)


def gate_stats(cot, wout, gate, gated, sq):
    tokens, width = cot.shape
    chan = gate.shape[1]
    rows = lambda n: pl.BlockSpec((STRETCH, n), lambda i: (i, 0))
    return pl.pallas_call(
        stats_kernel,
        name="gate_stats",
        grid=(tokens // STRETCH,),
        in_specs=[rows(width), whole((width, chan)), whole((1, chan)), rows(chan), rows(1)],
        out_specs=[rows(chan), pl.BlockSpec((8, STRETCH), lambda i: (0, i))],
        out_shape=[jax.ShapeDtypeStruct((tokens, chan), F32), jax.ShapeDtypeStruct((8, tokens), F32)],
        cost_estimate=pl.CostEstimate(
            flops=2 * tokens * width * chan, bytes_accessed=tokens * (2 * width + 8 * chan), transcendentals=0
        ),
        compiler_params=pltpu.CompilerParams(vmem_limit_bytes=40 << 20),
    )(cot, wout, gate, gated, sq)


def output_part(gated, stats, gate, wout, inner):
    tokens, chan = gated.shape
    width = wout.shape[0]
    rows = lambda n: pl.BlockSpec((STRETCH, n), lambda i: (i, 0))
    return pl.pallas_call(
        functools.partial(output_kernel, inner=inner),
        name="output_part",
        grid=(tokens // STRETCH,),
        in_specs=[rows(chan), pl.BlockSpec((8, STRETCH), lambda i: (0, i)), whole((1, chan)), whole((width, chan))],
        out_specs=[rows(chan), rows(width)],
        out_shape=[jax.ShapeDtypeStruct((tokens, chan), BF16), jax.ShapeDtypeStruct((tokens, width), BF16)],
        cost_estimate=pl.CostEstimate(
            flops=2 * tokens * width * chan, bytes_accessed=tokens * (2 * width + 4 * chan), transcendentals=0
        ),
        compiler_params=pltpu.CompilerParams(vmem_limit_bytes=40 << 20),
    )(gated, stats, gate, wout)


def padded(v, fill):
    return jnp.pad(v[None, :], ((0, 0), (0, LANES - v.shape[0])), constant_values=fill)


def shards(
    tokens, cotangent, seq_start, token_valid, norm_gain, proj_z, proj_x, proj_bc, proj_dt, conv_chan, bias_chan,
    conv_shared, bias_shared, a_log, dt_bias, skip_gain, gate_gain, proj_out,
):
    chan = proj_z.shape[1]
    width = tokens.shape[1]
    heads_here = proj_dt.shape[1]
    inner = chan * lax.axis_size("tp")
    wide = chan + 2 * STATE
    valid = token_valid.astype(F32)[:, None]
    pack_in = jnp.concatenate(
        [proj_z, proj_x, proj_bc, jnp.pad(proj_dt, ((0, 0), (0, LANES - heads_here)))], axis=1
    )
    tok_all = lax.all_gather(tokens, "tp", axis=0, tiled=True)
    w_in = lax.all_gather(pack_in, "fsdp", axis=0, tiled=True)
    w_out = lax.all_gather(proj_out.T, "fsdp", axis=0, tiled=True)
    cot_all = lax.all_gather(cotangent, "tp", axis=0, tiled=True)
    decay = -jnp.exp(a_log)
    heads = jnp.concatenate([padded(dt_bias, -100.0), padded(decay, 0.0), jnp.zeros((6, LANES), F32)], axis=0)
    taps = jnp.concatenate([conv_chan, conv_shared], axis=1)
    bias = jnp.concatenate([bias_chan, bias_shared])[None, :]
    skip = jnp.repeat(skip_gain, HEAD)[None, :]
    gate = gate_gain[None, :]
    normed, pre, y, gated, sq, enter = mixer_forward(
        seq_start, tok_all, valid, norm_gain[None, :], w_in, taps, bias, heads, skip
    )
    dgn, stats = gate_stats(cot_all, w_out, gate, gated, sq)
    stats = lax.psum(stats, "tp")
    gnormed, out_rows = output_part(gated, stats, gate, w_out, inner)
    mixed = lax.psum_scatter(out_rows, "tp", scatter_dimension=0, tiled=True)
    dpre, dn_rows, dtaps, dbias, dhead, dchan, dgain = mixer_backward(
        seq_start, tok_all, valid, w_in, taps, bias, heads, skip, gate, pre, y, enter, dgn, stats, inner
    )
    d_normed = lax.psum_scatter(dn_rows, "tp", scatter_dimension=0, tiled=True).astype(F32)
    grad_in = jnp.einsum("td,tc->dc", normed, dpre, preferred_element_type=F32).astype(BF16)
    grad_out = jnp.einsum("td,tc->dc", cot_all, gnormed, preferred_element_type=F32).astype(BF16)
    own_in = lax.psum_scatter(grad_in, "fsdp", scatter_dimension=0, tiled=True).astype(F32)
    own_out = lax.psum_scatter(grad_out, "fsdp", scatter_dimension=0, tiled=True).astype(F32)
    mine = jnp.concatenate([v.reshape(-1) for v in (dtaps[0:4, :chan], dbias[:, :chan], dhead[0:2], dchan[0:2])])
    shared = jnp.concatenate([v.reshape(-1) for v in (dtaps[0:4, chan:], dbias[:, chan:], dgain)])
    split = mine.shape[0]
    both = lax.psum(jnp.concatenate([mine, shared]), "fsdp")
    mine = both[:split]
    shared, own_bc = lax.psum((both[split:], own_in[:, 2 * chan:wide + chan]), "tp")
    at = 0

    def take(source, *shape):
        nonlocal at
        size = 1
        for extent in shape:
            size *= extent
        part = source[at:at + size].reshape(shape)
        at += size
        return part

    g_taps, g_bias, g_heads, g_chan = (
        take(mine, 4, chan), take(mine, chan), take(mine, 2, LANES), take(mine, 2, chan),
    )
    at = 0
    g_taps_s, g_bias_s, g_gain = take(shared, 4, 2 * STATE), take(shared, 2 * STATE), take(shared, width)
    resid = tokens.astype(F32)
    rstd = lax.rsqrt(jnp.mean(resid * resid, axis=1, keepdims=True) + EPSILON)
    output = (resid + mixed.astype(F32)).astype(BF16)
    scaled_in = d_normed * norm_gain[None, :]
    grad_tokens = (
        cotangent.astype(F32) + rstd * scaled_in
        - resid * (rstd * rstd * rstd) * jnp.mean(scaled_in * resid, axis=1, keepdims=True)
    ).astype(BF16)
    return (
        output, grad_tokens, g_gain, own_in[:, :chan], own_in[:, chan:2 * chan], own_bc,
        own_in[:, wide + chan:wide + chan + heads_here], g_taps, g_bias, g_taps_s, g_bias_s,
        g_heads[0, :heads_here], g_heads[1, :heads_here], g_chan[1].reshape(heads_here, HEAD).sum(axis=1),
        g_chan[0], own_out.T,
    )


def solution(mesh):
    in_specs = (
        P(("fsdp", "tp"), None), P(("fsdp", "tp"), None), P("fsdp"), P("fsdp"), P(), P("fsdp", "tp"),
        P("fsdp", "tp"), P("fsdp", None), P("fsdp", "tp"), P(None, "tp"), P("tp"), P(), P(), P("tp"), P("tp"),
        P("tp"), P("tp"), P("tp", "fsdp"),
    )
    out_specs = (
        P(("fsdp", "tp"), None), P(("fsdp", "tp"), None), P(), P("fsdp", "tp"), P("fsdp", "tp"), P("fsdp", None),
        P("fsdp", "tp"), P(None, "tp"), P("tp"), P(), P(), P("tp"), P("tp"), P("tp"), P("tp"), P("tp", "fsdp"),
    )
    return jax.shard_map(shards, mesh=mesh, in_specs=in_specs, out_specs=out_specs, check_vma=False)
```

time: 761 us -> 534 us (0.70); the launches traced: 748 us -> 529 us
  matrix products: 154 us -> 13.5 us
  Pallas kernels: 0 us -> 71.6 us
  other arithmetic: 78.7 us -> 8.65 us
  waiting for transfers between devices: 366 us -> 334 us
  local copies, waits for them, and re-layouts: 61.8 us -> 30.8 us
  blocking collectives: 69.7 us -> 55.8 us
    dot_general x29 -> x2, matrix products: 154 us -> 13.5 us  [the longest x1 10.5 us: shards(): jnp.einsum('td,tc->dc', normed, dpre, preferred_element_type=F32)]
    reduce_scatter x6 -> x3, waiting for transfers between devices: 252 us -> 127 us  [the longest x1 60.9 us: shards(): mixed = lax.psum_scatter(out_rows, 'tp', scatter_dimension=0, tiled=True)]
    pallas_call x0 -> x4, Pallas kernels: none -> 71.6 us  [the longest x1 39.6 us: mixer_backward(): pl.pallas_call(functools.partial(backward_kernel, inner=inner), name='mix...]
    all_gather x4 -> x3, waiting for transfers between devices: 61.3 us -> 111 us  [the longest x1 55.6 us: shards(): tok_all = lax.all_gather(tokens, 'tp', axis=0, tiled=True)]
    reduce_sum x12 -> x1, other arithmetic: 35.1 us -> 0.63 us  [shards(): g_chan[1].reshape(heads_here, HEAD).sum(axis=1)]
    all_gather x1, waiting for transfers between devices: 39.1 us -> 62 us  [shards(): cot_all = lax.all_gather(cotangent, 'tp', axis=0, tiled=True)]
    psum x1, waiting for transfers between devices: 11.1 us -> 32 us  [shards(): lax.psum((both[split:], own_in[:, 2 * chan:wide + chan]), 'tp')]
    all_gather x2 -> x0, blocking collectives: 20.2 us -> none  [the longest x1 10.4 us: shards(): lax.all_gather(proj_bc, 'fsdp', axis=0, tiled=True)]
  transfers between devices with their start and end apart: 13 -> 9, of which waited for: 10 -> 8; matrix products, arithmetic and copies ran while one was open for 21% -> 6% of each run, Pallas kernels for 0% -> 12%
where the time goes in v1:
time: 534 us; the launch traced here: 529 us
  waiting for transfers between devices  334 us (63%)
  Pallas kernels  71.6 us (13%)
  blocking collectives  55.8 us (10%)
  local copies, waits for them, and re-layouts  30.8 us (6%)
  between operations  14.2 us (3%)
  matrix products  13.5 us (3%)
  other arithmetic  8.65 us (2%)
    all_gather x1, waiting for transfers between devices, shards(): cot_all = lax.all_gather(cotangent, 'tp', axis=0, tiled=True)  62 us
    reduce_scatter x1, waiting for transfers between devices, shards(): mixed = lax.psum_scatter(out_rows, 'tp', scatter_dimension=0, tiled=True)  60.9 us
    reduce_scatter x1, waiting for transfers between devices, shards(): lax.psum_scatter(grad_in, 'fsdp', scatter_dimension=0, tiled=True)  60.5 us
    all_gather x1, waiting for transfers between devices, shards(): tok_all = lax.all_gather(tokens, 'tp', axis=0, tiled=True)  55.6 us
    all_gather x1, waiting for transfers between devices, shards(): w_in = lax.all_gather(pack_in, 'fsdp', axis=0, tiled=True)  47.8 us
    pallas_call x1, Pallas kernels, mixer_backward(): pl.pallas_call(functools.partial(backward_kernel, inner=inner), name='mix...  39.6 us
    psum x1, waiting for transfers between devices, shards(): lax.psum((both[split:], own_in[:, 2 * chan:wide + chan]), 'tp')  32 us
    psum x1, blocking collectives, shards(): both = lax.psum(jnp.concatenate([mine, shared]), 'fsdp')  25.3 us
  transfers between devices with their start and end apart: 9, of which 8 were waited for; matrix products, arithmetic and copies ran while one was open for 6% of the time, Pallas kernels for 12%

profile of v1, /device:TPU:9, one launch (start us, length us, event | category | flops | bytes accessed | tf_op | source)
XLA Modules:
  0.0 529.3 jit_solution(3420704285914710442)
XLA Ops:
  7.2 0.7 all-gather.5.cloned.1.call-update
  8.0 0.8 copy.47
  8.8 2.0 fusion.8
  11.0 0.7 all-gather.11.cloned.1.call-update
  13.0 0.7 broadcast_in_dim_reshape.3.skip_ref
  13.7 1.0 copy.48.valid_ref
  15.5 0.7 fusion.9.head_ref
  16.1 55.6 %all-gather.5.cloned.1.call-done.tok_ref = bf16[1024,1536]{1,0:T(8,128)(2,1)} async-done(((bf16[256,1536]{1,0:T(8,128)(2,1)}), bf16[1024,1536]{1,0:T(8,128)(2,1)}) %all-gather.5.cloned.1.call-update) | async-done | bytes 3145744 | tf_op jit(solution)/shard_map/all_gather | solution.py:446
  71.7 47.8 %all-gather.7.cloned.1.call-done.w_ref = bf16[1536,1920]{1,0:T(8,128)(2,1)} async-done(((bf16[192,1920]{1,0:T(8,128)(2,1)}), bf16[1536,1920]{1,0:T(8,128)(2,1)}) %all-gather.7.cloned.1.call-update) | async-done | bytes 5898256 | tf_op jit(solution)/shard_map/all_gather | solution.py:447
  119.5 23.5 %mixer_forward.1 = (bf16[1024,1536]{1,0:T(8,128)(2,1)}, f32[1024,1920]{1,0:T(8,128)}, f32[1024,768]{1,0:T(8,128)}, f32[1024,768]{1,0:T(8,128)}, f32[1024,1]{1,0:T(8,128)}, /*index=5*/f32[4,128,768]{2,1,0:T(8,128)}) custom-call(s32[4]{0:T(128)} %open_ref.3, bf16[1024,1536]{1,0:T(8,128)(2,1)} %all-gather.5.cloned.1.call-done.tok_ref, ...), custom_call_target="tpu_custom_call" | custom-call | flops 6039797760 | bytes 23592960 | tf_op jit(solution)/shard_map/mixer_forward/pallas_call | solution.py:281
  142.9 7.3 %all-gather.11.cloned.1.call-done.wout_ref = bf16[1536,768]{1,0:T(8,128)(2,1)} async-done(((bf16[192,768]{1,0:T(8,128)(2,1)}), bf16[1536,768]{1,0:T(8,128)(2,1)}) %all-gather.11.cloned.1.call-update) | async-done | bytes 2359312 | tf_op jit(solution)/shard_map/all_gather | solution.py:448
  150.3 62.0 %all-gather.9.cloned.1.call-done.cot_ref = bf16[1024,1536]{1,0:T(8,128)(2,1)} async-done(((bf16[256,1536]{1,0:T(8,128)(2,1)}), bf16[1024,1536]{1,0:T(8,128)(2,1)}) %all-gather.9.cloned.1.call-update) | async-done | bytes 3145744 | tf_op jit(solution)/shard_map/all_gather | solution.py:449
  212.2 1.9 copy-done
  214.1 1.9 copy-done.2
  216.0 1.7 copy-done.4
  217.7 1.0 copy-done.6
  218.7 3.6 gate_stats.1
  222.3 1.6 copy-done.9
  223.9 13.1 %psum.28.stats_ref = f32[8,1024]{1,0:T(8,128)S(1)} all-reduce(f32[8,1024]{1,0:T(8,128)S(1)} %get-tuple-element.35), channel_id=1, replica_groups=mesh['fsdp'=8,'tp'=4] {'tp'}, use_global_device_ids=true, to_apply=%region_0.1 | all-reduce | flops 8192 | bytes 65536 | tf_op jit(solution)/shard_map/psum | solution.py:460
  237.1 1.7 copy-done.5
  238.7 4.9 output_part.1
  243.6 3.0 fusion
  246.6 2.5 copy.52
  249.4 39.6 %mixer_backward.1 = (bf16[1024,1920]{1,0:T(8,128)(2,1)}, bf16[1024,1536]{1,0:T(8,128)(2,1)}, f32[8,1024]{1,0:T(8,128)}, f32[1,1024]{1,0:T(1,128)}, f32[8,128]{1,...) custom-call(s32[4]{0:T(128)} %open_ref.3, bf16[1024,1536]{1,0:T(8,128)(2,1)} %all-gather.5.cloned.1.call-done.tok_ref, ...), custom_call_target="tpu_custom_call" | custom-call | flops 12079595520 | bytes 23592960 | tf_op jit(solution)/shard_map/mixer_backward/pallas_call | solution.py:325
  289.1 0.7 reduce-scatter.7.cloned.1.call-update
  289.8 1.3 copy-done.28
  291.1 10.5 %convolution_convert_fusion = bf16[1536,1920]{1,0:T(8,128)(2,1)} fusion(bf16[1024,1536]{1,0:T(8,128)(2,1)S(1)} %copy-done.28, bf16[1024,1920]{1,0:T(8,128)(2,1)} %get-tuple-element.48), kind=kOutput, calls=%fused_computation | convolution fusion | flops 6042746880 | bytes 12976128 | tf_op jit(solution)/shard_map/td,tc->dc/dot_general | solution.py:467
  301.7 0.6 copy-done.19
  302.4 0.7 slice.117
  303.2 0.7 constant_dynamic-update-slice_fusion.7
  304.0 25.3 %psum.29 = f32[8448]{0:T(1024)S(1)} all-reduce(f32[8448]{0:T(1024)S(1)} %constant_dynamic-update-slice_fusion.3), channel_id=1, replica_groups=mesh['fsdp'=8,'tp'=4] {'fsdp'}, use_global_device_ids=true, to_apply=%region_5.6 | all-reduce | flops 8448 | bytes 67584 | tf_op jit(solution)/shard_map/psum | solution.py:474
  329.3 17.4 %psum.30 = f32[2816]{0:T(1024)S(1)} all-reduce(f32[2816]{0:T(1024)S(1)} %slice.139), channel_id=1, replica_groups=mesh['fsdp'=8,'tp'=4] {'tp'}, use_global_device_ids=true, to_apply=%region_6.7 | all-reduce | flops 2816 | bytes 22528 | tf_op jit(solution)/shard_map/psum | solution.py:476
  347.2 0.6 slice.140
  347.8 0.6 slice.127
  349.7 0.6 reduce_sum.29
  350.9 1.2 copy.53
  352.1 1.1 copy.51
  353.2 5.5 %reduce-scatter.9.cloned.1.call-done = bf16[256,1536]{1,0:T(8,128)(2,1)} async-done(((bf16[1024,1536]{1,0:T(8,128)(2,1)}), bf16[256,1536]{1,0:T(8,128)(2,1)}) %reduce-scatter.9.cloned.1.call-update) | async-done | bytes 786448 | tf_op jit(solution)/shard_map/reduce_scatter | solution.py:466
  358.8 1.6 fusion.2
  360.4 60.9 %reduce-scatter.7.cloned.1.call-done = bf16[256,1536]{1,0:T(8,128)(2,1)} async-done(((bf16[1024,1536]{1,0:T(8,128)(2,1)}), bf16[256,1536]{1,0:T(8,128)(2,1)}) %reduce-scatter.7.cloned.1.call-update) | async-done | bytes 786448 | tf_op jit(solution)/shard_map/reduce_scatter | solution.py:462
  421.3 3.0 fusion.5
  424.3 60.5 %reduce-scatter.11.cloned.1.call-done = bf16[192,1920]{1,0:T(8,128)(2,1)} async-done(((bf16[1536,1920]{1,0:T(8,128)(2,1)}), bf16[192,1920]{1,0:T(8,128)(2,1)}) %reduce-scatter.11.cloned.1.call-update) | async-done | bytes 737296 | tf_op jit(solution)/shard_map/reduce_scatter | solution.py:469
  484.9 0.9 slice.144
  485.7 0.7 copy.50
  486.4 1.6 slice.143
  488.0 1.1 fusion.11
  489.1 32.0 %all-reduce.5.cloned.1.call-done = f32[192,256]{1,0:T(8,128)} async-done(((f32[192,256]{1,0:T(8,128)}), f32[192,256]{1,0:T(8,128)}) %all-reduce.5.cloned.1.call-update) | async-done | bytes 196624 | tf_op jit(solution)/shard_map/psum | solution.py:476
  521.2 1.6 copy.63
  (101 shorter events, 5.2 us)
Async XLA Ops:
  7.2 64.5 %all-gather.5.cloned.1.call-start = ((), (), s32[]{:S(2)}) async-start(), calls=%async_computation.4 | async-start | bytes 3932160 | tf_op jit(solution)/shard_map/all_gather | solution.py:446
  7.9 111.6 %all-gather.7.cloned.1.call-start = ((), (), s32[]{:S(2)}) async-start(), calls=%async_computation.5 | async-start | bytes 6635520 | tf_op jit(solution)/shard_map/all_gather | solution.py:447
  8.8 3.5 copy-start.20
  8.8 3.5 copy-start.21
  8.8 3.5 copy-start.14
  8.8 4.1 copy-start.25
  10.9 3.9 copy-start.22
  10.9 3.9 copy-start.24
  10.9 4.5 copy-start.15
  10.9 4.5 copy-start.23
  10.9 4.5 copy-start.27
  10.9 4.6 copy-start.26
  10.9 139.3 %all-gather.11.cloned.1.call-start = ((), (), s32[]{:S(2)}) async-start(), calls=%async_computation.7 | async-start | bytes 2654208 | tf_op jit(solution)/shard_map/all_gather | solution.py:448
  11.7 200.6 %all-gather.9.cloned.1.call-start = ((), (), s32[]{:S(2)}) async-start(), calls=%async_computation.6 | async-start | bytes 3932160 | tf_op jit(solution)/shard_map/all_gather | solution.py:449
  12.2 338.6 %reduce-scatter.13.cloned.1.call-start = ((), (), s32[]{:S(2)}) async-start(), calls=%async_computation.12 | async-start | bytes 2654208
  12.3 224.7 %copy-start.8 = (f32[1,768]{1,0:T(1,128)}, f32[1,768]{1,0:T(1,128)S(1)}, u32[]{:S(2)}) copy-start(f32[1,768]{1,0:T(1,128)S(1)} %broadcast_in_dim.34.gate_ref) | copy-start | bytes 9220
  15.4 104.1 %copy-start.16 = (f32[4,1024]{1,0:T(4,128)}, f32[4,1024]{1,0:T(4,128)S(1)}, u32[]{:S(2)}) copy-start(f32[4,1024]{1,0:T(4,128)S(1)} %constant_dynamic-update-slice_fusion.taps_ref) | copy-start | bytes 49156
  212.2 1.9 copy-start
  214.1 1.9 copy-start.2
  216.0 1.7 copy-start.4
  217.7 1.0 copy-start.6
  218.7 18.3 %copy-start.3 = (f32[1024,768]{1,0:T(8,128)S(1)}, f32[1024,768]{1,0:T(8,128)}, u32[]{:S(2)}) copy-start(f32[1024,768]{1,0:T(8,128)} %get-tuple-element.33.gated_ref) | copy-start | bytes 9437188
  222.3 1.6 copy-start.9
  237.1 1.7 copy-start.5
  238.7 4.9 copy-start.7
  238.7 4.9 copy-start.1
  249.1 109.6 %reduce-scatter.9.cloned.1.call-start = ((), (), s32[]{:S(2)}) async-start(), calls=%async_computation.9 | async-start | bytes 3932160 | tf_op jit(solution)/shard_map/reduce_scatter | solution.py:466
  289.0 132.3 %reduce-scatter.7.cloned.1.call-start = ((), (), s32[]{:S(2)}) async-start(), calls=%async_computation.8 | async-start | bytes 3932160 | tf_op jit(solution)/shard_map/reduce_scatter | solution.py:462
  289.1 2.0 copy-start.28
  289.8 195.1 %reduce-scatter.11.cloned.1.call-start = ((), (), s32[]{:S(2)}) async-start(), calls=%async_computation.10 | async-start | bytes 6635520 | tf_op jit(solution)/shard_map/reduce_scatter | solution.py:469
  301.6 0.7 copy-start.19
  301.6 0.8 copy-start.17
  301.6 1.6 copy-start.18
  301.6 219.5 %all-reduce.5.cloned.1.call-start = ((), (), s32[]{:S(2)}) async-start(), calls=%async_computation.11 | async-start | bytes 393216 | tf_op jit(solution)/shard_map/psum | solution.py:476
  350.9 7.9 %copy-start.10 = (bf16[256,1536]{1,0:T(8,128)(2,1)S(1)}, bf16[256,1536]{1,0:T(8,128)(2,1)}, u32[]{:S(2)}) copy-start(bf16[256,1536]{1,0:T(8,128)(2,1)} %param.18) | copy-start | bytes 2359300
  352.1 69.2 %copy-start.11 = (bf16[256,1536]{1,0:T(8,128)(2,1)S(1)}, bf16[256,1536]{1,0:T(8,128)(2,1)}, u32[]{:S(2)}) copy-start(bf16[256,1536]{1,0:T(8,128)(2,1)} %param.19) | copy-start | bytes 2359300
  358.8 62.6 %copy-start.12 = (bf16[256,1536]{1,0:T(8,128)(2,1)S(1)}, bf16[256,1536]{1,0:T(8,128)(2,1)}, u32[]{:S(2)}) copy-start(bf16[256,1536]{1,0:T(8,128)(2,1)} %reduce-scatter.9.cloned.1.call-done) | copy-start | bytes 2359300
  484.9 3.2 copy-start.13
Sparse Core Ops, SparseCore 0:
  9.6 62.0 all-gather.4
  74.1 45.2 all-gather.6
  121.4 28.8 all-gather.10
  151.7 60.5 all-gather.8
  249.3 46.8 reduce-scatter.12
  298.3 60.3 reduce-scatter.8
  361.1 60.2 reduce-scatter.6
  424.8 60.0 reduce-scatter.10
  488.1 32.9 all-reduce.4

commit v2 on v1

--- a/solution.py
+++ b/solution.py
@@ -430,6 +430,422 @@
     return jnp.pad(v[None, :], ((0, 0), (0, LANES - v.shape[0])), constant_values=fill)
 
 
+MESH = pl.DeviceIdType.MESH
+TAGS = {"entry": 1, "stats": 2, "exit": 3}
+
+
+def remote(source, target, send, recv, **where):
+    return pltpu.make_async_remote_copy(
+        src_ref=source, dst_ref=target, send_sem=send, recv_sem=recv, device_id=where, device_id_type=MESH
+    )
+
+
+def rows_at(ref, index, count):
+    return ref.at[pl.ds(pl.multiple_of(index * count, count), count)]
+
+
+def greet(axis, peers):
+    barrier = pltpu.get_barrier_semaphore()
+    for peer in peers:
+        pl.semaphore_signal(barrier, inc=1, device_id={axis: peer}, device_id_type=MESH)
+
+
+def greet_line(tp, n_tp):
+    barrier = pltpu.get_barrier_semaphore()
+
+    @pl.when(tp > 0)
+    def _():
+        pl.semaphore_signal(barrier, inc=1, device_id={"tp": tp - 1}, device_id_type=MESH)
+
+    @pl.when(tp < n_tp - 1)
+    def _():
+        pl.semaphore_signal(barrier, inc=1, device_id={"tp": tp + 1}, device_id_type=MESH)
+
+    return jnp.where(tp > 0, 1, 0) + jnp.where(tp < n_tp - 1, 1, 0)
+
+
+class Line:
+    def __init__(self, tp, n_tp, own, whole_ref, send, recv):
+        self.tp, self.n, self.own, self.whole_ref, self.send, self.recv = tp, n_tp, own, whole_ref, send, recv
+        self.count = own.shape[0]
+
+    def copy(self, way, step, own=False):
+        shift = -1 if way == 0 else 1
+        index = self.tp + shift * step
+        slot = rows_at(self.whole_ref, index, self.count)
+        return remote(
+            self.own if own else slot, slot, self.send.at[way, step], self.recv.at[way, step], tp=self.tp - shift
+        )
+
+    def sends(self, way, step):
+        if way == 0:
+            return jnp.logical_and(self.tp < self.n - 1, self.tp >= step)
+        return jnp.logical_and(self.tp > 0, self.tp + step <= self.n - 1)
+
+    def takes(self, way, step):
+        return self.tp >= step + 1 if way == 0 else self.tp + step + 1 <= self.n - 1
+
+    def start(self, way, step):
+        @pl.when(self.sends(way, step))
+        def _():
+            self.copy(way, step, own=step == 0).start()
+
+    def arrive(self, way, step):
+        @pl.when(self.takes(way, step))
+        def _():
+            shift = -1 if way == 0 else 1
+            slot = rows_at(self.whole_ref, self.tp + shift * (step + 1), self.count)
+            remote(
+                slot, slot, self.send.at[way, step], self.recv.at[way, step], tp=self.tp + shift
+            ).wait_recv()
+
+    def finish(self, way, step):
+        @pl.when(self.sends(way, step))
+        def _():
+            self.copy(way, step, own=step == 0).wait_send()
+
+
+def entry_kernel(
+    tok_ref, pin_ref, pout_ref, tok_all, w_in, w_out, own_sem, z_send, z_recv, f_send, f_recv, p_send, p_recv,
+    *, n_tp, n_fs,
+):
+    tp, me = lax.axis_index("tp"), lax.axis_index("fsdp")
+    chip, core, chips = me // 2, me % 2, n_fs // 2
+    partner = chip * 2 + 1 - core
+    greet("fsdp", [((chip + d) % chips) * 2 + core for d in range(1, chips)] + [partner])
+    line_count = greet_line(tp, n_tp)
+    pl.semaphore_wait(pltpu.get_barrier_semaphore(), chips + line_count)
+
+    packs = ((pin_ref, w_in), (pout_ref, w_out))
+    count = pin_ref.shape[0]
+    line = Line(tp, n_tp, tok_ref, tok_all, z_send, z_recv)
+    for way in range(2):
+        line.start(way, 0)
+    for j, (pack, full) in enumerate(packs):
+        for d in range(1, chips):
+            remote(
+                pack, rows_at(full, me, count), f_send.at[j, d], f_recv.at[j, d], fsdp=((chip + d) % chips) * 2 + core
+            ).start()
+        remote(pack, rows_at(full, me, count), p_send.at[j, 0], p_recv.at[j, 0], fsdp=partner).start()
+    own = [
+        pltpu.make_async_copy(tok_ref, rows_at(tok_all, tp, tok_ref.shape[0]), own_sem.at[0]),
+        pltpu.make_async_copy(pin_ref, rows_at(w_in, me, count), own_sem.at[1]),
+        pltpu.make_async_copy(pout_ref, rows_at(w_out, me, count), own_sem.at[2]),
+    ]
+    for copy in own:
+        copy.start()
+    for step in range(n_tp - 1):
+        for way in range(2):
+            line.arrive(way, step)
+            if step + 1 < n_tp - 1:
+                line.start(way, step + 1)
+        if step == n_tp - 3 or n_tp < 3 and step == 0:
+            for j, (pack, full) in enumerate(packs):
+                for d in range(1, chips):
+                    slot = rows_at(full, ((chip + chips - d) % chips) * 2 + core, count)
+                    remote(slot, slot, f_send.at[j, d], f_recv.at[j, d], fsdp=partner).wait_recv()
+                    remote(slot, slot, p_send.at[j, d], p_recv.at[j, d], fsdp=partner).start()
+    for j, (pack, full) in enumerate(packs):
+        for d in range(chips):
+            slot = rows_at(full, ((chip + chips - d) % chips) * 2 + 1 - core, count)
+            remote(slot, slot, p_send.at[j, d], p_recv.at[j, d], fsdp=partner).wait()
+        for d in range(1, chips):
+            remote(pack, rows_at(full, me, count), f_send.at[j, d], f_recv.at[j, d], fsdp=partner).wait_send()
+    for step in range(n_tp - 1):
+        for way in range(2):
+            line.finish(way, step)
+    for copy in own:
+        copy.wait()
+
+
+def entry(tokens, pack_in, pack_out, n_tp, n_fs):
+    rows, width = tokens.shape
+    count, cols = pack_in.shape
+    chan = pack_out.shape[1]
+    dma = pltpu.SemaphoreType.DMA
+    anywhere = pl.BlockSpec(memory_space=pl.ANY)
+    vmem = pl.BlockSpec(memory_space=pltpu.VMEM)
+    chips = n_fs // 2
+    sent = 2 * (n_tp * rows * width + n_fs * count * (cols + chan))
+    return pl.pallas_call(
+        functools.partial(entry_kernel, n_tp=n_tp, n_fs=n_fs),
+        name="entry",
+        in_specs=[vmem] * 3,
+        out_specs=[anywhere] * 3,
+        out_shape=[
+            jax.ShapeDtypeStruct((rows * n_tp, width), BF16),
+            jax.ShapeDtypeStruct((count * n_fs, cols), BF16),
+            jax.ShapeDtypeStruct((count * n_fs, chan), BF16),
+        ],
+        scratch_shapes=[
+            dma((3,)), dma((2, n_tp - 1)), dma((2, n_tp - 1)), dma((2, chips)), dma((2, chips)), dma((2, chips)),
+            dma((2, chips)),
+        ],
+        cost_estimate=pl.CostEstimate(flops=0, bytes_accessed=sent * 8, transcendentals=0),
+        compiler_params=pltpu.CompilerParams(
+            collective_id=TAGS["entry"], has_side_effects=True, vmem_limit_bytes=16 << 20
+        ),
+    )(tokens, pack_in, pack_out)
+
+
+def exchange_kernel(part_ref, total_ref, held, send, recv, *, n_tp):
+    tp = lax.axis_index("tp")
+    greet("tp", [(tp + d) % n_tp for d in range(1, n_tp)])
+    pl.semaphore_wait(pltpu.get_barrier_semaphore(), n_tp - 1)
+    copies = [
+        remote(part_ref, held.at[tp], send.at[d], recv.at[d], tp=(tp + d) % n_tp) for d in range(1, n_tp)
+    ]
+    for copy in copies:
+        copy.start()
+    held[tp] = part_ref[...]
+    for d in range(1, n_tp):
+        slot = held.at[(tp + n_tp - d) % n_tp]
+        remote(slot, slot, send.at[d], recv.at[d], tp=(tp + d) % n_tp).wait_recv()
+    total = held[0]
+    for peer in range(1, n_tp):
+        total = total + held[peer]
+    total_ref[...] = total
+    for copy in copies:
+        copy.wait_send()
+
+
+def exchange(part, n_tp):
+    dma = pltpu.SemaphoreType.DMA
+    vmem = pl.BlockSpec(memory_space=pltpu.VMEM)
+    return pl.pallas_call(
+        functools.partial(exchange_kernel, n_tp=n_tp),
+        name="stats_exchange",
+        in_specs=[vmem],
+        out_specs=vmem,
+        out_shape=jax.ShapeDtypeStruct(part.shape, F32),
+        scratch_shapes=[pltpu.VMEM((n_tp,) + part.shape, F32), dma((n_tp,)), dma((n_tp,))],
+        compiler_params=pltpu.CompilerParams(
+            collective_id=TAGS["stats"], has_side_effects=True, vmem_limit_bytes=4 << 20
+        ),
+    )(part)
+
+
+def add_into(target, *sources):
+    rows, tile = target.shape[0], 32
+
+    @pl.loop(0, rows // tile)
+    def _(i):
+        at = pl.ds(pl.multiple_of(i * tile, tile), tile)
+        total = sources[0][at, :].astype(F32)
+        for source in sources[1:]:
+            total = total + source[at, :].astype(F32)
+        target[at, :] = total.astype(target.dtype)
+
+
+def exit_kernel(
+    dn_ref, gin_ref, gout_ref, mine_ref, shared_ref,
+    dn_out, z_out, x_out, bc_out, dt_out, out_out, mine_out, shared_out,
+    z_held, z_got, near_in, near_out, far_in, far_out, got_in, got_out, mine_got, shared_got, shared_held, shared_z,
+    bc_held, bc_got,
+    zs, zr, ns, nr, fs, fr, ms, mr, ss, sr, ts, tr, bs, br,
+    *, n_tp, n_fs,
+):
+    tp, me = lax.axis_index("tp"), lax.axis_index("fsdp")
+    chip, core, chips = me // 2, me % 2, n_fs // 2
+    partner = chip * 2 + 1 - core
+    chan = gout_ref.shape[1]
+    cols = gin_ref.shape[1]
+    block, count = dn_out.shape[0], z_out.shape[0]
+    greet("fsdp", [(me + d) % n_fs for d in range(1, n_fs)])
+    greet("tp", [(tp + d) % n_tp for d in range(1, n_tp)])
+    pl.semaphore_wait(pltpu.get_barrier_semaphore(), n_fs - 1 + n_tp - 1)
+
+    def ahead(way, step):
+        return n_tp - 1 - step if way == 0 else step
+
+    def passes(way, step):
+        return ahead(way, step) > tp if way == 0 else ahead(way, step) < tp
+
+    def first(way):
+        return tp == 0 if way == 0 else tp == n_tp - 1
+
+    def pass_on(way, step):
+        towards = tp + 1 if way == 0 else tp - 1
+        return remote(z_held.at[way, step], z_got.at[way, step], zs.at[way, step], zr.at[way, step], tp=towards)
+
+    for way in range(2):
+        @pl.when(first(way))
+        def _():
+            for step in range(n_tp - 1):
+                towards = tp + 1 if way == 0 else tp - 1
+                remote(
+                    rows_at(dn_ref, ahead(way, step), block), z_got.at[way, step], zs.at[way, step], zr.at[way, step],
+                    tp=towards,
+                ).start()
+
+    parts = (
+        (gin_ref, slice(2 * chan, cols), near_in, far_in, got_in),
+        (gin_ref, slice(0, 2 * chan), near_in, far_in, got_in),
+        (gout_ref, slice(0, chan), near_out, far_out, got_out),
+    )
+
+    def near(j, d):
+        source, span, held, _, _ = parts[j]
+        rows = rows_at(source, ((chip + d) % chips) * 2 + 1 - core, count)
+        return remote(rows.at[:, span], held.at[d, :, span], ns.at[j, d], nr.at[j, d], fsdp=partner)
+
+    def far(j, d):
+        _, span, _, held, got = parts[j]
+        return remote(
+            held.at[d, :, span], got.at[d, :, span], fs.at[j, d], fr.at[j, d], fsdp=((chip + d) % chips) * 2 + core
+        )
+
+    order = [d for d in range(1, chips)]
+    for j in range(3):
+        for d in order + [0]:
+            near(j, d).start()
+
+    def small(d):
+        peer = (me + d) % n_fs
+        return (
+            remote(mine_ref, mine_got.at[me], ms.at[d], mr.at[d], fsdp=peer),
+            remote(shared_ref, shared_got.at[me], ss.at[d], sr.at[d], fsdp=peer),
+        )
+
+    for d in range(1, n_fs):
+        for copy in small(d):
+            copy.start()
+    mine_got[me] = mine_ref[...]
+    shared_got[me] = shared_ref[...]
+
+    for j in range(3):
+        source, span, held, summed, _ = parts[j]
+        for d in order:
+            near(j, d).wait_recv()
+            rows = rows_at(source, ((chip + d) % chips) * 2 + core, count)
+            add_into(summed.at[d, :, span], rows.at[:, span], held.at[d, :, span])
+            far(j, d).start()
+        near(j, 0).wait_recv()
+
+    def relay(step):
+        for way in range(2):
+            @pl.when(jnp.logical_and(passes(way, step), jnp.logical_not(first(way))))
+            def _():
+                pass_on(way, step).wait_recv()
+                add_into(z_held.at[way, step], rows_at(dn_ref, ahead(way, step), block), z_got.at[way, step])
+                pass_on(way, step).start()
+
+    if n_tp > 2:
+        relay(0)
+    for d in range(1, n_fs):
+        for copy in small(d):
+            copy.wait_recv()
+    total, again = mine_got[0], shared_got[0]
+    for peer in range(1, n_fs):
+        total, again = total + mine_got[peer], again + shared_got[peer]
+    mine_out[...] = total
+    shared_held[...] = again
+    shared_z[tp] = again
+    for d in range(1, n_tp):
+        remote(shared_held, shared_z.at[tp], ts.at[d], tr.at[d], tp=(tp + d) % n_tp).start()
+    for step in range(1, n_tp - 2):
+        relay(step)
+
+    def settle(j, target, span):
+        source, _, held, _, got = parts[j]
+        rows = rows_at(source, me, count)
+        add_into(
+            target, rows.at[:, span], held.at[0, :, span], *[got.at[d, :, span] for d in order]
+        )
+
+    for d in order:
+        far(0, d).wait_recv()
+    settle(0, bc_held, slice(2 * chan, 2 * chan + 2 * STATE))
+    settle(0, dt_out, slice(2 * chan + 2 * STATE, cols))
+    bc_got[tp] = bc_held[...]
+    for d in range(1, n_tp):
+        remote(bc_held, bc_got.at[tp], bs.at[d], br.at[d], tp=(tp + d) % n_tp).start()
+    for j in (1, 2):
+        for d in order:
+            far(j, d).wait_recv()
+    settle(1, z_out, slice(0, chan))
+    settle(1, x_out, slice(chan, 2 * chan))
+    settle(2, out_out, slice(0, chan))
+    for d in range(1, n_tp):
+        peer = (tp + n_tp - d) % n_tp
+        remote(shared_held, shared_z.at[peer], ts.at[d], tr.at[d], tp=peer).wait_recv()
+        remote(bc_held, bc_got.at[peer], bs.at[d], br.at[d], tp=peer).wait_recv()
+    total = shared_z[0]
+    for peer in range(1, n_tp):
+        total = total + shared_z[peer]
+    shared_out[...] = total
+    add_into(bc_out, *[bc_got.at[peer] for peer in range(n_tp)])
+
+    own = rows_at(dn_ref, tp, block)
+    for way in range(2):
+        for step in range(n_tp - 1):
+            @pl.when(jnp.logical_and(ahead(way, step) == tp, jnp.logical_not(first(way))))
+            def _():
+                pass_on(way, step).wait_recv()
+
+    for value in range(n_tp):
+        @pl.when(tp == value)
+        def _():
+            incoming = []
+            if value > 0:
+                incoming.append(z_got.at[0, n_tp - 1 - value])
+            if value < n_tp - 1:
+                incoming.append(z_got.at[1, value])
+            add_into(dn_out, own, *incoming)
+
+    for way in range(2):
+        for step in range(n_tp - 1):
+            @pl.when(passes(way, step))
+            def _():
+                pass_on(way, step).wait_send()
+    for j in range(3):
+        for d in range(chips):
+            near(j, d).wait_send()
+        for d in order:
+            far(j, d).wait_send()
+    for d in range(1, n_fs):
+        for copy in small(d):
+            copy.wait_send()
+    for d in range(1, n_tp):
+        remote(shared_held, shared_z.at[tp], ts.at[d], tr.at[d], tp=(tp + d) % n_tp).wait_send()
+        remote(bc_held, bc_got.at[tp], bs.at[d], br.at[d], tp=(tp + d) % n_tp).wait_send()
+
+
+def leave(dn, grad_in, grad_out, mine, shared, n_tp, n_fs):
+    block, width = dn.shape[0] // n_tp, dn.shape[1]
+    count, cols = grad_in.shape[0] // n_fs, grad_in.shape[1]
+    chan = grad_out.shape[1]
+    chips = n_fs // 2
+    dma = pltpu.SemaphoreType.DMA
+    vmem = pl.BlockSpec(memory_space=pltpu.VMEM)
+    room = lambda *shape: pltpu.VMEM(shape, BF16)
+    shape = lambda *extents: jax.ShapeDtypeStruct(extents, F32)
+    return pl.pallas_call(
+        functools.partial(exit_kernel, n_tp=n_tp, n_fs=n_fs),
+        name="exit",
+        in_specs=[vmem] * 5,
+        out_specs=[vmem] * 8,
+        out_shape=[
+            shape(block, width), shape(count, chan), shape(count, chan), shape(count, 2 * STATE), shape(count, LANES),
+            shape(count, chan), shape(*mine.shape), shape(*shared.shape),
+        ],
+        scratch_shapes=[
+            room(2, n_tp - 1, block, width), room(2, n_tp - 1, block, width),
+            room(chips, count, cols), room(chips, count, chan), room(chips, count, cols), room(chips, count, chan),
+            room(chips, count, cols), room(chips, count, chan),
+            pltpu.VMEM((n_fs,) + mine.shape, F32), pltpu.VMEM((n_fs,) + shared.shape, F32),
+            pltpu.VMEM(shared.shape, F32), pltpu.VMEM((n_tp,) + shared.shape, F32),
+            room(count, 2 * STATE), room(n_tp, count, 2 * STATE),
+            dma((2, n_tp - 1)), dma((2, n_tp - 1)), dma((3, chips)), dma((3, chips)), dma((3, chips)), dma((3, chips)),
+            dma((n_fs,)), dma((n_fs,)), dma((n_fs,)), dma((n_fs,)), dma((n_tp,)), dma((n_tp,)), dma((n_tp,)),
+            dma((n_tp,)),
+        ],
+        compiler_params=pltpu.CompilerParams(
+            collective_id=TAGS["exit"], has_side_effects=True, vmem_limit_bytes=62 << 20
+        ),
+    )(dn, grad_in, grad_out, mine, shared)
+
+
 def shards(
     tokens, cotangent, seq_start, token_valid, norm_gain, proj_z, proj_x, proj_bc, proj_dt, conv_chan, bias_chan,
     conv_shared, bias_shared, a_log, dt_bias, skip_gain, gate_gain, proj_out,
@@ -443,10 +859,10 @@
     pack_in = jnp.concatenate(
         [proj_z, proj_x, proj_bc, jnp.pad(proj_dt, ((0, 0), (0, LANES - heads_here)))], axis=1
     )
-    tok_all = lax.all_gather(tokens, "tp", axis=0, tiled=True)
-    w_in = lax.all_gather(pack_in, "fsdp", axis=0, tiled=True)
-    w_out = lax.all_gather(proj_out.T, "fsdp", axis=0, tiled=True)
-    cot_all = lax.all_gather(cotangent, "tp", axis=0, tiled=True)
+    n_tp, n_fs = lax.axis_size("tp"), lax.axis_size("fsdp")
+    tok_all, w_in, w_out = entry(tokens, pack_in, proj_out.T, n_tp, n_fs)
+    late_cot, _ = lax.optimization_barrier((cotangent, tok_all))
+    cot_all = lax.all_gather(late_cot, "tp", axis=0, tiled=True)
     decay = -jnp.exp(a_log)
     heads = jnp.concatenate([padded(dt_bias, -100.0), padded(decay, 0.0), jnp.zeros((6, LANES), F32)], axis=0)
     taps = jnp.concatenate([conv_chan, conv_shared], axis=1)
@@ -457,23 +873,22 @@
         seq_start, tok_all, valid, norm_gain[None, :], w_in, taps, bias, heads, skip
     )
     dgn, stats = gate_stats(cot_all, w_out, gate, gated, sq)
-    stats = lax.psum(stats, "tp")
+    stats = exchange(stats, n_tp)
     gnormed, out_rows = output_part(gated, stats, gate, w_out, inner)
     mixed = lax.psum_scatter(out_rows, "tp", scatter_dimension=0, tiled=True)
     dpre, dn_rows, dtaps, dbias, dhead, dchan, dgain = mixer_backward(
         seq_start, tok_all, valid, w_in, taps, bias, heads, skip, gate, pre, y, enter, dgn, stats, inner
     )
-    d_normed = lax.psum_scatter(dn_rows, "tp", scatter_dimension=0, tiled=True).astype(F32)
     grad_in = jnp.einsum("td,tc->dc", normed, dpre, preferred_element_type=F32).astype(BF16)
     grad_out = jnp.einsum("td,tc->dc", cot_all, gnormed, preferred_element_type=F32).astype(BF16)
-    own_in = lax.psum_scatter(grad_in, "fsdp", scatter_dimension=0, tiled=True).astype(F32)
-    own_out = lax.psum_scatter(grad_out, "fsdp", scatter_dimension=0, tiled=True).astype(F32)
-    mine = jnp.concatenate([v.reshape(-1) for v in (dtaps[0:4, :chan], dbias[:, :chan], dhead[0:2], dchan[0:2])])
-    shared = jnp.concatenate([v.reshape(-1) for v in (dtaps[0:4, chan:], dbias[:, chan:], dgain)])
-    split = mine.shape[0]
-    both = lax.psum(jnp.concatenate([mine, shared]), "fsdp")
-    mine = both[:split]
-    shared, own_bc = lax.psum((both[split:], own_in[:, 2 * chan:wide + chan]), "tp")
+    pack = lambda *vs: jnp.concatenate([v.reshape(-1) for v in vs])
+    mine = pack(dtaps[0:4, :chan], dbias[:, :chan], dhead[0:2], dchan[0:2])
+    shared = pack(dtaps[0:4, chan:], dbias[:, chan:], dgain)
+    tiles = lambda v: jnp.pad(v, (0, -v.shape[0] % (8 * LANES))).reshape(-1, LANES)
+    d_normed, own_z, own_x, own_bc, own_dt, own_out, mine, shared = leave(
+        dn_rows, grad_in, grad_out, tiles(mine), tiles(shared), n_tp, n_fs
+    )
+    mine, shared = mine.reshape(-1), shared.reshape(-1)
     at = 0
 
     def take(source, *shape):
@@ -499,8 +914,7 @@
         - resid * (rstd * rstd * rstd) * jnp.mean(scaled_in * resid, axis=1, keepdims=True)
     ).astype(BF16)
     return (
-        output, grad_tokens, g_gain, own_in[:, :chan], own_in[:, chan:2 * chan], own_bc,
-        own_in[:, wide + chan:wide + chan + heads_here], g_taps, g_bias, g_taps_s, g_bias_s,
+        output, grad_tokens, g_gain, own_z, own_x, own_bc, own_dt[:, :heads_here], g_taps, g_bias, g_taps_s, g_bias_s,
         g_heads[0, :heads_here], g_heads[1, :heads_here], g_chan[1].reshape(heads_here, HEAD).sum(axis=1),
         g_chan[0], own_out.T,
     )

time: 534 us -> 334 us (0.63)
  waiting for transfers between devices: 334 us -> 35.4 us
  Pallas kernels: 71.6 us -> 222 us
  blocking collectives: 55.8 us -> 0 us
    pallas_call x0 -> x3, Pallas kernels: none -> 151 us  [the longest x1 90.8 us: leave(): pl.pallas_call(functools.partial(exit_kernel, n_tp=n_tp, n_fs=n_fs), name...]
    all_gather x4 -> x1, waiting for transfers between devices: 173 us -> 35.3 us  [shards(): cot_all = lax.all_gather(late_cot, 'tp', axis=0, tiled=True)]
    reduce_scatter x2 -> x0, waiting for transfers between devices: 66.1 us -> none  [the longest x1 60.5 us: shards(): lax.psum_scatter(grad_in, 'fsdp', scatter_dimension=0, tiled=True)]
    reduce_scatter x1, waiting for transfers between devices: 60.9 us -> 0.01 us  [shards(): mixed = lax.psum_scatter(out_rows, 'tp', scatter_dimension=0, tiled=True)]
    psum x3 -> x0, blocking collectives: 55.8 us -> none  [the longest x1 25.3 us: shards(): both = lax.psum(jnp.concatenate([mine, shared]), 'fsdp')]
    psum x1 -> x0, waiting for transfers between devices: 32 us -> none  [shards(): lax.psum((both[split:], own_in[:, 2 * chan:wide + chan]), 'tp')]
    unnamed x73 -> x75, local copies, waits for them, and re-layouts: 20.4 us -> 20.4 us
  transfers between devices with their start and end apart: 9 -> 2, of which waited for: 8 -> 1; matrix products, arithmetic and copies ran while one was open for 6% -> 11% of each run, Pallas kernels for 12% -> 47%
where the time goes in v2:
time: 334 us; the launch traced here: 330 us
  Pallas kernels  222 us (66%)
  waiting for transfers between devices  35.4 us (11%)
  local copies, waits for them, and re-layouts  33.6 us (10%)
  matrix products  14.7 us (4%)
  between operations  14.4 us (4%)
  other arithmetic  9.76 us (3%)
    pallas_call x1, Pallas kernels, leave(): pl.pallas_call(functools.partial(exit_kernel, n_tp=n_tp, n_fs=n_fs), name...  90.8 us
    pallas_call x1, Pallas kernels, entry(): pl.pallas_call(functools.partial(entry_kernel, n_tp=n_tp, n_fs=n_fs), nam...  53.7 us
    pallas_call x1, Pallas kernels, mixer_backward(): pl.pallas_call(functools.partial(backward_kernel, inner=inner), name='mix...  40 us
    all_gather x1, waiting for transfers between devices, shards(): cot_all = lax.all_gather(late_cot, 'tp', axis=0, tiled=True)  35.3 us
    pallas_call x1, Pallas kernels, mixer_forward(): pl.pallas_call(forward_kernel, name='mixer_forward', grid_spec=pltpu.Pref...  23.5 us
    unnamed x75, local copies, waits for them, and re-layouts  20.4 us
    dot_general x1, matrix products, shards(): jnp.einsum('td,tc->dc', normed, dpre, preferred_element_type=F32)  8.52 us
  transfers between devices with their start and end apart: 2, of which 1 were waited for; matrix products, arithmetic and copies ran while one was open for 11% of the time, Pallas kernels for 47%

profile of v2, /device:TPU:9, one launch (start us, length us, event | category | flops | bytes accessed | tf_op | source)
XLA Modules:
  0.0 329.9 jit_solution(13118178586330809880)
XLA Ops:
  7.2 0.9 copy.36
  8.1 1.2 fusion.7.pin_ref
  9.5 53.7 %entry.1 = (bf16[1024,1536]{1,0:T(8,128)(2,1)S(1)}, bf16[1536,1920]{1,0:T(8,128)(2,1)S(1)}, bf16[1536,768]{1,0:T(8,128)(2,1)S(1)}) custom-call(bf16[256,1536]{1,0:T(8,128)(2,1)S(1)} %copy-done, bf16[192,1920]{1,0:T(8,128)(2,1)S(1)} %fusion.7.pin_ref, bf16[192,768]{1,0:T(8,128)(2,1)S(1)} %bitcast.34), custom_call_target="tpu_custom_call" | custom-call | bytes 91226112 | tf_op jit(solution)/shard_map/entry/pallas_call | solution.py:570
  63.1 2.6 copy-done.8
  65.7 1.6 copy-done.9
  68.1 0.7 broadcast_in_dim_reshape.3.skip_ref
  68.8 1.0 copy.37.valid_ref
  70.6 0.7 fusion.10.head_ref
  71.2 23.5 %mixer_forward.1 = (bf16[1024,1536]{1,0:T(8,128)(2,1)}, f32[1024,1920]{1,0:T(8,128)}, f32[1024,768]{1,0:T(8,128)}, f32[1024,768]{1,0:T(8,128)}, f32[1024,1]{1,0:T(8,128)}, /*index=5*/f32[4,128,768]{2,1,0:T(8,128)}) custom-call(s32[4]{0:T(128)} %open_ref.3, bf16[1024,1536]{1,0:T(8,128)(2,1)} %copy-done.9, f32[1024,1]{1,0:T(8,128)} %copy.37.valid_ref, ...), custom_call_target="tpu_custom_call" | custom-call | flops 6039797760 | bytes 23592960 | tf_op jit(solution)/shard_map/mixer_forward/pallas_call | solution.py:281
  94.7 35.3 %all-gather.2.cloned.1.call-done.cot_ref = bf16[1024,1536]{1,0:T(8,128)(2,1)} async-done(((bf16[256,1536]{1,0:T(8,128)(2,1)}), bf16[1024,1536]{1,0:T(8,128)(2,1)}) %all-gather.2.cloned.1.call-update) | async-done | bytes 3145744 | tf_op jit(solution)/shard_map/all_gather | solution.py:865
  130.0 1.9 copy-done.2
  131.9 1.9 copy-done.3
  133.8 1.0 copy-done.4
  134.8 3.6 %gate_stats.1 = (f32[1024,768]{1,0:T(8,128)S(1)}, f32[8,1024]{1,0:T(8,128)S(1)}) custom-call(bf16[1024,1536]{1,0:T(8,128)(2,1)S(1)} %copy-done.2, bf16[1536,768]{1,0:T(8,128)(2,1)S(1)} %get-tuple-element.49.wout_ref, f32[1,768]{1,0:T(1,128)S(1)} %broadcast_in_dim.34.gate_ref, f32[1024,768]{1,0:T(8,128)S(1)} %copy-done.3, f32[1024,1]{1,0:T(8,128)S(1)} %copy-done.4), custom_call_target="tpu_custom_call" | custom-call | flops 2415919104 | bytes 9437184 | tf_op jit(solution)/shard_map/gate_stats/pallas_call | solution.py:397
  138.4 1.7 copy-done.10
  140.1 6.5 %stats_exchange.1.stats_ref = f32[8,1024]{1,0:T(8,128)S(1)} custom-call(f32[8,1024]{1,0:T(8,128)S(1)} %get-tuple-element.51.part_ref), custom_call_target="tpu_custom_call" | custom-call | tf_op jit(solution)/shard_map/stats_exchange/pallas_call | solution.py:615
  146.6 4.0 %output_part.1 = (bf16[1024,768]{1,0:T(8,128)(2,1)S(1)}, bf16[1024,1536]{1,0:T(8,128)(2,1)S(1)}) custom-call(f32[1024,768]{1,0:T(8,128)S(1)} %copy-done.3, f32[8,1024]{1,0:T(8,128)S(1)} %stats_exchange.1.stats_ref, f32[1,768]{1,0:T(1,128)S(1)} %broadcast_in_dim.34.gate_ref, bf16[1536,768]{1,0:T(8,128)(2,1)S(1)} %get-tuple-element.49.wout_ref), custom_call_target="tpu_custom_call" | custom-call | flops 2415919104 | bytes 6291456 | tf_op jit(solution)/shard_map/output_part/pallas_call | solution.py:415
  150.6 1.6 copy-done.1
  152.3 1.2 copy-done.11
  153.5 40.0 %mixer_backward.1 = (bf16[1024,1920]{1,0:T(8,128)(2,1)}, bf16[1024,1536]{1,0:T(8,128)(2,1)}, f32[8,1024]{1,0:T(8,128)}, f32[1,1024]{1,0:T(1,128)}, f32[8,128]{1,...) custom-call(s32[4]{0:T(128)} %open_ref.3, bf16[1024,1536]{1,0:T(8,128)(2,1)} %copy-done.9, f32[1024,1]{1,0:T(8,128)} %copy.37.valid_ref, ...), custom_call_target="tpu_custom_call" | custom-call | flops 12079595520 | bytes 23592960 | tf_op jit(solution)/shard_map/mixer_backward/pallas_call | solution.py:325
  193.4 0.7 slice.74
  194.1 0.7 slice.69
  194.9 0.7 slice_bitcast_fusion.3
  195.6 0.7 slice.72
  196.3 0.7 reduce.1
  197.0 0.6 fusion.9.shared_ref
  197.6 0.7 slice_reduce_fusion
  198.3 0.7 slice_bitcast_fusion.5
  199.0 0.6 fusion.8.mine_ref
  199.7 6.2 %convolution_convert_fusion.1.gout_ref = bf16[1536,768]{1,0:T(8,128)(2,1)} fusion(bf16[1024,1536]{1,0:T(8,128)(2,1)} %all-gather.2.cloned.1.call-done.cot_ref, bf16[1024,768]{1,0:T(8,128)(2,1)S(1)} %copy-done.12), kind=kOutput, calls=%fused_computation.1 | convolution fusion | flops 2417098752 | bytes 7077888 | tf_op jit(solution)/shard_map/td,tc->dc/dot_general | solution.py:883
  205.8 8.5 %convolution_convert_fusion.gin_ref = bf16[1536,1920]{1,0:T(8,128)(2,1)} fusion(bf16[1024,1536]{1,0:T(8,128)(2,1)S(1)} %copy-done.32, bf16[1024,1920]{1,0:T(8,128)(2,1)S(1)} %copy-done.31), kind=kOutput, calls=%fused_computation | convolution fusion | flops 6042746880 | bytes 12976128 | tf_op jit(solution)/shard_map/td,tc->dc/dot_general | solution.py:882
  214.3 90.8 %exit.1 = (f32[256,1536]{1,0:T(8,128)}, f32[192,768]{1,0:T(8,128)}, f32[192,768]{1,0:T(8,128)}, f32[192,256]{1,0:T(8,128)}, f32[192,128]{1,0:T(8,128)}, /*index=...) custom-call(bf16[1024,1536]{1,0:T(8,128)(2,1)} %get-tuple-element.57.dn_ref, ...), custom_call_target="tpu_custom_call" | custom-call | tf_op jit(solution)/shard_map/exit/pallas_call | solution.py:823
  305.2 0.8 slice.81
  306.0 0.6 reshape.113
  306.6 0.7 slice.78
  307.3 0.6 reshape.112
  307.9 1.4 slice_bitcast_fusion.1
  309.3 0.6 reduce_sum.29
  310.0 1.6 copy.39
  311.5 1.2 slice_bitcast_fusion.4
  312.8 1.3 slice_bitcast_fusion.6
  314.1 1.8 fusion.1
  315.9 0.6 slice_bitcast_fusion
  316.5 3.0 fusion.4
  319.5 0.8 copy.46
  320.7 0.8 copy.47
  321.5 0.7 copy.48
  322.2 0.8 copy.49
  (78 shorter events, 2.2 us)
Async XLA Ops:
  7.2 2.2 copy-start
  7.2 2.2 copy-start.5
  7.2 122.8 %all-gather.2.cloned.1.call-start = ((), (), s32[]{:S(2)}) async-start(), calls=%async_computation.1 | async-start | bytes 3932160 | tf_op jit(solution)/shard_map/all_gather | solution.py:865
  9.3 58.1 %copy-start.23 = (f32[768]{0:T(1024)S(1)}, f32[768]{0:T(1024)}, u32[]{:S(2)}) copy-start(f32[768]{0:T(1024)} %param.34) | copy-start | bytes 9220
  9.3 58.1 %copy-start.24 = (s32[1024]{0:T(1024)S(1)}, s32[1024]{0:T(1024)}, u32[]{:S(2)}) copy-start(s32[1024]{0:T(1024)} %param.21) | copy-start | bytes 12292
  9.3 58.1 %copy-start.19 = (f32[1536]{0:T(1024)S(1)}, f32[1536]{0:T(1024)}, u32[]{:S(2)}) copy-start(f32[1536]{0:T(1024)} %param.22) | copy-start | bytes 18436
  9.3 58.7 %copy-start.28 = (f32[12]{0:T(128)S(1)}, f32[12]{0:T(128)}, u32[]{:S(2)}) copy-start(f32[12]{0:T(128)} %param.33) | copy-start | bytes 148
  9.4 60.5 %copy-start.25 = (f32[768]{0:T(1024)S(1)}, f32[768]{0:T(1024)}, u32[]{:S(2)}) copy-start(f32[768]{0:T(1024)} %param.28) | copy-start | bytes 9220
  9.4 60.5 %copy-start.27 = (f32[256]{0:T(256)S(1)}, f32[256]{0:T(256)}, u32[]{:S(2)}) copy-start(f32[256]{0:T(256)} %param.30) | copy-start | bytes 3076
  9.4 61.1 %copy-start.21 = (f32[4,768]{1,0:T(4,128)S(1)}, f32[4,768]{1,0:T(4,128)}, u32[]{:S(2)}) copy-start(f32[4,768]{1,0:T(4,128)} %param.27) | copy-start | bytes 36868
  9.4 61.1 %copy-start.26 = (f32[4,256]{1,0:T(4,128)S(1)}, f32[4,256]{1,0:T(4,128)}, u32[]{:S(2)}) copy-start(f32[4,256]{1,0:T(4,128)} %param.29) | copy-start | bytes 12292
  9.4 61.1 %copy-start.30 = (f32[12]{0:T(128)S(1)}, f32[12]{0:T(128)}, u32[]{:S(2)}) copy-start(f32[12]{0:T(128)} %param.31) | copy-start | bytes 148
  9.4 61.1 %copy-start.29 = (f32[12]{0:T(128)S(1)}, f32[12]{0:T(128)}, u32[]{:S(2)}) copy-start(f32[12]{0:T(128)} %param.32) | copy-start | bytes 148
  63.1 2.6 copy-start.8
  65.7 1.6 copy-start.9
  67.3 249.1 %reduce-scatter.2.cloned.1.call-start = ((), (), s32[]{:S(2)}) async-start(), calls=%async_computation.2 | async-start | bytes 3932160 | tf_op jit(solution)/shard_map/reduce_scatter | solution.py:878
  67.4 79.1 %copy-start.7 = (f32[1,768]{1,0:T(1,128)}, f32[1,768]{1,0:T(1,128)S(1)}, u32[]{:S(2)}) copy-start(f32[1,768]{1,0:T(1,128)S(1)} %broadcast_in_dim.34.gate_ref) | copy-start | bytes 9220
  70.5 0.7 copy-start.22
  130.0 1.9 copy-start.2
  131.9 1.9 copy-start.3
  133.8 1.0 copy-start.4
  138.4 1.7 copy-start.10
  146.6 4.1 %copy-start.6 = (f32[8,1024]{1,0:T(8,128)}, f32[8,1024]{1,0:T(8,128)S(1)}, u32[]{:S(2)}) copy-start(f32[8,1024]{1,0:T(8,128)S(1)} %stats_exchange.1.stats_ref) | copy-start | bytes 98308
  150.6 1.6 copy-start.1
  152.3 1.2 copy-start.11
  153.5 46.2 %copy-start.12 = (bf16[1024,768]{1,0:T(8,128)(2,1)S(1)}, bf16[1024,768]{1,0:T(8,128)(2,1)}, u32[]{:S(2)}) copy-start(bf16[1024,768]{1,0:T(8,128)(2,1)} %copy-done.11) | copy-start | bytes 4718596
  199.6 6.2 %copy-start.31 = (bf16[1024,1920]{1,0:T(8,128)(2,1)S(1)}, bf16[1024,1920]{1,0:T(8,128)(2,1)}, u32[]{:S(2)}) copy-start(bf16[1024,1920]{1,0:T(8,128)(2,1)} %get-tuple-element.59) | copy-start | bytes 11796484
  199.7 6.2 %copy-start.32 = (bf16[1024,1536]{1,0:T(8,128)(2,1)S(1)}, bf16[1024,1536]{1,0:T(8,128)(2,1)}, u32[]{:S(2)}) copy-start(bf16[1024,1536]{1,0:T(8,128)(2,1)} %get-tuple-element.58) | copy-start | bytes 9437188
  305.1 10.7 %copy-start.20 = (f32[24,128]{1,0:T(8,128)S(1)}, f32[24,128]{1,0:T(8,128)}, u32[]{:S(2)}) copy-start(f32[24,128]{1,0:T(8,128)} %get-tuple-element.67) | copy-start | bytes 36868
  305.1 11.3 %copy-start.13 = (f32[256,1536]{1,0:T(8,128)S(1)}, f32[256,1536]{1,0:T(8,128)}, u32[]{:S(2)}) copy-start(f32[256,1536]{1,0:T(8,128)} %get-tuple-element.66) | copy-start | bytes 4718596
  305.2 11.3 %copy-start.14 = (bf16[256,1536]{1,0:T(8,128)(2,1)S(1)}, bf16[256,1536]{1,0:T(8,128)(2,1)}, u32[]{:S(2)}) copy-start(bf16[256,1536]{1,0:T(8,128)(2,1)} %param.19) | copy-start | bytes 2359300
  316.5 3.0 copy-start.17
  319.5 1.3 copy-start.16
  319.5 2.1 copy-start.18
  319.5 2.8 copy-start.15
Sparse Core Ops, SparseCore 0:
  67.5 62.5 all-gather.1
  153.6 61.2 reduce-scatter.1

commit v3 on v2

--- a/solution.py
+++ b/solution.py
@@ -431,6 +431,7 @@
 
 
 MESH = pl.DeviceIdType.MESH
+CHUNKS = 4
 TAGS = {"entry": 1, "stats": 2, "exit": 3}
 
 
@@ -637,9 +638,28 @@
         target[at, :] = total.astype(target.dtype)
 
 
+def fill_rows(target, pieces):
+    places, at = [], 0
+    for source, row, start, length in pieces:
+        places.append(at)
+        for k in range(length // LANES):
+            target[at:at + 1, :] = source[row:row + 1, start + k * LANES:start + (k + 1) * LANES]
+            at += 1
+    if at < target.shape[0]:
+        target[at:, :] = jnp.zeros((target.shape[0] - at, LANES), F32)
+    return places
+
+
+def spill_row(target, row, source, at):
+    for k in range(target.shape[1] // LANES):
+        target[row:row + 1, k * LANES:(k + 1) * LANES] = source[at + k:at + k + 1, :]
+
+
 def exit_kernel(
-    dn_ref, gin_ref, gout_ref, mine_ref, shared_ref,
-    dn_out, z_out, x_out, bc_out, dt_out, out_out, mine_out, shared_out,
+    dn_ref, normed_ref, dpre_ref, cot_ref, gn_ref, dtaps_ref, dbias_ref, dhead_ref, dchan_ref, dgain_ref,
+    dn_out, z_out, x_out, bc_out, dt_out, out_out,
+    taps_out, bias_out, taps_s_out, bias_s_out, log_out, step_out, skip_out, gate_out, gain_out,
+    gin_ref, gout_ref, mine_ref, shared_ref,
     z_held, z_got, near_in, near_out, far_in, far_out, got_in, got_out, mine_got, shared_got, shared_held, shared_z,
     bc_held, bc_got,
     zs, zr, ns, nr, fs, fr, ms, mr, ss, sr, ts, tr, bs, br,
@@ -650,13 +670,25 @@
     partner = chip * 2 + 1 - core
     chan = gout_ref.shape[1]
     cols = gin_ref.shape[1]
+    width = gin_ref.shape[0]
+    mine_at = fill_rows(
+        mine_ref, [(dtaps_ref, tap, 0, chan) for tap in range(4)] + [(dbias_ref, 0, 0, chan)]
+        + [(dchan_ref, row, 0, chan) for row in range(2)] + [(dhead_ref, row, 0, LANES) for row in range(2)]
+    )
+    shared_at = fill_rows(
+        shared_ref, [(dtaps_ref, tap, chan, 2 * STATE) for tap in range(4)] + [(dbias_ref, 0, chan, 2 * STATE)]
+        + [(dgain_ref, 0, 0, width)]
+    )
     block, count = dn_out.shape[0], z_out.shape[0]
     greet("fsdp", [(me + d) % n_fs for d in range(1, n_fs)])
     greet("tp", [(tp + d) % n_tp for d in range(1, n_tp)])
     pl.semaphore_wait(pltpu.get_barrier_semaphore(), n_fs - 1 + n_tp - 1)
 
+    chunk = block // CHUNKS
+    steps = (n_tp - 1) * CHUNKS
+
     def ahead(way, step):
-        return n_tp - 1 - step if way == 0 else step
+        return n_tp - 1 - step // CHUNKS if way == 0 else step // CHUNKS
 
     def passes(way, step):
         return ahead(way, step) > tp if way == 0 else ahead(way, step) < tp
@@ -664,19 +696,33 @@
     def first(way):
         return tp == 0 if way == 0 else tp == n_tp - 1
 
-    def pass_on(way, step):
+    def local(way, step):
+        return dn_ref.at[pl.ds(pl.multiple_of(ahead(way, step) * block + step % CHUNKS * chunk, chunk), chunk)]
+
+    def pass_on(way, step, direct=False):
         towards = tp + 1 if way == 0 else tp - 1
-        return remote(z_held.at[way, step], z_got.at[way, step], zs.at[way, step], zr.at[way, step], tp=towards)
-
-    for way in range(2):
-        @pl.when(first(way))
-        def _():
-            for step in range(n_tp - 1):
-                towards = tp + 1 if way == 0 else tp - 1
-                remote(
-                    rows_at(dn_ref, ahead(way, step), block), z_got.at[way, step], zs.at[way, step], zr.at[way, step],
-                    tp=towards,
-                ).start()
+        source = local(way, step) if direct else z_held.at[way, step]
+        return remote(source, z_got.at[way, step], zs.at[way, step], zr.at[way, step], tp=towards)
+
+    def advance(turn):
+        for way in range(2):
+            lag = jnp.maximum(tp - 1 if way == 0 else n_tp - 2 - tp, 0)
+            step = turn - lag
+            live = jnp.logical_and(step >= 0, step < steps)
+
+            @pl.when(jnp.logical_and(first(way), live))
+            def _():
+                @pl.when(step >= 2)
+                def _():
+                    pass_on(way, step - 2, True).wait_send()
+
+                pass_on(way, step, True).start()
+
+            @pl.when(jnp.logical_and(jnp.logical_and(passes(way, step), live), jnp.logical_not(first(way))))
+            def _():
+                pass_on(way, step).wait_recv()
+                add_into(z_held.at[way, step], local(way, step), z_got.at[way, step])
+                pass_on(way, step).start()
 
     parts = (
         (gin_ref, slice(2 * chan, cols), near_in, far_in, got_in),
@@ -696,9 +742,6 @@
         )
 
     order = [d for d in range(1, chips)]
-    for j in range(3):
-        for d in order + [0]:
-            near(j, d).start()
 
     def small(d):
         peer = (me + d) % n_fs
@@ -713,6 +756,19 @@
     mine_got[me] = mine_ref[...]
     shared_got[me] = shared_ref[...]
 
+    advance(0)
+    tile = 256
+    pieces = width // tile
+    for piece in range(pieces):
+        rows = slice(piece * tile, (piece + 1) * tile)
+        gin_ref[rows, :] = mm(normed_ref[:, rows], dpre_ref[...], TN).astype(BF16)
+        gout_ref[rows, :] = mm(cot_ref[:, rows], gn_ref[...], TN).astype(BF16)
+        if piece % 2 == 1:
+            advance(piece // 2 + 1)
+    at = pieces // 2 + 1
+    for j in range(3):
+        for d in order + [0]:
+            near(j, d).start()
     for j in range(3):
         source, span, held, summed, _ = parts[j]
         for d in order:
@@ -721,30 +777,31 @@
             add_into(summed.at[d, :, span], rows.at[:, span], held.at[d, :, span])
             far(j, d).start()
         near(j, 0).wait_recv()
-
-    def relay(step):
-        for way in range(2):
-            @pl.when(jnp.logical_and(passes(way, step), jnp.logical_not(first(way))))
-            def _():
-                pass_on(way, step).wait_recv()
-                add_into(z_held.at[way, step], rows_at(dn_ref, ahead(way, step), block), z_got.at[way, step])
-                pass_on(way, step).start()
-
-    if n_tp > 2:
-        relay(0)
+        if j == 0:
+            advance(at)
+    turns = steps + max(n_tp - 3, 0)
     for d in range(1, n_fs):
         for copy in small(d):
             copy.wait_recv()
     total, again = mine_got[0], shared_got[0]
     for peer in range(1, n_fs):
         total, again = total + mine_got[peer], again + shared_got[peer]
-    mine_out[...] = total
+    skip_sum = gather_heads(jnp.concatenate(
+        [total[at_row:at_row + 1, :] for at_row in range(mine_at[6], mine_at[6] + chan // LANES)] , axis=1
+    ) + jnp.zeros((8, chan), F32))
+    heads_here = log_out.shape[1]
+    for tap in range(4):
+        spill_row(taps_out, tap, total, mine_at[tap])
+    spill_row(bias_out, 0, total, mine_at[4])
+    spill_row(gate_out, 0, total, mine_at[5])
+    skip_out[...] = skip_sum[0:1, :heads_here]
+    log_out[...] = total[mine_at[7]:mine_at[7] + 1, :heads_here]
+    step_out[...] = total[mine_at[8]:mine_at[8] + 1, :heads_here]
     shared_held[...] = again
     shared_z[tp] = again
     for d in range(1, n_tp):
         remote(shared_held, shared_z.at[tp], ts.at[d], tr.at[d], tp=(tp + d) % n_tp).start()
-    for step in range(1, n_tp - 2):
-        relay(step)
+    pl.loop(at + 1, at + 5)(advance)
 
     def settle(j, target, span):
         source, _, held, _, got = parts[j]
@@ -760,6 +817,7 @@
     bc_got[tp] = bc_held[...]
     for d in range(1, n_tp):
         remote(bc_held, bc_got.at[tp], bs.at[d], br.at[d], tp=(tp + d) % n_tp).start()
+    pl.loop(at + 5, turns)(advance)
     for j in (1, 2):
         for d in order:
             far(j, d).wait_recv()
@@ -773,12 +831,15 @@
     total = shared_z[0]
     for peer in range(1, n_tp):
         total = total + shared_z[peer]
-    shared_out[...] = total
+    for tap in range(4):
+        spill_row(taps_s_out, tap, total, shared_at[tap])
+    spill_row(bias_s_out, 0, total, shared_at[4])
+    spill_row(gain_out, 0, total, shared_at[5])
     add_into(bc_out, *[bc_got.at[peer] for peer in range(n_tp)])
 
     own = rows_at(dn_ref, tp, block)
     for way in range(2):
-        for step in range(n_tp - 1):
+        for step in range(steps):
             @pl.when(jnp.logical_and(ahead(way, step) == tp, jnp.logical_not(first(way))))
             def _():
                 pass_on(way, step).wait_recv()
@@ -786,16 +847,23 @@
     for value in range(n_tp):
         @pl.when(tp == value)
         def _():
-            incoming = []
-            if value > 0:
-                incoming.append(z_got.at[0, n_tp - 1 - value])
-            if value < n_tp - 1:
-                incoming.append(z_got.at[1, value])
-            add_into(dn_out, own, *incoming)
+            for part in range(CHUNKS):
+                span = pl.ds(part * chunk, chunk)
+                incoming = []
+                if value > 0:
+                    incoming.append(z_got.at[0, (n_tp - 1 - value) * CHUNKS + part])
+                if value < n_tp - 1:
+                    incoming.append(z_got.at[1, value * CHUNKS + part])
+                add_into(dn_out.at[span], own.at[span], *incoming)
 
     for way in range(2):
-        for step in range(n_tp - 1):
-            @pl.when(passes(way, step))
+        @pl.when(first(way))
+        def _():
+            for step in range(steps - 2, steps):
+                pass_on(way, step, True).wait_send()
+
+        for step in range(steps):
+            @pl.when(jnp.logical_and(passes(way, step), jnp.logical_not(first(way))))
             def _():
                 pass_on(way, step).wait_send()
     for j in range(3):
@@ -811,39 +879,45 @@
         remote(bc_held, bc_got.at[tp], bs.at[d], br.at[d], tp=(tp + d) % n_tp).wait_send()
 
 
-def leave(dn, grad_in, grad_out, mine, shared, n_tp, n_fs):
+def leave(dn, normed, dpre, cot, gnormed, small, heads_here, n_tp, n_fs):
     block, width = dn.shape[0] // n_tp, dn.shape[1]
-    count, cols = grad_in.shape[0] // n_fs, grad_in.shape[1]
-    chan = grad_out.shape[1]
-    chips = n_fs // 2
+    count, cols = width // n_fs, dpre.shape[1]
+    chan = gnormed.shape[1]
+    chips, steps = n_fs // 2, (n_tp - 1) * CHUNKS
     dma = pltpu.SemaphoreType.DMA
     vmem = pl.BlockSpec(memory_space=pltpu.VMEM)
     room = lambda *shape: pltpu.VMEM(shape, BF16)
     shape = lambda *extents: jax.ShapeDtypeStruct(extents, F32)
+    up = lambda n: -(-n // 8) * 8
+    mine = (up(7 * chan // LANES + 2), LANES)
+    shared = (up((10 * STATE + width) // LANES), LANES)
+    outs = [
+        shape(block, width), shape(count, chan), shape(count, chan), shape(count, 2 * STATE), shape(count, LANES),
+        shape(count, chan), shape(4, chan), shape(1, chan), shape(4, 2 * STATE), shape(1, 2 * STATE),
+        shape(1, heads_here), shape(1, heads_here), shape(1, heads_here), shape(1, chan), shape(1, width),
+    ]
     return pl.pallas_call(
         functools.partial(exit_kernel, n_tp=n_tp, n_fs=n_fs),
         name="exit",
-        in_specs=[vmem] * 5,
-        out_specs=[vmem] * 8,
-        out_shape=[
-            shape(block, width), shape(count, chan), shape(count, chan), shape(count, 2 * STATE), shape(count, LANES),
-            shape(count, chan), shape(*mine.shape), shape(*shared.shape),
-        ],
+        in_specs=[vmem] * 10,
+        out_specs=[vmem] * len(outs),
+        out_shape=outs,
         scratch_shapes=[
-            room(2, n_tp - 1, block, width), room(2, n_tp - 1, block, width),
+            room(width, cols), room(width, chan), pltpu.VMEM(mine, F32), pltpu.VMEM(shared, F32),
+            room(2, steps, block // CHUNKS, width), room(2, steps, block // CHUNKS, width),
             room(chips, count, cols), room(chips, count, chan), room(chips, count, cols), room(chips, count, chan),
             room(chips, count, cols), room(chips, count, chan),
-            pltpu.VMEM((n_fs,) + mine.shape, F32), pltpu.VMEM((n_fs,) + shared.shape, F32),
-            pltpu.VMEM(shared.shape, F32), pltpu.VMEM((n_tp,) + shared.shape, F32),
+            pltpu.VMEM((n_fs,) + mine, F32), pltpu.VMEM((n_fs,) + shared, F32),
+            pltpu.VMEM(shared, F32), pltpu.VMEM((n_tp,) + shared, F32),
             room(count, 2 * STATE), room(n_tp, count, 2 * STATE),
-            dma((2, n_tp - 1)), dma((2, n_tp - 1)), dma((3, chips)), dma((3, chips)), dma((3, chips)), dma((3, chips)),
+            dma((2, steps)), dma((2, steps)), dma((3, chips)), dma((3, chips)), dma((3, chips)), dma((3, chips)),
             dma((n_fs,)), dma((n_fs,)), dma((n_fs,)), dma((n_fs,)), dma((n_tp,)), dma((n_tp,)), dma((n_tp,)),
             dma((n_tp,)),
         ],
         compiler_params=pltpu.CompilerParams(
             collective_id=TAGS["exit"], has_side_effects=True, vmem_limit_bytes=62 << 20
         ),
-    )(dn, grad_in, grad_out, mine, shared)
+    )(dn, normed, dpre, cot, gnormed, *small)
 
 
 def shards(
@@ -854,7 +928,6 @@
     width = tokens.shape[1]
     heads_here = proj_dt.shape[1]
     inner = chan * lax.axis_size("tp")
-    wide = chan + 2 * STATE
     valid = token_valid.astype(F32)[:, None]
     pack_in = jnp.concatenate(
         [proj_z, proj_x, proj_bc, jnp.pad(proj_dt, ((0, 0), (0, LANES - heads_here)))], axis=1
@@ -879,32 +952,12 @@
     dpre, dn_rows, dtaps, dbias, dhead, dchan, dgain = mixer_backward(
         seq_start, tok_all, valid, w_in, taps, bias, heads, skip, gate, pre, y, enter, dgn, stats, inner
     )
-    grad_in = jnp.einsum("td,tc->dc", normed, dpre, preferred_element_type=F32).astype(BF16)
-    grad_out = jnp.einsum("td,tc->dc", cot_all, gnormed, preferred_element_type=F32).astype(BF16)
-    pack = lambda *vs: jnp.concatenate([v.reshape(-1) for v in vs])
-    mine = pack(dtaps[0:4, :chan], dbias[:, :chan], dhead[0:2], dchan[0:2])
-    shared = pack(dtaps[0:4, chan:], dbias[:, chan:], dgain)
-    tiles = lambda v: jnp.pad(v, (0, -v.shape[0] % (8 * LANES))).reshape(-1, LANES)
-    d_normed, own_z, own_x, own_bc, own_dt, own_out, mine, shared = leave(
-        dn_rows, grad_in, grad_out, tiles(mine), tiles(shared), n_tp, n_fs
-    )
-    mine, shared = mine.reshape(-1), shared.reshape(-1)
-    at = 0
-
-    def take(source, *shape):
-        nonlocal at
-        size = 1
-        for extent in shape:
-            size *= extent
-        part = source[at:at + size].reshape(shape)
-        at += size
-        return part
-
-    g_taps, g_bias, g_heads, g_chan = (
-        take(mine, 4, chan), take(mine, chan), take(mine, 2, LANES), take(mine, 2, chan),
-    )
-    at = 0
-    g_taps_s, g_bias_s, g_gain = take(shared, 4, 2 * STATE), take(shared, 2 * STATE), take(shared, width)
+    (
+        d_normed, own_z, own_x, own_bc, own_dt, own_out, g_taps, g_bias, g_taps_s, g_bias_s, g_log, g_step, g_skip,
+        g_gate, g_gain,
+    ) = leave(
+        dn_rows, normed, dpre, cot_all, gnormed, (dtaps, dbias, dhead, dchan, dgain), heads_here, n_tp, n_fs
+    )
     resid = tokens.astype(F32)
     rstd = lax.rsqrt(jnp.mean(resid * resid, axis=1, keepdims=True) + EPSILON)
     output = (resid + mixed.astype(F32)).astype(BF16)
@@ -914,9 +967,8 @@
         - resid * (rstd * rstd * rstd) * jnp.mean(scaled_in * resid, axis=1, keepdims=True)
     ).astype(BF16)
     return (
-        output, grad_tokens, g_gain, own_z, own_x, own_bc, own_dt[:, :heads_here], g_taps, g_bias, g_taps_s, g_bias_s,
-        g_heads[0, :heads_here], g_heads[1, :heads_here], g_chan[1].reshape(heads_here, HEAD).sum(axis=1),
-        g_chan[0], own_out.T,
+        output, grad_tokens, g_gain[0], own_z, own_x, own_bc, own_dt[:, :heads_here], g_taps, g_bias[0], g_taps_s,
+        g_bias_s[0], g_log[0], g_step[0], g_skip[0], g_gate[0], own_out.T,
     )
 
 

time: 334 us -> 310 us (0.928); the launches traced: 330 us -> 309 us
  matrix products: 14.7 us -> 0 us
  local copies, waits for them, and re-layouts: 33.6 us -> 25.3 us
    dot_general x2 -> x0, matrix products: 14.7 us -> none  [the longest x1 8.52 us: shards(): jnp.einsum('td,tc->dc', normed, dpre, preferred_element_type=F32)]
    slice x8 -> x0, local copies, waits for them, and re-layouts: 6.23 us -> none  [the longest x4 3.37 us: take(): part = source[at:at + size].reshape(shape)]
    unnamed x75 -> x83, local copies, waits for them, and re-layouts: 20.4 us -> 22.8 us
  transfers between devices with their start and end apart: 2 -> 2, of which waited for: 1 -> 1; matrix products, arithmetic and copies ran while one was open for 11% -> 4% of each run, Pallas kernels for 47% -> 50%
where the time goes in v3:
time: 310 us; the launch traced here: 309 us
  Pallas kernels  223 us (72%)
  waiting for transfers between devices  35.4 us (11%)
  local copies, waits for them, and re-layouts  25.3 us (8%)
  between operations  14.5 us (5%)
  other arithmetic  11.2 us (4%)
    pallas_call x1, Pallas kernels, leave(): pl.pallas_call(functools.partial(exit_kernel, n_tp=n_tp, n_fs=n_fs), name...  91.8 us
    pallas_call x1, Pallas kernels, entry(): pl.pallas_call(functools.partial(entry_kernel, n_tp=n_tp, n_fs=n_fs), nam...  53.7 us
    pallas_call x1, Pallas kernels, mixer_backward(): pl.pallas_call(functools.partial(backward_kernel, inner=inner), name='mix...  39.8 us
    all_gather x1, waiting for transfers between devices, shards(): cot_all = lax.all_gather(late_cot, 'tp', axis=0, tiled=True)  35.3 us
    pallas_call x1, Pallas kernels, mixer_forward(): pl.pallas_call(forward_kernel, name='mixer_forward', grid_spec=pltpu.Pref...  23.5 us
    unnamed x83, local copies, waits for them, and re-layouts  22.8 us
    pallas_call x1, Pallas kernels, exchange(): pl.pallas_call(functools.partial(exchange_kernel, n_tp=n_tp), name='stats...  6.45 us
  transfers between devices with their start and end apart: 2, of which 1 were waited for; matrix products, arithmetic and copies ran while one was open for 4% of the time, Pallas kernels for 50%

profile of v3, /device:TPU:9, one launch (start us, length us, event | category | flops | bytes accessed | tf_op | source)
XLA Modules:
  0.0 309.3 jit_solution(1783784571239604541)
XLA Ops:
  7.2 0.0 all-gather.2.cloned.1.call-start
  7.2 0.9 copy.36
  8.1 1.2 fusion.7.pin_ref
  9.3 0.0 copy-start.22
  9.5 53.7 %entry.1 = (bf16[1024,1536]{1,0:T(8,128)(2,1)S(1)}, bf16[1536,1920]{1,0:T(8,128)(2,1)S(1)}, bf16[1536,768]{1,0:T(8,128)(2,1)S(1)}) custom-call(bf16[256,1536]{1,0:T(8,128)(2,1)S(1)} %copy-done.1, bf16[192,1920]{1,0:T(8,128)(2,1)S(1)} %fusion.7.pin_ref, bf16[192,768]{1,0:T(8,128)(2,1)S(1)} %bitcast.12), custom_call_target="tpu_custom_call" | custom-call | bytes 91226112 | tf_op jit(solution)/shard_map/entry/pallas_call | solution.py:571
  63.1 2.6 copy-done.9
  65.7 1.6 copy-done.10
  67.3 0.0 all-gather.2.cloned.1.call-update
  67.3 0.0 reduce-scatter.2.cloned.1.call-start
  67.5 0.6 broadcast_in_dim.28.gain_ref
  68.1 0.1 broadcast_in_dim.33
  68.1 0.7 broadcast_in_dim_reshape.3.skip_ref
  68.8 1.0 copy.37.valid_ref
  69.8 0.1 pad.16.clone
  69.9 0.6 pad_maximum_fusion
  70.6 0.7 fusion.8.head_ref
  71.2 23.5 %mixer_forward.1 = (bf16[1024,1536]{1,0:T(8,128)(2,1)}, f32[1024,1920]{1,0:T(8,128)}, f32[1024,768]{1,0:T(8,128)}, f32[1024,768]{1,0:T(8,128)}, f32[1024,1]{1,0:T(8,128)}, /*index=5*/f32[4,128,768]{2,1,0:T(8,128)}) custom-call(s32[4]{0:T(128)} %open_ref.3, bf16[1024,1536]{1,0:T(8,128)(2,1)} %copy-done.10, f32[1024,1]{1,0:T(8,128)} %copy.37.valid_ref, ...), custom_call_target="tpu_custom_call" | custom-call | flops 6039797760 | bytes 23592960 | tf_op jit(solution)/shard_map/mixer_forward/pallas_call | solution.py:281
  94.7 35.3 %all-gather.2.cloned.1.call-done.cot_ref = bf16[1024,1536]{1,0:T(8,128)(2,1)} async-done(((bf16[256,1536]{1,0:T(8,128)(2,1)}), bf16[1024,1536]{1,0:T(8,128)(2,1)}) %all-gather.2.cloned.1.call-update) | async-done | bytes 3145744 | tf_op jit(solution)/shard_map/all_gather | solution.py:938
  130.0 1.9 copy-done
  131.9 1.9 copy-done.3
  133.8 1.0 copy-done.5
  134.8 3.6 %gate_stats.1 = (f32[1024,768]{1,0:T(8,128)S(1)}, f32[8,1024]{1,0:T(8,128)S(1)}) custom-call(bf16[1024,1536]{1,0:T(8,128)(2,1)S(1)} %copy-done, bf16[1536,768]{1,0:T(8,128)(2,1)S(1)} %get-tuple-element.56.wout_ref, f32[1,768]{1,0:T(1,128)S(1)} %broadcast_in_dim.34.gate_ref, f32[1024,768]{1,0:T(8,128)S(1)} %copy-done.3, f32[1024,1]{1,0:T(8,128)S(1)} %copy-done.5), custom_call_target="tpu_custom_call" | custom-call | flops 2415919104 | bytes 9437184 | tf_op jit(solution)/shard_map/gate_stats/pallas_call | solution.py:397
  138.4 1.7 copy-done.11
  140.1 6.5 %stats_exchange.1.stats_ref = f32[8,1024]{1,0:T(8,128)S(1)} custom-call(f32[8,1024]{1,0:T(8,128)S(1)} %get-tuple-element.58.part_ref), custom_call_target="tpu_custom_call" | custom-call | tf_op jit(solution)/shard_map/stats_exchange/pallas_call | solution.py:616
  146.6 4.0 %output_part.1 = (bf16[1024,768]{1,0:T(8,128)(2,1)S(1)}, bf16[1024,1536]{1,0:T(8,128)(2,1)S(1)}) custom-call(f32[1024,768]{1,0:T(8,128)S(1)} %copy-done.3, f32[8,1024]{1,0:T(8,128)S(1)} %stats_exchange.1.stats_ref, f32[1,768]{1,0:T(1,128)S(1)} %broadcast_in_dim.34.gate_ref, bf16[1536,768]{1,0:T(8,128)(2,1)S(1)} %get-tuple-element.56.wout_ref), custom_call_target="tpu_custom_call" | custom-call | flops 2415919104 | bytes 6291456 | tf_op jit(solution)/shard_map/output_part/pallas_call | solution.py:415
  150.6 1.6 copy-done.2
  152.3 1.1 copy-done.4
  153.4 0.0 reduce-scatter.2.cloned.1.call-update
  153.4 39.8 %mixer_backward.1 = (bf16[1024,1920]{1,0:T(8,128)(2,1)}, bf16[1024,1536]{1,0:T(8,128)(2,1)}, f32[8,1024]{1,0:T(8,128)}, f32[1,1024]{1,0:T(1,128)}, f32[8,128]{1,...) custom-call(s32[4]{0:T(128)} %open_ref.3, bf16[1024,1536]{1,0:T(8,128)(2,1)} %copy-done.10, f32[1024,1]{1,0:T(8,128)} %copy.37.valid_ref, ...), custom_call_target="tpu_custom_call" | custom-call | flops 12079595520 | bytes 23592960 | tf_op jit(solution)/shard_map/mixer_backward/pallas_call | solution.py:325
  193.2 91.8 %exit.1 = (f32[256,1536]{1,0:T(8,128)}, f32[192,768]{1,0:T(8,128)}, f32[192,768]{1,0:T(8,128)}, f32[192,256]{1,0:T(8,128)}, f32[192,128]{1,0:T(8,128)}, /*index=...) custom-call(bf16[1024,1536]{1,0:T(8,128)(2,1)} %get-tuple-element.64, ...), custom_call_target="tpu_custom_call" | custom-call | tf_op jit(solution)/shard_map/exit/pallas_call | solution.py:899
  285.1 1.5 reduce
  286.6 1.3 reduce.1
  287.9 1.3 reduce.2
  289.1 1.6 copy.39
  290.7 1.8 fusion.1
  292.5 0.0 reduce-scatter.2.cloned.1.call-done
  292.6 3.0 fusion.4
  295.6 0.8 copy.51
  296.4 0.4 copy-done.15
  296.8 0.8 copy.52
  297.6 0.7 copy.53
  298.3 0.6 copy.54
  298.9 0.6 copy.55
  299.5 0.6 copy.56
  300.1 0.5 copy.57
  300.6 0.5 copy.58
  301.1 0.5 copy.59
  301.6 0.8 copy.60
  (67 shorter events, 0.2 us)
Async XLA Ops:
  7.2 2.2 copy-start.1
  7.2 2.2 copy-start.6
  7.2 122.8 %all-gather.2.cloned.1.call-start = ((), (), s32[]{:S(2)}) async-start(), calls=%async_computation.1 | async-start | bytes 3932160 | tf_op jit(solution)/shard_map/all_gather | solution.py:938
  9.3 58.1 %copy-start.22 = (f32[768]{0:T(1024)S(1)}, f32[768]{0:T(1024)}, u32[]{:S(2)}) copy-start(f32[768]{0:T(1024)} %param.34) | copy-start | bytes 9220
  9.3 58.1 %copy-start.23 = (s32[1024]{0:T(1024)S(1)}, s32[1024]{0:T(1024)}, u32[]{:S(2)}) copy-start(s32[1024]{0:T(1024)} %param.21) | copy-start | bytes 12292
  9.3 58.1 %copy-start.18 = (f32[1536]{0:T(1024)S(1)}, f32[1536]{0:T(1024)}, u32[]{:S(2)}) copy-start(f32[1536]{0:T(1024)} %param.22) | copy-start | bytes 18436
  9.3 58.7 %copy-start.29 = (f32[12]{0:T(128)S(1)}, f32[12]{0:T(128)}, u32[]{:S(2)}) copy-start(f32[12]{0:T(128)} %param.33) | copy-start | bytes 148
  9.4 60.5 %copy-start.24 = (f32[768]{0:T(1024)S(1)}, f32[768]{0:T(1024)}, u32[]{:S(2)}) copy-start(f32[768]{0:T(1024)} %param.28) | copy-start | bytes 9220
  9.4 60.5 %copy-start.27 = (f32[256]{0:T(256)S(1)}, f32[256]{0:T(256)}, u32[]{:S(2)}) copy-start(f32[256]{0:T(256)} %param.30) | copy-start | bytes 3076
  9.4 61.1 %copy-start.19 = (f32[4,768]{1,0:T(4,128)S(1)}, f32[4,768]{1,0:T(4,128)}, u32[]{:S(2)}) copy-start(f32[4,768]{1,0:T(4,128)} %param.27) | copy-start | bytes 36868
  9.4 61.1 %copy-start.25 = (f32[4,256]{1,0:T(4,128)S(1)}, f32[4,256]{1,0:T(4,128)}, u32[]{:S(2)}) copy-start(f32[4,256]{1,0:T(4,128)} %param.29) | copy-start | bytes 12292
  9.4 61.1 %copy-start.31 = (f32[12]{0:T(128)S(1)}, f32[12]{0:T(128)}, u32[]{:S(2)}) copy-start(f32[12]{0:T(128)} %param.31) | copy-start | bytes 148
  9.4 61.1 %copy-start.30 = (f32[12]{0:T(128)S(1)}, f32[12]{0:T(128)}, u32[]{:S(2)}) copy-start(f32[12]{0:T(128)} %param.32) | copy-start | bytes 148
  63.1 2.6 copy-start.9
  65.7 1.6 copy-start.10
  67.3 225.2 %reduce-scatter.2.cloned.1.call-start = ((), (), s32[]{:S(2)}) async-start(), calls=%async_computation.2 | async-start | bytes 3932160 | tf_op jit(solution)/shard_map/reduce_scatter | solution.py:951
  67.4 79.1 %copy-start.8 = (f32[1,768]{1,0:T(1,128)}, f32[1,768]{1,0:T(1,128)S(1)}, u32[]{:S(2)}) copy-start(f32[1,768]{1,0:T(1,128)S(1)} %broadcast_in_dim.34.gate_ref) | copy-start | bytes 9220
  70.5 0.7 copy-start.21
  130.0 1.9 copy-start
  131.9 1.9 copy-start.3
  133.8 1.0 copy-start.5
  138.4 1.7 copy-start.11
  146.6 4.1 %copy-start.7 = (f32[8,1024]{1,0:T(8,128)}, f32[8,1024]{1,0:T(8,128)S(1)}, u32[]{:S(2)}) copy-start(f32[8,1024]{1,0:T(8,128)S(1)} %stats_exchange.1.stats_ref) | copy-start | bytes 98308
  150.6 1.6 copy-start.2
  152.3 1.1 copy-start.4
  285.1 7.5 %copy-start.12 = (f32[256,1536]{1,0:T(8,128)S(1)}, f32[256,1536]{1,0:T(8,128)}, u32[]{:S(2)}) copy-start(f32[256,1536]{1,0:T(8,128)} %get-tuple-element.73) | copy-start | bytes 4718596
  285.1 7.5 %copy-start.13 = (bf16[256,1536]{1,0:T(8,128)(2,1)S(1)}, bf16[256,1536]{1,0:T(8,128)(2,1)}, u32[]{:S(2)}) copy-start(bf16[256,1536]{1,0:T(8,128)(2,1)} %param.19) | copy-start | bytes 2359300
  292.6 3.0 copy-start.16
  295.5 1.3 copy-start.15
  295.5 2.1 copy-start.17
  295.5 2.7 copy-start.20
  295.5 3.3 %copy-start.26 = (f32[4,256]{1,0:T(4,128)S(1)}, f32[4,256]{1,0:T(4,128)}, u32[]{:S(2)}) copy-start(f32[4,256]{1,0:T(4,128)} %get-tuple-element.152) | copy-start | bytes 12292
  295.6 3.9 %copy-start.28 = (f32[1,256]{1,0:T(1,128)S(1)}, f32[1,256]{1,0:T(1,128)}, u32[]{:S(2)}) copy-start(f32[1,256]{1,0:T(1,128)} %get-tuple-element.82) | copy-start | bytes 3076
  295.6 4.5 %copy-start.34 = (f32[1,12]{1,0:T(1,128)S(1)}, f32[1,12]{1,0:T(1,128)}, u32[]{:S(2)}) copy-start(f32[1,12]{1,0:T(1,128)} %get-tuple-element.83) | copy-start | bytes 148
  295.6 5.0 %copy-start.33 = (f32[1,12]{1,0:T(1,128)S(1)}, f32[1,12]{1,0:T(1,128)}, u32[]{:S(2)}) copy-start(f32[1,12]{1,0:T(1,128)} %get-tuple-element.84) | copy-start | bytes 148
  295.6 5.5 %copy-start.32 = (f32[1,12]{1,0:T(1,128)S(1)}, f32[1,12]{1,0:T(1,128)}, u32[]{:S(2)}) copy-start(f32[1,12]{1,0:T(1,128)} %get-tuple-element.85) | copy-start | bytes 148
  295.6 6.0 %copy-start.14 = (f32[192,768]{1,0:T(8,128)S(1)}, f32[192,768]{1,0:T(8,128)}, u32[]{:S(2)}) copy-start(f32[192,768]{1,0:T(8,128)} %get-tuple-element.87) | copy-start | bytes 1769476
Sparse Core Ops, SparseCore 0:
  67.5 62.5 all-gather.1
  153.5 64.4 reduce-scatter.1

commit v4 on v3

v4 whole, which is shorter than its diff:
```python
import functools
import jax
import jax.numpy as jnp
from jax import lax
from jax.experimental import pallas as pl
from jax.experimental.pallas import tpu as pltpu
from jax.sharding import PartitionSpec as P

HEAD = 64
STATE = 128
STRETCH = 256
LANES = 128
EPSILON = 1e-05
F32 = jnp.float32
BF16 = jnp.bfloat16
NN = (((1,), (0,)), ((), ()))
NT = (((1,), (1,)), ((), ()))
TN = (((0,), (0,)), ((), ()))


def mm(a, b, dims=NN):
    return lax.dot_general(a, b, dims, preferred_element_type=F32)


def exact(a, b):
    return lax.dot_general(a, b, NN, precision=lax.Precision.HIGHEST, preferred_element_type=F32)


def halves(v):
    high = v.astype(BF16)
    return high, (v - high.astype(F32)).astype(BF16)


def iota(shape, dim):
    return lax.broadcasted_iota(jnp.int32, shape, dim)


def spread_heads(v, chan):
    high, rest = halves(v)
    rows = iota((2 * LANES, chan), 0) & (LANES - 1)
    pick = jnp.where(rows == (iota((2 * LANES, chan), 1) >> 6), 1.0, 0.0).astype(BF16)
    return mm(jnp.concatenate([high, rest], axis=1), pick)


def gather_heads(v):
    chan = v.shape[1]
    high, rest = halves(v)
    pick = jnp.where((iota((chan, LANES), 0) >> 6) == iota((chan, LANES), 1), 1.0, 0.0).astype(BF16)
    return mm(high, pick) + mm(rest, pick)


def softplus(v):
    return jnp.maximum(v, 0.0) + jnp.log1p(jnp.exp(-jnp.abs(v)))


def sigmoid(v):
    return 1.0 / (1.0 + jnp.exp(-v))


def lower_mask():
    return iota((STRETCH, STRETCH), 0) >= iota((STRETCH, STRETCH), 1)


def convolve(xs_ref, taps_ref, bias_ref):
    total = bias_ref[...] + taps_ref[0:1, :] * xs_ref[5:5 + STRETCH, :]
    for tap in range(1, 4):
        total = total + taps_ref[tap:tap + 1, :] * xs_ref[5 + tap:5 + tap + STRETCH, :]
    return total


def decays(pre_dt, head_ref, valid):
    rates = softplus(pre_dt + head_ref[0:1, :]) * valid
    log_decay = rates * head_ref[1:2, :]
    lower = lower_mask().astype(F32)
    cumulative = exact(lower, log_decay)
    last = cumulative[STRETCH - 1:STRETCH, :]
    return rates, cumulative, jnp.exp(cumulative), jnp.exp(last - cumulative)


def weights_of(cumulative, across, head):
    return jnp.exp(jnp.minimum(cumulative[:, head:head + 1] - across[head:head + 1, :], 0.0))


def backward_kernel(
    open_ref, tok_ref, w_ref, taps_ref, bias_ref, head_ref, skip_ref, gate_ref,
    pre_ref, halo_ref, y_ref, enter_ref, dgn_ref, stats_ref,
    dpre_ref, dnormed_ref, dtaps_ref, dbias_ref, dhead_ref, dchan_ref, dgain_ref,
    dstate, xs, dus,
    *, inner,
):
    chan = y_ref.shape[1]
    wide = chan + 2 * STATE
    step = pl.program_id(0)
    block = pl.num_programs(0) - 1 - step
    opening = open_ref[block] == 1
    keep = jnp.where(opening, 0.0, 1.0).astype(F32)

    @pl.when(step == 0)
    def _():
        dstate[...] = jnp.zeros_like(dstate)
        dus[...] = jnp.zeros_like(dus)
        dtaps_ref[...] = jnp.zeros_like(dtaps_ref)
        dbias_ref[...] = jnp.zeros_like(dbias_ref)
        dhead_ref[...] = jnp.zeros_like(dhead_ref)
        dchan_ref[...] = jnp.zeros_like(dchan_ref)
        dgain_ref[...] = jnp.zeros_like(dgain_ref)

    grstd, cross, valid = row_stats(stats_ref, inner)
    xs[0:8, :] = halo_ref[:, chan:2 * chan + 2 * STATE] * keep
    xs[8:8 + STRETCH, :] = pre_ref[:, chan:2 * chan + 2 * STATE]
    conv = convolve(xs, taps_ref, bias_ref)
    gate_u = sigmoid(conv)
    feats = conv * gate_u
    slope = gate_u * (1.0 + conv * (1.0 - gate_u))
    x = feats[:, :chan]
    bs = feats[:, chan:chan + STATE].astype(BF16)
    cs = feats[:, chan + STATE:].astype(BF16)
    pre_dt = pre_ref[:, 2 * chan + 2 * STATE:]
    rates, cumulative, grown, to_end = decays(pre_dt, head_ref, valid)
    across = cumulative.T
    grown_e = spread_heads(grown, chan)
    rates_e = spread_heads(rates, chan)
    to_end_e = spread_heads(to_end, chan)
    leave_e = grown_e[STRETCH - 1:STRETCH, :]

    pre_z = pre_ref[:, :chan]
    gate_z = sigmoid(pre_z)
    silu_z = pre_z * gate_z * valid
    y = y_ref[...]
    mixed = y + skip_ref[...] * x
    gated = mixed * silu_z
    dgn = dgn_ref[...]
    d_gated = grstd * (gate_ref[...] * dgn) - gated * (grstd * grstd * grstd * cross * (1.0 / inner))
    d_mixed = d_gated * silu_z
    dpre_ref[:, :chan] = (
        d_gated * mixed * (valid * (gate_z * (1.0 + pre_z * (1.0 - gate_z))))
    ).astype(BF16)
    dchan_ref[0:1, :] += jnp.sum(dgn * gated * grstd, axis=0, keepdims=True)
    dchan_ref[1:2, :] += jnp.sum(d_mixed * x, axis=0, keepdims=True)

    dy_b = d_mixed.astype(BF16)
    dy = dy_b.astype(F32)
    scaled = x * rates_e
    scaled_b = scaled.astype(BF16)
    entering = enter_ref[0]
    d_leaving = dstate[...]
    d_leaving_b = d_leaving.astype(BF16)
    tail = mm(bs, d_leaving_b) * to_end_e
    overlap = jnp.where(lower_mask(), mm(cs, bs, NT), 0.0)
    first = iota((STRETCH, LANES), 1) < HEAD
    d_overlap = jnp.zeros((STRETCH, STRETCH), F32)
    parts = []
    for pair in range(chan // LANES):
        cols = slice(pair * LANES, (pair + 1) * LANES)
        dy_pair = dy_b[:, cols]
        x_pair = scaled_b[:, cols]
        zero = jnp.zeros_like(dy_pair)
        sides = [jnp.where(first, dy_pair, zero), jnp.where(first, zero, dy_pair)]
        mats = []
        for side in range(2):
            weight = weights_of(cumulative, across, 2 * pair + side)
            mats.append((weight * overlap).astype(BF16))
            d_overlap = d_overlap + mm(sides[side], x_pair, NT) * weight
        parts.append(mm(jnp.concatenate(mats, axis=0), jnp.concatenate(sides, axis=0), TN))
    d_scaled = jnp.concatenate(parts, axis=1) + tail
    scaled_r = scaled_b.astype(F32)
    d_cum = gather_heads(dy * y - scaled_r * d_scaled)
    d_last = jnp.sum(scaled_r * tail, axis=0, keepdims=True) + leave_e * jnp.sum(
        d_leaving * entering, axis=0, keepdims=True
    )
    d_last = gather_heads(jnp.broadcast_to(d_last, (8, chan)))[0:1, :]
    upper = (iota((STRETCH, STRETCH), 0) <= iota((STRETCH, STRETCH), 1)).astype(F32)
    d_log = exact(upper, d_cum) + d_last
    decay = head_ref[1:2, :]
    d_rates = d_log * decay + gather_heads(x * d_scaled)
    d_dt = d_rates * valid * sigmoid(pre_dt + head_ref[0:1, :])
    dhead_ref[0:1, :] += jnp.sum(d_log * rates, axis=0, keepdims=True) * decay
    dhead_ref[1:2, :] += jnp.sum(d_dt, axis=0, keepdims=True)
    dpre_ref[:, 2 * chan + 2 * STATE:] = d_dt.astype(BF16)

    d_x = d_scaled * rates_e + skip_ref[...] * d_mixed
    d_overlap_b = jnp.where(lower_mask(), d_overlap, 0.0).astype(BF16)
    dy_grown = (dy * grown_e).astype(BF16)
    x_end = (scaled * to_end_e).astype(BF16)
    d_b = mm(d_overlap_b, cs, TN) + mm(x_end, d_leaving_b, NT)
    d_c = mm(d_overlap_b, bs) + mm(dy_grown, entering.astype(BF16), NT)
    dstate[...] = (d_leaving * leave_e + mm(cs, dy_grown, TN)) * keep

    dus[0:STRETCH, :chan] = d_x * slope[:, :chan]
    dus[0:STRETCH, chan:chan + STATE] = d_b * slope[:, chan:chan + STATE]
    dus[0:STRETCH, chan + STATE:] = d_c * slope[:, chan + STATE:]
    d_conv = dus[0:STRETCH, :]
    dbias_ref[...] += jnp.sum(d_conv, axis=0, keepdims=True)
    d_pre = jnp.zeros((STRETCH, wide), F32)
    for tap in range(4):
        dtaps_ref[tap:tap + 1, :] += jnp.sum(d_conv * xs[5 + tap:5 + tap + STRETCH, :], axis=0, keepdims=True)
        d_pre = d_pre + taps_ref[tap:tap + 1, :] * dus[3 - tap:3 - tap + STRETCH, :]
    dpre_ref[:, chan:2 * chan + 2 * STATE] = d_pre.astype(BF16)
    dus[STRETCH:STRETCH + 8, :] = d_conv[0:8, :] * keep

    d_normed = mm(dpre_ref[...], w_ref[...], NT)
    dnormed_ref[...] = d_normed.astype(BF16)
    resid = tok_ref[...].astype(F32)
    rstd = lax.rsqrt(jnp.mean(resid * resid, axis=1, keepdims=True) + EPSILON)
    dgain_ref[...] += jnp.sum(d_normed * (resid * rstd), axis=0, keepdims=True)


def whole(shape):
    return pl.BlockSpec(shape, lambda *_: (0,) * len(shape), pipeline_mode=pl.Buffered(1))


def mixer_backward(
    openings, tok, w_in, taps, bias, heads, skip, gate, pre, y, enter, dgn, stats, inner
):
    tokens, width = tok.shape
    cols = w_in.shape[1]
    chan = skip.shape[1]
    blocks = tokens // STRETCH
    wide = chan + 2 * STATE
    per = STRETCH // 8
    rows = lambda n: pl.BlockSpec((STRETCH, n), lambda i, *_: (blocks - 1 - i, 0))
    return pl.pallas_call(
        functools.partial(backward_kernel, inner=inner),
        name="mixer_backward",
        grid_spec=pltpu.PrefetchScalarGridSpec(
            num_scalar_prefetch=1,
            grid=(blocks,),
            in_specs=[
                rows(width), whole((width, cols)), whole((4, wide)), whole((1, wide)),
                whole((8, LANES)), whole((1, chan)), whole((1, chan)),
                rows(cols),
                pl.BlockSpec((8, cols), lambda i, *_: (jnp.maximum((blocks - 1 - i) * per - 1, 0), 0)),
                rows(chan),
                pl.BlockSpec((1, STATE, chan), lambda i, *_: (blocks - 1 - i, 0, 0)),
                rows(chan),
                pl.BlockSpec((8, STRETCH), lambda i, *_: (0, blocks - 1 - i)),
            ],
            out_specs=[
                rows(cols), rows(width),
                pl.BlockSpec((8, wide), lambda i, *_: (0, 0)),
                pl.BlockSpec((1, wide), lambda i, *_: (0, 0)),
                pl.BlockSpec((8, LANES), lambda i, *_: (0, 0)),
                pl.BlockSpec((8, chan), lambda i, *_: (0, 0)),
                pl.BlockSpec((1, width), lambda i, *_: (0, 0)),
            ],
            scratch_shapes=[
                pltpu.VMEM((STATE, chan), F32),
                pltpu.VMEM((STRETCH + 8, wide), F32),
                pltpu.VMEM((STRETCH + 8, wide), F32),
            ],
        ),
        out_shape=[
            jax.ShapeDtypeStruct((tokens, cols), BF16),
            jax.ShapeDtypeStruct((tokens, width), BF16),
            jax.ShapeDtypeStruct((8, wide), F32),
            jax.ShapeDtypeStruct((1, wide), F32),
            jax.ShapeDtypeStruct((8, LANES), F32),
            jax.ShapeDtypeStruct((8, chan), F32),
            jax.ShapeDtypeStruct((1, width), F32),
        ],
        cost_estimate=pl.CostEstimate(
            flops=4 * tokens * width * cols, bytes_accessed=tokens * cols * 12, transcendentals=tokens * chan
        ),
        compiler_params=pltpu.CompilerParams(vmem_limit_bytes=60 << 20, dimension_semantics=("arbitrary",)),
    )(openings, tok, w_in, taps, bias, heads, skip, gate, pre, pre, y, enter, dgn, stats)


MESH = pl.DeviceIdType.MESH
CHUNKS = 4
TAGS = {"ahead": 1, "exit": 2}


def remote(source, target, send, recv, **where):
    return pltpu.make_async_remote_copy(
        src_ref=source, dst_ref=target, send_sem=send, recv_sem=recv, device_id=where, device_id_type=MESH
    )


def rows_at(ref, index, count):
    return ref.at[pl.ds(pl.multiple_of(index * count, count), count)]


def greet(axis, peers):
    barrier = pltpu.get_barrier_semaphore()
    for peer in peers:
        pl.semaphore_signal(barrier, inc=1, device_id={axis: peer}, device_id_type=MESH)


class Line:
    def __init__(self, tp, n_tp, own, whole_ref, send, recv):
        self.tp, self.n, self.own, self.whole_ref, self.send, self.recv = tp, n_tp, own, whole_ref, send, recv
        self.count = own.shape[0]

    def copy(self, way, step, own=False):
        shift = -1 if way == 0 else 1
        index = self.tp + shift * step
        slot = rows_at(self.whole_ref, index, self.count)
        return remote(
            self.own if own else slot, slot, self.send.at[way, step], self.recv.at[way, step], tp=self.tp - shift
        )

    def sends(self, way, step):
        if way == 0:
            return jnp.logical_and(self.tp < self.n - 1, self.tp >= step)
        return jnp.logical_and(self.tp > 0, self.tp + step <= self.n - 1)

    def takes(self, way, step):
        return self.tp >= step + 1 if way == 0 else self.tp + step + 1 <= self.n - 1

    def start(self, way, step):
        @pl.when(self.sends(way, step))
        def _():
            self.copy(way, step, own=step == 0).start()

    def arrive(self, way, step):
        @pl.when(self.takes(way, step))
        def _():
            shift = -1 if way == 0 else 1
            slot = rows_at(self.whole_ref, self.tp + shift * (step + 1), self.count)
            remote(
                slot, slot, self.send.at[way, step], self.recv.at[way, step], tp=self.tp + shift
            ).wait_recv()

    def finish(self, way, step):
        @pl.when(self.sends(way, step))
        def _():
            self.copy(way, step, own=step == 0).wait_send()


def forward_block(keep, tok, valid, gain_ref, w_ref, taps_ref, bias_ref, head_ref, skip_ref,
                  normed_ref, pre_ref, y_ref, gated_ref, enter_ref, state, xs):
    chan = y_ref.shape[1]
    xs[0:8, :] = xs[STRETCH:STRETCH + 8, :] * keep
    resid = tok.astype(F32)
    rstd = lax.rsqrt(jnp.mean(resid * resid, axis=1, keepdims=True) + EPSILON)
    normed = (resid * rstd * gain_ref[...]).astype(BF16)
    normed_ref[...] = normed
    pre_ref[...] = mm(normed, w_ref[...])
    xs[8:8 + STRETCH, :] = pre_ref[:, chan:2 * chan + 2 * STATE]
    conv = convolve(xs, taps_ref, bias_ref)
    feats = conv * sigmoid(conv)
    x = feats[:, :chan]
    bs = feats[:, chan:chan + STATE].astype(BF16)
    cs = feats[:, chan + STATE:].astype(BF16)
    rates, cumulative, grown, to_end = decays(pre_ref[:, 2 * chan + 2 * STATE:], head_ref, valid)
    across = cumulative.T
    grown_e = spread_heads(grown, chan)
    scaled = x * spread_heads(rates, chan)
    entering = state[...] * keep
    enter_ref[...] = entering
    y_ref[...] = mm(cs, entering.astype(BF16)) * grown_e
    state[...] = entering * grown_e[STRETCH - 1:STRETCH, :] + mm(
        bs, (scaled * spread_heads(to_end, chan)).astype(BF16), TN
    )
    overlap = jnp.where(lower_mask(), mm(cs, bs, NT), 0.0)
    scaled_b = scaled.astype(BF16)
    first = iota((STRETCH, LANES), 1) < HEAD
    for pair in range(chan // LANES):
        cols = slice(pair * LANES, (pair + 1) * LANES)
        both = scaled_b[:, cols]
        mats = [
            (weights_of(cumulative, across, 2 * pair + side) * overlap).astype(BF16) for side in range(2)
        ]
        zero = jnp.zeros_like(both)
        y_ref[:, cols] += mm(
            jnp.concatenate(mats, axis=1),
            jnp.concatenate([jnp.where(first, both, zero), jnp.where(first, zero, both)], axis=0),
        )
    pre_z = pre_ref[:, :chan]
    gated = (y_ref[...] + skip_ref[...] * x) * (pre_z * sigmoid(pre_z)) * valid
    gated_ref[...] = gated
    return jnp.sum(gated * gated, axis=1, keepdims=True)


def as_row(column):
    lane = iota((STRETCH, LANES), 1)
    return jnp.where(lane == 0, column, 0.0).T[0:8, :]


def as_column(row):
    return jnp.concatenate([row, jnp.zeros((LANES - 8, STRETCH), F32)], axis=0).T


def row_stats(stats_ref, inner):
    filled = as_column(stats_ref[...])
    return lax.rsqrt(filled[:, 0:1] * (1.0 / inner) + EPSILON), filled[:, 1:2], filled[:, 2:3]


def ahead_kernel(
    open_ref, step_bias, log_rate, direct, tok_ref, cot_ref, pz_ref, px_ref, pbc_ref, pdt_ref, pout_ref, mask_ref,
    norm_gain, conv_chan, bias_chan, conv_shared, bias_shared, gate_gain,
    tok_out, cot_out, win_out, normed_out, pre_out, y_out, enter_out, dgn_out, gn_out, rows_out, stats_ref,
    taps_ref, bias_ref, head_ref, skip_ref, gate_ref,
    pin_ref, gain_ref, tok_all, cot_all, w_in, w_out, normed, pre, y, gated, enter, dgn, gnormed, rows, state, xs, squares, crosses,
    squares_got, crosses_got,
    own_sem, z_send, z_recv, c_send, c_recv, f_send, f_recv, p_send, p_recv, q_send, q_recv, r_send, r_recv,
    all_sem, out_sem,
    *, n_tp, n_fs, inner,
):
    tp, me = lax.axis_index("tp"), lax.axis_index("fsdp")
    chip, core, chips = me // 2, me % 2, n_fs // 2
    partner = chip * 2 + 1 - core
    blocks = tok_all.shape[0] // STRETCH
    per = tok_ref.shape[0]
    chan = pout_ref.shape[1]
    pin_ref[:, :chan] = pz_ref[...]
    pin_ref[:, chan:2 * chan] = px_ref[...]
    pin_ref[:, 2 * chan:2 * chan + 2 * STATE] = pbc_ref[...]
    heads_here, rows_dt = pdt_ref.shape
    pin_ref[:, 2 * chan + 2 * STATE:] = jnp.concatenate(
        [pdt_ref[...].astype(F32), jnp.zeros((LANES - heads_here, rows_dt), F32)], axis=0
    ).T.astype(BF16)
    greet("fsdp", [((chip + d) % chips) * 2 + core for d in range(1, chips)] + [partner])
    greet("tp", [(tp + d) % n_tp for d in range(1, n_tp)])
    pl.semaphore_wait(pltpu.get_barrier_semaphore(), chips + n_tp - 1)

    packs = ((pin_ref, w_in), (pout_ref, w_out))
    count = pin_ref.shape[0]
    line = Line(tp, n_tp, tok_ref, tok_all, z_send, z_recv)
    late = Line(tp, n_tp, cot_ref, cot_all, c_send, c_recv)
    for way in range(2):
        line.start(way, 0)
    for j, (pack, full) in enumerate(packs):
        for d in range(1, chips):
            remote(
                pack, rows_at(full, me, count), f_send.at[j, d], f_recv.at[j, d], fsdp=((chip + d) % chips) * 2 + core
            ).start()
        remote(pack, rows_at(full, me, count), p_send.at[j, 0], p_recv.at[j, 0], fsdp=partner).start()
    own = [
        pltpu.make_async_copy(tok_ref, rows_at(tok_all, tp, per), own_sem.at[0]),
        pltpu.make_async_copy(pin_ref, rows_at(w_in, me, count), own_sem.at[1]),
        pltpu.make_async_copy(pout_ref, rows_at(w_out, me, count), own_sem.at[2]),
        pltpu.make_async_copy(cot_ref, rows_at(cot_all, tp, per), own_sem.at[3]),
    ]
    for copy in own:
        copy.start()
    state[...] = jnp.zeros_like(state)
    xs[...] = jnp.zeros_like(xs)
    lane = iota((8, LANES), 1)
    place = iota((8, LANES), 0)
    step_row, rate_row, skip_row = (
        sum(jnp.where(lane == head, source[head], 0.0) for head in range(heads_here))
        for source in (step_bias, log_rate, direct)
    )
    live = lane < heads_here
    head_ref[...] = jnp.where(
        place == 0, jnp.where(live, step_row, -100.0), jnp.where(live & (place == 1), -jnp.exp(rate_row), 0.0)
    )
    skip_ref[...] = spread_heads(skip_row, chan)[0:1, :]
    gain_ref[...] = norm_gain[...].reshape(gain_ref.shape)
    gate_ref[...] = gate_gain[...].reshape(gate_ref.shape)
    taps_ref[:, :chan] = conv_chan[...]
    taps_ref[:, chan:] = conv_shared[...]
    bias_ref[:, :chan] = bias_chan[...].reshape(1, chan)
    bias_ref[:, chan:] = bias_shared[...].reshape(1, 2 * STATE)
    for step in range(n_tp - 1):
        for way in range(2):
            line.arrive(way, step)
            if step + 1 < n_tp - 1:
                line.start(way, step + 1)
        if step == n_tp - 3 or n_tp < 3 and step == 0:
            for j, (pack, full) in enumerate(packs):
                for d in range(1, chips):
                    slot = rows_at(full, ((chip + chips - d) % chips) * 2 + core, count)
                    remote(slot, slot, f_send.at[j, d], f_recv.at[j, d], fsdp=partner).wait_recv()
                    remote(slot, slot, p_send.at[j, d], p_recv.at[j, d], fsdp=partner).start()
    for step in range(n_tp - 1):
        for way in range(2):
            line.finish(way, step)
    for way in range(2):
        late.start(way, 0)
    for j, (pack, full) in enumerate(packs):
        for d in range(chips):
            slot = rows_at(full, ((chip + chips - d) % chips) * 2 + 1 - core, count)
            remote(slot, slot, p_send.at[j, d], p_recv.at[j, d], fsdp=partner).wait()
        for d in range(1, chips):
            remote(pack, rows_at(full, me, count), f_send.at[j, d], f_recv.at[j, d], fsdp=partner).wait_send()
    for copy in own:
        copy.wait()
    wholes = [
        pltpu.make_async_copy(tok_all, tok_out, all_sem.at[0]), pltpu.make_async_copy(w_in, win_out, all_sem.at[1]),
    ]
    for copy in wholes:
        copy.start()

    def span(block):
        return pl.ds(pl.multiple_of(block * STRETCH, STRETCH), STRETCH)

    def out(k, block):
        at = span(block)
        pairs = (
            (normed.at[at], normed_out.at[at]), (pre.at[block % 2], pre_out.at[at]), (y.at[at], y_out.at[at]),
            (enter.at[block], enter_out.at[block]), (gnormed.at[at], gn_out.at[at]),
            (rows.at[block % 2], rows_out.at[at]), (dgn.at[at], dgn_out.at[at]), (cot_all.at[at], cot_out.at[at]),
        )
        return pltpu.make_async_copy(*pairs[k], out_sem.at[k, block])

    @pl.loop(0, blocks)
    def _(block):
        at = span(block)
        keep = jnp.where(open_ref[block] == 1, 0.0, 1.0).astype(F32)

        @pl.when(block >= 2)
        def _():
            out(1, block - 2).wait()

        valid = mask_ref[at].reshape(1, STRETCH).astype(F32)
        squares[:, at] = jnp.where(iota((8, STRETCH), 0) == 2, valid, 0.0)
        total = forward_block(
            keep, tok_all[at, :], as_column(squares[:, at])[:, 2:3], gain_ref, w_in, taps_ref, bias_ref, head_ref, skip_ref,
            normed.at[at], pre.at[block % 2], y.at[at], gated.at[at], enter.at[block], state, xs,
        )
        squares[0:1, at] = as_row(total)[0:1, :]
        for k in range(4):
            out(k, block).start()

        @pl.when(block == max(blocks - 2, 0))
        def _():
            for way in range(2):
                late.arrive(way, 0)
                if n_tp > 2:
                    late.start(way, 1)

    def swap(part, got, send, recv):
        for d in range(1, n_tp):
            remote(part, got.at[tp], send.at[d], recv.at[d], tp=(tp + d) % n_tp).start()
        got[tp] = part[...]
        for d in range(1, n_tp):
            slot = got.at[(tp + n_tp - d) % n_tp]
            remote(slot, slot, send.at[d], recv.at[d], tp=(tp + d) % n_tp).wait_recv()
        total = got[0]
        for peer in range(1, n_tp):
            total = total + got[peer]
        return total

    stats_ref[...] = swap(squares, squares_got, q_send, q_recv)

    @pl.loop(0, blocks)
    def _(block):
        at = span(block)

        @pl.when(block >= 2)
        def _():
            out(5, block - 2).wait()

        grstd, _, _ = row_stats(stats_ref.at[:, at], inner)
        value = (gated[at, :] * grstd * gate_ref[...]).astype(BF16)
        gnormed[at, :] = value
        rows[block % 2] = mm(value, w_out[...], NT).astype(BF16)
        out(4, block).start()
        out(5, block).start()

    def gradient(block):
        at = span(block)
        value = mm(cot_all[at, :], w_out[...])
        dgn[at, :] = value
        crosses[:, at] = as_row(jnp.sum(gate_ref[...] * value * gated[at, :], axis=1, keepdims=True))
        out(6, block).start()
        out(7, block).start()

    ratio = per // STRETCH

    def gradients(index):
        for k in range(ratio):
            gradient(index * ratio + k)

    gradients(tp)
    for step in range(n_tp - 1):
        for way in range(2):
            if step > 0:
                late.arrive(way, step)
                if step + 1 < n_tp - 1:
                    late.start(way, step + 1)
        for way in range(2):
            @pl.when(late.takes(way, step))
            def _():
                gradients(tp - step - 1 if way == 0 else tp + step + 1)

    total = swap(crosses, crosses_got, r_send, r_recv)
    stats_ref[1:2, :] = total[0:1, :]
    stats_ref[2:3, :] = squares[2:3, :]

    for copy in wholes:
        copy.wait()

    @pl.loop(0, blocks)
    def _(block):
        for k in (0, 2, 3, 4, 6, 7):
            out(k, block).wait()

    for block in range(max(blocks - 2, 0), blocks):
        out(1, block).wait()
        out(5, block).wait()
    for step in range(n_tp - 1):
        for way in range(2):
            late.finish(way, step)
    for d in range(1, n_tp):
        remote(squares, squares_got.at[tp], q_send.at[d], q_recv.at[d], tp=(tp + d) % n_tp).wait_send()
        remote(crosses, crosses_got.at[tp], r_send.at[d], r_recv.at[d], tp=(tp + d) % n_tp).wait_send()


def ahead(
    openings, heads, tokens, cotangent, projections, mask, vectors, n_tp, n_fs
):
    per, width = tokens.shape
    total = per * n_tp
    count, chan = projections[0].shape
    wide = chan + 2 * STATE
    cols = chan + wide + LANES
    blocks = total // STRETCH
    chips = n_fs // 2
    dma = pltpu.SemaphoreType.DMA
    anywhere = pl.BlockSpec(memory_space=pl.ANY)
    vmem = pl.BlockSpec(memory_space=pltpu.VMEM)
    shape = jax.ShapeDtypeStruct
    return pl.pallas_call(
        functools.partial(ahead_kernel, n_tp=n_tp, n_fs=n_fs, inner=chan * n_tp),
        name="ahead",
        in_specs=[pl.BlockSpec(memory_space=pltpu.SMEM)] * 4 + [vmem] * 14,
        out_specs=[anywhere] * 10 + [vmem] * 6,
        out_shape=[
            shape((total, width), BF16), shape((total, width), BF16), shape((count * n_fs, cols), BF16),
            shape((total, width), BF16), shape((total, cols), F32), shape((total, chan), F32),
            shape((blocks, STATE, chan), F32), shape((total, chan), F32), shape((total, chan), BF16),
            shape((total, width), BF16), shape((8, total), F32), shape((4, wide), F32), shape((1, wide), F32),
            shape((8, LANES), F32), shape((1, chan), F32), shape((1, chan), F32),
        ],
        scratch_shapes=[
            pltpu.VMEM((count, cols), BF16), pltpu.VMEM((1, width), F32),
            pltpu.VMEM((total, width), BF16), pltpu.VMEM((total, width), BF16),
            pltpu.VMEM((count * n_fs, cols), BF16), pltpu.VMEM((count * n_fs, chan), BF16),
            pltpu.VMEM((total, width), BF16), pltpu.VMEM((2, STRETCH, cols), F32), pltpu.VMEM((total, chan), F32),
            pltpu.VMEM((total, chan), F32), pltpu.VMEM((blocks, STATE, chan), F32), pltpu.VMEM((total, chan), F32),
            pltpu.VMEM((total, chan), BF16), pltpu.VMEM((2, STRETCH, width), BF16),
            pltpu.VMEM((STATE, chan), F32), pltpu.VMEM((STRETCH + 8, wide), F32),
            pltpu.VMEM((8, total), F32), pltpu.VMEM((8, total), F32),
            pltpu.VMEM((n_tp, 8, total), F32), pltpu.VMEM((n_tp, 8, total), F32),
            dma((4,)), dma((2, n_tp - 1)), dma((2, n_tp - 1)), dma((2, n_tp - 1)), dma((2, n_tp - 1)),
            dma((2, chips)), dma((2, chips)), dma((2, chips)), dma((2, chips)),
            dma((n_tp,)), dma((n_tp,)), dma((n_tp,)), dma((n_tp,)), dma((2,)), dma((8, blocks)),
        ],
        compiler_params=pltpu.CompilerParams(
            collective_id=TAGS["ahead"], has_side_effects=True, vmem_limit_bytes=63 << 20
        ),
    )(openings, *heads, tokens, cotangent, *projections, mask, *vectors)


def add_into(target, *sources):
    rows, tile = target.shape[0], 32

    @pl.loop(0, rows // tile)
    def _(i):
        at = pl.ds(pl.multiple_of(i * tile, tile), tile)
        total = sources[0][at, :].astype(F32)
        for source in sources[1:]:
            total = total + source[at, :].astype(F32)
        target[at, :] = total.astype(target.dtype)


def fill_rows(target, pieces):
    at = 0
    for source, row, start, length in pieces:
        for k in range(length // LANES):
            target[at:at + 1, :] = source[row:row + 1, start + k * LANES:start + (k + 1) * LANES]
            at += 1
    if at < target.shape[0]:
        target[at:, :] = jnp.zeros((target.shape[0] - at, LANES), F32)


def finish_kernel(
    tok_ref, cot_ref, mixed_ref, gain_ref, dn_ref, own_ref, bc_ref, mine_ref, shared_ref,
    output, grad_tokens, g_gain, g_z, g_x, g_bc, g_dt, g_taps, g_bias, g_taps_s, g_bias_s, g_log, g_step, g_skip, g_gate,
    g_out,
):
    chan, heads_here = g_z.shape[1], g_log.shape[0]
    resid = tok_ref[...].astype(F32)
    output[...] = (resid + mixed_ref[...].astype(F32)).astype(BF16)
    rstd = lax.rsqrt(jnp.mean(resid * resid, axis=1, keepdims=True) + EPSILON)
    scaled = dn_ref[...] * gain_ref[...].reshape(1, resid.shape[1])
    grad_tokens[...] = (
        cot_ref[...].astype(F32) + rstd * scaled
        - resid * (rstd * rstd * rstd) * jnp.mean(scaled * resid, axis=1, keepdims=True)
    ).astype(BF16)
    g_z[...] = own_ref[:, :chan]
    g_x[...] = own_ref[:, chan:2 * chan]
    g_dt[...] = own_ref[:, 2 * chan:2 * chan + LANES].T[0:heads_here, :]
    g_out[...] = own_ref[:, 2 * chan + LANES:]
    g_bc[...] = bc_ref[...]

    def row(source, at, length):
        return jnp.concatenate([source[at + k:at + k + 1, :] for k in range(length // LANES)], axis=1)

    per = chan // LANES
    for tap in range(4):
        g_taps[tap:tap + 1, :] = row(mine_ref, tap * per, chan)
        g_taps_s[tap:tap + 1, :] = row(shared_ref, tap * 2, 2 * STATE)
    g_bias[...] = row(mine_ref, 4 * per, chan).reshape(chan)
    g_gate[...] = row(mine_ref, 5 * per, chan).reshape(chan)
    skip = gather_heads(jnp.broadcast_to(row(mine_ref, 6 * per, chan), (8, chan)))
    g_skip[...] = skip[0:1, :heads_here].reshape(heads_here)
    g_log[...] = mine_ref[7 * per:7 * per + 1, :heads_here].reshape(heads_here)
    g_step[...] = mine_ref[7 * per + 1:7 * per + 2, :heads_here].reshape(heads_here)
    g_bias_s[...] = row(shared_ref, 8, 2 * STATE).reshape(2 * STATE)
    g_gain[...] = row(shared_ref, 10, g_gain.shape[0]).reshape(g_gain.shape[0])


def finish(tokens, cotangent, mixed, gain, dn, own, bc, mine, shared, heads_here):
    rows, width = tokens.shape
    count = own.shape[0]
    chan = (own.shape[1] - LANES) // 3
    vmem = pl.BlockSpec(memory_space=pltpu.VMEM)
    shape = lambda *extents: jax.ShapeDtypeStruct(extents, F32)
    outs = [
        jax.ShapeDtypeStruct((rows, width), BF16), jax.ShapeDtypeStruct((rows, width), BF16), shape(width),
        shape(count, chan), shape(count, chan), shape(count, 2 * STATE), shape(heads_here, count), shape(4, chan),
        shape(chan), shape(4, 2 * STATE), shape(2 * STATE), shape(heads_here), shape(heads_here), shape(heads_here),
        shape(chan), shape(count, chan),
    ]
    return pl.pallas_call(
        finish_kernel, name="finish", in_specs=[vmem] * 9, out_specs=[vmem] * len(outs), out_shape=outs,
        compiler_params=pltpu.CompilerParams(vmem_limit_bytes=40 << 20),
    )(tokens, cotangent, mixed, gain, dn, own, bc, mine, shared)


def exit_kernel(
    dn_ref, normed_ref, dpre_ref, cot_ref, gn_ref, dtaps_ref, dbias_ref, dhead_ref, dchan_ref, dgain_ref,
    dn_out, own_out, bc_out, mine_out, shared_out,
    gin_ref, gout_ref, mine_ref, shared_ref,
    z_held, z_got, near_in, near_out, far_in, far_out, got_in, got_out, mine_got, shared_got, shared_held, shared_z,
    bc_held, bc_got,
    zs, zr, ns, nr, fs, fr, ms, mr, ss, sr, ts, tr, bs, br,
    *, n_tp, n_fs,
):
    tp, me = lax.axis_index("tp"), lax.axis_index("fsdp")
    chip, core, chips = me // 2, me % 2, n_fs // 2
    partner = chip * 2 + 1 - core
    chan = gout_ref.shape[1]
    cols = gin_ref.shape[1]
    width = gin_ref.shape[0]
    fill_rows(
        mine_ref, [(dtaps_ref, tap, 0, chan) for tap in range(4)] + [(dbias_ref, 0, 0, chan)]
        + [(dchan_ref, row, 0, chan) for row in range(2)] + [(dhead_ref, row, 0, LANES) for row in range(2)]
    )
    fill_rows(
        shared_ref, [(dtaps_ref, tap, chan, 2 * STATE) for tap in range(4)] + [(dbias_ref, 0, chan, 2 * STATE)]
        + [(dgain_ref, 0, 0, width)]
    )
    block, count = dn_out.shape[0], own_out.shape[0]
    greet("fsdp", [(me + d) % n_fs for d in range(1, n_fs)])
    greet("tp", [(tp + d) % n_tp for d in range(1, n_tp)])
    pl.semaphore_wait(pltpu.get_barrier_semaphore(), n_fs - 1 + n_tp - 1)

    chunk = block // CHUNKS
    steps = (n_tp - 1) * CHUNKS

    def ahead(way, step):
        return n_tp - 1 - step // CHUNKS if way == 0 else step // CHUNKS

    def passes(way, step):
        return ahead(way, step) > tp if way == 0 else ahead(way, step) < tp

    def first(way):
        return tp == 0 if way == 0 else tp == n_tp - 1

    def local(way, step):
        return dn_ref.at[pl.ds(pl.multiple_of(ahead(way, step) * block + step % CHUNKS * chunk, chunk), chunk)]

    def pass_on(way, step, direct=False):
        towards = tp + 1 if way == 0 else tp - 1
        source = local(way, step) if direct else z_held.at[way, step]
        return remote(source, z_got.at[way, step], zs.at[way, step], zr.at[way, step], tp=towards)

    for way in range(2):
        @pl.when(first(way))
        def _():
            for step in range(2):
                pass_on(way, step, True).start()

    def advance(turn):
        for way in range(2):
            lag = jnp.maximum(tp - 1 if way == 0 else n_tp - 2 - tp, 0)
            step = turn - lag
            live = jnp.logical_and(step >= 0, step < steps)

            @pl.when(jnp.logical_and(first(way), live))
            def _():
                pass_on(way, step, True).wait_send()

                @pl.when(step + 2 < steps)
                def _():
                    pass_on(way, step + 2, True).start()

            @pl.when(jnp.logical_and(jnp.logical_and(passes(way, step), live), jnp.logical_not(first(way))))
            def _():
                pass_on(way, step).wait_recv()
                add_into(z_held.at[way, step], local(way, step), z_got.at[way, step])
                pass_on(way, step).start()

    parts = (
        (gin_ref, slice(2 * chan, cols), near_in, far_in, got_in),
        (gout_ref, slice(0, chan), near_out, far_out, got_out),
        (gin_ref, slice(chan, 2 * chan), near_in, far_in, got_in),
        (gin_ref, slice(0, chan), near_in, far_in, got_in),
    )

    def near(j, d):
        source, span, held, _, _ = parts[j]
        rows = rows_at(source, ((chip + d) % chips) * 2 + 1 - core, count)
        return remote(rows.at[:, span], held.at[d, :, span], ns.at[j, d], nr.at[j, d], fsdp=partner)

    def far(j, d):
        _, span, _, held, got = parts[j]
        return remote(
            held.at[d, :, span], got.at[d, :, span], fs.at[j, d], fr.at[j, d], fsdp=((chip + d) % chips) * 2 + core
        )

    order = [d for d in range(1, chips)]

    def small(d):
        peer = (me + d) % n_fs
        return (
            remote(mine_ref, mine_got.at[me], ms.at[d], mr.at[d], fsdp=peer),
            remote(shared_ref, shared_got.at[me], ss.at[d], sr.at[d], fsdp=peer),
        )

    for d in range(1, n_fs):
        for copy in small(d):
            copy.start()
    mine_got[me] = mine_ref[...]
    shared_got[me] = shared_ref[...]

    def differentiate(j):
        _, span, *_ = parts[j]
        left, right, target = (cot_ref, gn_ref, gout_ref) if j == 1 else (normed_ref, dpre_ref, gin_ref)
        tile = 256

        @pl.loop(0, width // tile)
        def _(piece):
            at = pl.ds(pl.multiple_of(piece * tile, tile), tile)
            target[at, span] = mm(left[:, at], right[:, span], TN).astype(BF16)

        for d in order + [0]:
            near(j, d).start()

    def send_sums(j):
        source, span, held, summed, _ = parts[j]
        for d in order:
            near(j, d).wait_recv()
            rows = rows_at(source, ((chip + d) % chips) * 2 + core, count)
            add_into(summed.at[d, :, span], rows.at[:, span], held.at[d, :, span])
            far(j, d).start()
        near(j, 0).wait_recv()

    differentiate(0)
    advance(0)
    differentiate(1)
    send_sums(0)
    advance(1)
    differentiate(2)
    send_sums(1)
    advance(2)
    differentiate(3)
    send_sums(2)
    advance(3)
    send_sums(3)
    at = 3
    turns = steps + max(n_tp - 3, 0)
    for d in range(1, n_fs):
        for copy in small(d):
            copy.wait_recv()
    total, again = mine_got[0], shared_got[0]
    for peer in range(1, n_fs):
        total, again = total + mine_got[peer], again + shared_got[peer]
    mine_out[...] = total
    shared_held[...] = again
    shared_z[tp] = again
    for d in range(1, n_tp):
        remote(shared_held, shared_z.at[tp], ts.at[d], tr.at[d], tp=(tp + d) % n_tp).start()
    pl.loop(at + 1, at + 5)(advance)

    def settle(j, target, span):
        source, _, held, _, got = parts[j]
        rows = rows_at(source, me, count)
        add_into(
            target, rows.at[:, span], held.at[0, :, span], *[got.at[d, :, span] for d in order]
        )

    for d in order:
        far(0, d).wait_recv()
    settle(0, bc_held, slice(2 * chan, 2 * chan + 2 * STATE))
    bc_got[tp] = bc_held[...]
    for d in range(1, n_tp):
        remote(bc_held, bc_got.at[tp], bs.at[d], br.at[d], tp=(tp + d) % n_tp).start()
    pl.loop(at + 5, turns)(advance)
    settle(0, own_out.at[:, 2 * chan:2 * chan + LANES], slice(2 * chan + 2 * STATE, cols))
    for j in (1, 2, 3):
        for d in order:
            far(j, d).wait_recv()
    settle(1, own_out.at[:, 2 * chan + LANES:], slice(0, chan))
    settle(2, own_out.at[:, chan:2 * chan], slice(chan, 2 * chan))
    settle(3, own_out.at[:, :chan], slice(0, chan))
    for d in range(1, n_tp):
        peer = (tp + n_tp - d) % n_tp
        remote(shared_held, shared_z.at[peer], ts.at[d], tr.at[d], tp=peer).wait_recv()
        remote(bc_held, bc_got.at[peer], bs.at[d], br.at[d], tp=peer).wait_recv()
    total = shared_z[0]
    for peer in range(1, n_tp):
        total = total + shared_z[peer]
    shared_out[...] = total
    add_into(bc_out, *[bc_got.at[peer] for peer in range(n_tp)])

    own = rows_at(dn_ref, tp, block)
    for way in range(2):
        for step in range(steps):
            @pl.when(jnp.logical_and(ahead(way, step) == tp, jnp.logical_not(first(way))))
            def _():
                pass_on(way, step).wait_recv()

    for value in range(n_tp):
        @pl.when(tp == value)
        def _():
            for part in range(CHUNKS):
                span = pl.ds(part * chunk, chunk)
                incoming = []
                if value > 0:
                    incoming.append(z_got.at[0, (n_tp - 1 - value) * CHUNKS + part])
                if value < n_tp - 1:
                    incoming.append(z_got.at[1, value * CHUNKS + part])
                add_into(dn_out.at[span], own.at[span], *incoming)

    for way in range(2):
        for step in range(steps):
            @pl.when(jnp.logical_and(passes(way, step), jnp.logical_not(first(way))))
            def _():
                pass_on(way, step).wait_send()
    for j in range(4):
        for d in range(chips):
            near(j, d).wait_send()
        for d in order:
            far(j, d).wait_send()
    for d in range(1, n_fs):
        for copy in small(d):
            copy.wait_send()
    for d in range(1, n_tp):
        remote(shared_held, shared_z.at[tp], ts.at[d], tr.at[d], tp=(tp + d) % n_tp).wait_send()
        remote(bc_held, bc_got.at[tp], bs.at[d], br.at[d], tp=(tp + d) % n_tp).wait_send()


def leave(dn, normed, dpre, cot, gnormed, small, n_tp, n_fs):
    block, width = dn.shape[0] // n_tp, dn.shape[1]
    count, cols = width // n_fs, dpre.shape[1]
    chan = gnormed.shape[1]
    chips, steps = n_fs // 2, (n_tp - 1) * CHUNKS
    dma = pltpu.SemaphoreType.DMA
    vmem = pl.BlockSpec(memory_space=pltpu.VMEM)
    room = lambda *shape: pltpu.VMEM(shape, BF16)
    shape = lambda *extents: jax.ShapeDtypeStruct(extents, F32)
    up = lambda n: -(-n // 8) * 8
    mine = (up(7 * chan // LANES + 2), LANES)
    shared = (up((10 * STATE + width) // LANES), LANES)
    outs = [
        shape(block, width), shape(count, 3 * chan + LANES), shape(count, 2 * STATE), shape(*mine), shape(*shared),
    ]
    return pl.pallas_call(
        functools.partial(exit_kernel, n_tp=n_tp, n_fs=n_fs),
        name="exit",
        in_specs=[vmem] * 10,
        out_specs=[vmem] * len(outs),
        out_shape=outs,
        scratch_shapes=[
            room(width, cols), room(width, chan), pltpu.VMEM(mine, F32), pltpu.VMEM(shared, F32),
            room(2, steps, block // CHUNKS, width), room(2, steps, block // CHUNKS, width),
            room(chips, count, cols), room(chips, count, chan), room(chips, count, cols), room(chips, count, chan),
            room(chips, count, cols), room(chips, count, chan),
            pltpu.VMEM((n_fs,) + mine, F32), pltpu.VMEM((n_fs,) + shared, F32),
            pltpu.VMEM(shared, F32), pltpu.VMEM((n_tp,) + shared, F32),
            room(count, 2 * STATE), room(n_tp, count, 2 * STATE),
            dma((2, steps)), dma((2, steps)), dma((4, chips)), dma((4, chips)), dma((4, chips)), dma((4, chips)),
            dma((n_fs,)), dma((n_fs,)), dma((n_fs,)), dma((n_fs,)), dma((n_tp,)), dma((n_tp,)), dma((n_tp,)),
            dma((n_tp,)),
        ],
        compiler_params=pltpu.CompilerParams(
            collective_id=TAGS["exit"], has_side_effects=True, vmem_limit_bytes=62 << 20
        ),
    )(dn, normed, dpre, cot, gnormed, *small)


def shards(
    tokens, cotangent, seq_start, token_valid, norm_gain, proj_z, proj_x, proj_bc, proj_dt, conv_chan, bias_chan,
    conv_shared, bias_shared, a_log, dt_bias, skip_gain, gate_gain, proj_out,
):
    chan, heads_here = proj_z.shape[1], proj_dt.shape[1]
    n_tp, n_fs = lax.axis_size("tp"), lax.axis_size("fsdp")
    tok_all, cot_all, w_in, normed, pre, y, enter, dgn, gnormed, out_rows, stats, taps, bias, heads, skip, gate = ahead(
        seq_start, (dt_bias, a_log, skip_gain), tokens, cotangent,
        (proj_z, proj_x, proj_bc, proj_dt.T, proj_out.T), token_valid,
        (norm_gain, conv_chan, bias_chan, conv_shared, bias_shared, gate_gain), n_tp, n_fs,
    )
    mixed = lax.psum_scatter(out_rows, "tp", scatter_dimension=0, tiled=True)
    dpre, dn_rows, *small = mixer_backward(
        seq_start, tok_all, w_in, taps, bias, heads, skip, gate, pre, y, enter, dgn, stats, chan * n_tp
    )
    sums = leave(dn_rows, normed, dpre, cot_all, gnormed, small, n_tp, n_fs)
    grads = list(finish(tokens, cotangent, mixed, norm_gain, *sums, heads_here))
    grads[6], grads[15] = grads[6].T, grads[15].T
    return tuple(grads)


def solution(mesh):
    in_specs = (
        P(("fsdp", "tp"), None), P(("fsdp", "tp"), None), P("fsdp"), P("fsdp"), P(), P("fsdp", "tp"),
        P("fsdp", "tp"), P("fsdp", None), P("fsdp", "tp"), P(None, "tp"), P("tp"), P(), P(), P("tp"), P("tp"),
        P("tp"), P("tp"), P("tp", "fsdp"),
    )
    out_specs = (
        P(("fsdp", "tp"), None), P(("fsdp", "tp"), None), P(), P("fsdp", "tp"), P("fsdp", "tp"), P("fsdp", None),
        P("fsdp", "tp"), P(None, "tp"), P("tp"), P(), P(), P("tp"), P("tp"), P("tp"), P("tp"), P("tp", "fsdp"),
    )
    return jax.shard_map(shards, mesh=mesh, in_specs=in_specs, out_specs=out_specs, check_vma=False)
```

time: 310 us -> 267 us (0.86)
  waiting for transfers between devices: 35.4 us -> 0.04 us
  Pallas kernels: 223 us -> 245 us
  local copies, waits for them, and re-layouts: 25.3 us -> 6.43 us
  other arithmetic: 11.2 us -> 0 us
    all_gather x1 -> x0, waiting for transfers between devices: 35.3 us -> none  [shards(): cot_all = lax.all_gather(late_cot, 'tp', axis=0, tiled=True)]
    pallas_call x5 -> x2, Pallas kernels: 91.2 us -> 119 us  [the longest x1 116 us: ahead(): pl.pallas_call(functools.partial(ahead_kernel, n_tp=n_tp, n_fs=n_fs, inne...]
    unnamed x83 -> x18, local copies, waits for them, and re-layouts: 22.8 us -> 6.43 us
    pallas_call x1, Pallas kernels: 91.8 us -> 85.4 us  [leave(): pl.pallas_call(functools.partial(exit_kernel, n_tp=n_tp, n_fs=n_fs), name...]
    pallas_call x3 -> x0, other arithmetic: 4.02 us -> none  [leave(): pl.pallas_call(functools.partial(exit_kernel, n_tp=n_tp, n_fs=n_fs), name...]
  transfers between devices with their start and end apart: 2 -> 1, of which waited for: 1 -> 0; matrix products, arithmetic and copies ran while one was open for 4% -> 0% of each run, Pallas kernels for 50% -> 48%
where the time goes in v4:
time: 267 us; the launch traced here: 265 us
  Pallas kernels  245 us (92%)
  between operations  14.1 us (5%)
  local copies, waits for them, and re-layouts  6.43 us (2%)
    pallas_call x1, Pallas kernels, ahead(): pl.pallas_call(functools.partial(ahead_kernel, n_tp=n_tp, n_fs=n_fs, inne...  116 us
    pallas_call x1, Pallas kernels, leave(): pl.pallas_call(functools.partial(exit_kernel, n_tp=n_tp, n_fs=n_fs), name...  85.4 us
    pallas_call x1, Pallas kernels, mixer_backward(): pl.pallas_call(functools.partial(backward_kernel, inner=inner), name='mix...  40.7 us
    unnamed x18, local copies, waits for them, and re-layouts  6.43 us
  transfers between devices with their start and end apart: 1, of which 0 were waited for; matrix products, arithmetic and copies ran while one was open for 0% of the time, Pallas kernels for 48%

profile of v4, /device:TPU:9, one launch (start us, length us, event | category | flops | bytes accessed | tf_op | source)
XLA Modules:
  0.0 265.3 jit_solution(10156442211868890760)
XLA Ops:
  7.2 0.0 reduce-scatter.2.cloned.1.call-start
  7.2 116.2 %ahead.1 = (bf16[1024,1536]{1,0:T(8,128)(2,1)}, bf16[1024,1536]{1,0:T(8,128)(2,1)}, bf16[1536,1920]{1,0:T(8,128)(2,1)}, bf16[1024,1536]{1,0:T(8,128)(2,1)}, f32[...) custom-call(s32[4]{0:T(128)} %open_ref.3, ...), custom_call_target="tpu_custom_call" | custom-call | tf_op jit(solution)/shard_map/ahead/pallas_call | solution.py:616
  123.4 0.0 reduce-scatter.2.cloned.1.call-update
  123.4 40.7 %mixer_backward.1 = (bf16[1024,1920]{1,0:T(8,128)(2,1)}, bf16[1024,1536]{1,0:T(8,128)(2,1)}, f32[8,1024]{1,0:T(8,128)}, f32[1,1024]{1,0:T(1,128)}, f32[8,128]{1,...) custom-call(s32[4]{0:T(128)} %open_ref.3, bf16[1024,1536]{1,0:T(8,128)(2,1)} %get-tuple-element.61.tok_ref, ...), custom_call_target="tpu_custom_call" | custom-call | flops 12079595520 | bytes 23592960 | tf_op jit(solution)/shard_map/mixer_backward/pallas_call | solution.py:222
  164.1 0.0 copy-start
  164.1 0.0 copy-start.1
  164.1 0.0 copy-start.6
  164.1 85.4 %exit.1 = (f32[256,1536]{1,0:T(8,128)}, f32[192,2432]{1,0:T(8,128)}, f32[192,256]{1,0:T(8,128)}, f32[48,128]{1,0:T(8,128)}, f32[24,128]{1,0:T(8,128)}) custom-call(bf16[1024,1536]{1,0:T(8,128)(2,1)} %get-tuple-element.73.dn_ref, bf16[1024,1536]{1,0:T(8,128)(2,1)} %get-tuple-element.74.normed_ref, bf16[1024,1920]{1,0:T(8,128)(2,1)} %get-tuple-element.75.dpre_ref, ...), custom_call_target="tpu_custom_call" | custom-call | tf_op jit(solution)/shard_map/exit/pallas_call | solution.py:964
  249.5 0.0 reduce-scatter.2.cloned.1.call-done.mixed_ref
  249.5 0.0 copy-done
  249.5 0.0 copy-done.1
  249.5 0.0 copy-done.6
  249.6 0.0 copy-start.2
  249.6 1.5 copy-done.2
  251.1 0.0 copy-start.3
  251.1 1.4 copy-done.3
  252.5 0.0 copy-start.4
  252.5 1.1 copy-done.4
  253.6 0.0 copy-start.5
  253.6 0.9 copy-done.5
  254.5 0.0 copy-start.7
  254.5 0.7 copy-done.7
  255.3 0.0 copy-start.8
  255.3 0.7 copy-done.8
  256.0 2.4 finish.1
Async XLA Ops:
  7.2 242.3 %reduce-scatter.2.cloned.1.call-start = ((), (), s32[]{:S(2)}) async-start(), calls=%async_computation.1 | async-start | bytes 3932160 | tf_op jit(solution)/shard_map/reduce_scatter | solution.py:999
  164.1 85.4 %copy-start = (bf16[256,1536]{1,0:T(8,128)(2,1)S(1)}, bf16[256,1536]{1,0:T(8,128)(2,1)}, u32[]{:S(2)}) copy-start(bf16[256,1536]{1,0:T(8,128)(2,1)} %tok_ref.3) | copy-start | bytes 2359300
  164.1 85.4 %copy-start.1 = (bf16[256,1536]{1,0:T(8,128)(2,1)S(1)}, bf16[256,1536]{1,0:T(8,128)(2,1)}, u32[]{:S(2)}) copy-start(bf16[256,1536]{1,0:T(8,128)(2,1)} %cot_ref.3) | copy-start | bytes 2359300
  164.1 85.4 %copy-start.6 = (f32[1536]{0:T(1024)S(1)}, f32[1536]{0:T(1024)}, u32[]{:S(2)}) copy-start(f32[1536]{0:T(1024)} %gain_ref.1) | copy-start | bytes 18436
  249.6 1.5 copy-start.2
  251.1 1.4 copy-start.3
  252.5 1.1 copy-start.4
  253.6 0.9 copy-start.5
  254.5 0.7 copy-start.7
  255.3 0.7 copy-start.8
Sparse Core Ops, SparseCore 0:
  123.5 70.1 reduce-scatter.1

commit v5 on v4

--- a/solution.py
+++ b/solution.py
@@ -11,6 +11,7 @@
 STRETCH = 256
 LANES = 128
 EPSILON = 1e-05
+PLACES = 3
 F32 = jnp.float32
 BF16 = jnp.bfloat16
 NN = (((1,), (0,)), ((), ()))
@@ -82,11 +83,11 @@
 
 
 def backward_kernel(
-    open_ref, tok_ref, w_ref, taps_ref, bias_ref, head_ref, skip_ref, gate_ref,
-    pre_ref, halo_ref, y_ref, enter_ref, dgn_ref, stats_ref,
-    dpre_ref, dnormed_ref, dtaps_ref, dbias_ref, dhead_ref, dchan_ref, dgain_ref,
-    dstate, xs, dus,
-    *, inner,
+    open_ref, tok_ref, w_hbm, taps_ref, bias_ref, head_ref, skip_ref, gate_ref,
+    pre_ref, halo_ref, y_ref, enter_ref, dgn_ref, stats_ref, rows_ref,
+    dpre_ref, dnormed_ref, dtaps_ref, dbias_ref, dhead_ref, dchan_ref, dgain_ref, mixed_ref,
+    dstate, xs, dus, rows, w_ref, o_got, fetch_sem, o_send, o_recv,
+    *, inner, n_tp,
 ):
     chan = y_ref.shape[1]
     wide = chan + 2 * STATE
@@ -94,6 +95,31 @@
     block = pl.num_programs(0) - 1 - step
     opening = open_ref[block] == 1
     keep = jnp.where(opening, 0.0, 1.0).astype(F32)
+    tp = lax.axis_index("tp")
+    per = rows.shape[0] // n_tp
+    chunk = per // CHUNKS
+    sums = LineSum(
+        tp, n_tp, CHUNKS - EARLY, lambda index, part: chunk_of(rows, index, per, part + EARLY, chunk),
+        lambda index, part: chunk_of(rows_ref, index, per, part + EARLY, chunk), o_got, o_send, o_recv,
+    )
+
+    fetches = (
+        pltpu.make_async_copy(rows_ref, rows, fetch_sem.at[0]), pltpu.make_async_copy(w_hbm, w_ref, fetch_sem.at[1])
+    )
+
+    def turn(place):
+        at = step * PLACES + place - 2
+
+        @pl.when(jnp.logical_and(at >= 0, at < sums.turns))
+        def _():
+            sums.advance(at)
+
+    @pl.when(step == 0)
+    def _():
+        for fetch in fetches:
+            fetch.start()
+        line_greeting(tp, n_tp)
+        sums.kick()
 
     @pl.when(step == 0)
     def _():
@@ -138,6 +164,7 @@
     dchan_ref[0:1, :] += jnp.sum(dgn * gated * grstd, axis=0, keepdims=True)
     dchan_ref[1:2, :] += jnp.sum(d_mixed * x, axis=0, keepdims=True)
 
+    turn(0)
     dy_b = d_mixed.astype(BF16)
     dy = dy_b.astype(F32)
     scaled = x * rates_e
@@ -162,6 +189,7 @@
             mats.append((weight * overlap).astype(BF16))
             d_overlap = d_overlap + mm(sides[side], x_pair, NT) * weight
         parts.append(mm(jnp.concatenate(mats, axis=0), jnp.concatenate(sides, axis=0), TN))
+    turn(1)
     d_scaled = jnp.concatenate(parts, axis=1) + tail
     scaled_r = scaled_b.astype(F32)
     d_cum = gather_heads(dy * y - scaled_r * d_scaled)
@@ -198,19 +226,31 @@
     dpre_ref[:, chan:2 * chan + 2 * STATE] = d_pre.astype(BF16)
     dus[STRETCH:STRETCH + 8, :] = d_conv[0:8, :] * keep
 
+    @pl.when(step == 0)
+    def _():
+        for fetch in fetches:
+            fetch.wait()
+
+    turn(2)
     d_normed = mm(dpre_ref[...], w_ref[...], NT)
     dnormed_ref[...] = d_normed.astype(BF16)
     resid = tok_ref[...].astype(F32)
     rstd = lax.rsqrt(jnp.mean(resid * resid, axis=1, keepdims=True) + EPSILON)
     dgain_ref[...] += jnp.sum(d_normed * (resid * rstd), axis=0, keepdims=True)
 
+    @pl.when(step == pl.num_programs(0) - 1)
+    def _():
+        pl.loop(jnp.minimum(step * PLACES + 1, sums.turns), sums.turns)(sums.advance)
+        sums.settle(lambda part: mixed_ref.at[pl.ds(part * chunk, chunk)])
+        sums.drain()
+
 
 def whole(shape):
     return pl.BlockSpec(shape, lambda *_: (0,) * len(shape), pipeline_mode=pl.Buffered(1))
 
 
 def mixer_backward(
-    openings, tok, w_in, taps, bias, heads, skip, gate, pre, y, enter, dgn, stats, inner
+    openings, tok, w_in, taps, bias, heads, skip, gate, pre, y, enter, dgn, stats, out_rows, inner, n_tp
 ):
     tokens, width = tok.shape
     cols = w_in.shape[1]
@@ -218,15 +258,17 @@
     blocks = tokens // STRETCH
     wide = chan + 2 * STATE
     per = STRETCH // 8
+    steps = (n_tp - 1) * (CHUNKS - EARLY)
+    kept = tokens // n_tp // CHUNKS * (CHUNKS - EARLY)
     rows = lambda n: pl.BlockSpec((STRETCH, n), lambda i, *_: (blocks - 1 - i, 0))
     return pl.pallas_call(
-        functools.partial(backward_kernel, inner=inner),
+        functools.partial(backward_kernel, inner=inner, n_tp=n_tp),
         name="mixer_backward",
         grid_spec=pltpu.PrefetchScalarGridSpec(
             num_scalar_prefetch=1,
             grid=(blocks,),
             in_specs=[
-                rows(width), whole((width, cols)), whole((4, wide)), whole((1, wide)),
+                rows(width), pl.BlockSpec(memory_space=pl.ANY), whole((4, wide)), whole((1, wide)),
                 whole((8, LANES)), whole((1, chan)), whole((1, chan)),
                 rows(cols),
                 pl.BlockSpec((8, cols), lambda i, *_: (jnp.maximum((blocks - 1 - i) * per - 1, 0), 0)),
@@ -234,6 +276,7 @@
                 pl.BlockSpec((1, STATE, chan), lambda i, *_: (blocks - 1 - i, 0, 0)),
                 rows(chan),
                 pl.BlockSpec((8, STRETCH), lambda i, *_: (0, blocks - 1 - i)),
+                pl.BlockSpec(memory_space=pl.ANY),
             ],
             out_specs=[
                 rows(cols), rows(width),
@@ -242,11 +285,18 @@
                 pl.BlockSpec((8, LANES), lambda i, *_: (0, 0)),
                 pl.BlockSpec((8, chan), lambda i, *_: (0, 0)),
                 pl.BlockSpec((1, width), lambda i, *_: (0, 0)),
+                pl.BlockSpec((kept, width), lambda i, *_: (0, 0)),
             ],
             scratch_shapes=[
                 pltpu.VMEM((STATE, chan), F32),
                 pltpu.VMEM((STRETCH + 8, wide), F32),
                 pltpu.VMEM((STRETCH + 8, wide), F32),
+                pltpu.VMEM((tokens, width), BF16),
+                pltpu.VMEM((width, cols), BF16),
+                pltpu.VMEM((2, steps, tokens // n_tp // CHUNKS, width), BF16),
+                pltpu.SemaphoreType.DMA((2,)),
+                pltpu.SemaphoreType.DMA((2, steps)),
+                pltpu.SemaphoreType.DMA((2, steps)),
             ],
         ),
         out_shape=[
@@ -257,17 +307,22 @@
             jax.ShapeDtypeStruct((8, LANES), F32),
             jax.ShapeDtypeStruct((8, chan), F32),
             jax.ShapeDtypeStruct((1, width), F32),
+            jax.ShapeDtypeStruct((kept, width), F32),
         ],
         cost_estimate=pl.CostEstimate(
             flops=4 * tokens * width * cols, bytes_accessed=tokens * cols * 12, transcendentals=tokens * chan
         ),
-        compiler_params=pltpu.CompilerParams(vmem_limit_bytes=60 << 20, dimension_semantics=("arbitrary",)),
-    )(openings, tok, w_in, taps, bias, heads, skip, gate, pre, pre, y, enter, dgn, stats)
+        compiler_params=pltpu.CompilerParams(
+            collective_id=TAGS["backward"], has_side_effects=True, vmem_limit_bytes=60 << 20,
+            dimension_semantics=("arbitrary",),
+        ),
+    )(openings, tok, w_in, taps, bias, heads, skip, gate, pre, pre, y, enter, dgn, stats, out_rows)
 
 
 MESH = pl.DeviceIdType.MESH
 CHUNKS = 4
-TAGS = {"ahead": 1, "exit": 2}
+EARLY = 1
+TAGS = {"ahead": 1, "backward": 2, "exit": 3}
 
 
 def remote(source, target, send, recv, **where):
@@ -325,6 +380,110 @@
         @pl.when(self.sends(way, step))
         def _():
             self.copy(way, step, own=step == 0).wait_send()
+
+
+class LineSum:
+    def __init__(self, tp, n_tp, per, local, origin, got, send, recv):
+        self.tp, self.n, self.per, self.local_of, self.origin = tp, n_tp, per, local, origin
+        self.got, self.send, self.recv = got, send, recv
+        self.steps = (n_tp - 1) * per
+        self.paced = max(n_tp - 2, 0) * per
+        self.turns = self.paced + max(n_tp - 3, 0)
+
+    def ahead(self, way, step):
+        return self.n - 1 - step // self.per if way == 0 else step // self.per
+
+    def passes(self, way, step):
+        return self.ahead(way, step) > self.tp if way == 0 else self.ahead(way, step) < self.tp
+
+    def first(self, way):
+        return self.tp == 0 if way == 0 else self.tp == self.n - 1
+
+    def local(self, way, step):
+        return self.local_of(self.ahead(way, step), step % self.per)
+
+    def copy(self, way, step, direct):
+        source = (self.origin if direct else self.local_of)(self.ahead(way, step), step % self.per)
+        return remote(
+            source, self.got.at[way, step], self.send.at[way, step], self.recv.at[way, step],
+            tp=self.tp + 1 if way == 0 else self.tp - 1,
+        )
+
+    def kick(self):
+        for way in range(2):
+            @pl.when(self.first(way))
+            def _():
+                for step in range(min(2, self.steps) if self.paced else self.steps):
+                    self.copy(way, step, True).start()
+
+    def advance(self, turn):
+        for way in range(2):
+            lag = jnp.maximum(self.tp - 1 if way == 0 else self.n - 2 - self.tp, 0)
+            step = turn - lag
+            live = jnp.logical_and(step >= 0, step < self.paced)
+
+            @pl.when(jnp.logical_and(self.first(way), live))
+            def _():
+                self.copy(way, step, True).wait_send()
+
+                @pl.when(step + 2 < self.steps)
+                def _():
+                    self.copy(way, step + 2, True).start()
+
+                @pl.when(step == self.paced - 1)
+                def _():
+                    for rest in range(self.paced + 2, self.steps):
+                        self.copy(way, rest, True).start()
+
+            @pl.when(jnp.logical_and(jnp.logical_and(self.passes(way, step), live), jnp.logical_not(self.first(way))))
+            def _():
+                copy = self.copy(way, step, False)
+                copy.wait_recv()
+                add_into(self.local(way, step), self.local(way, step), self.got.at[way, step])
+                copy.start()
+
+    def settle(self, target):
+        for way in range(2):
+            for step in range(self.steps):
+                @pl.when(jnp.logical_and(self.ahead(way, step) == self.tp, jnp.logical_not(self.first(way))))
+                def _():
+                    self.copy(way, step, False).wait_recv()
+
+        for value in range(self.n):
+            @pl.when(self.tp == value)
+            def _():
+                for part in range(self.per):
+                    incoming = []
+                    if value > 0:
+                        incoming.append(self.got.at[0, (self.n - 1 - value) * self.per + part])
+                    if value < self.n - 1:
+                        incoming.append(self.got.at[1, value * self.per + part])
+                    add_into(target(part), self.local_of(value, part), *incoming)
+
+    def drain(self):
+        for way in range(2):
+            @pl.when(self.first(way))
+            def _():
+                for step in range(self.paced, self.steps):
+                    self.copy(way, step, True).wait_send()
+
+            for step in range(self.steps):
+                @pl.when(jnp.logical_and(self.passes(way, step), jnp.logical_not(self.first(way))))
+                def _():
+                    self.copy(way, step, False).wait_send()
+
+
+def chunk_of(ref, block, rows, part, chunk):
+    return ref.at[pl.ds(pl.multiple_of(block * rows + part * chunk, chunk), chunk)]
+
+
+def line_greeting(tp, n_tp):
+    barrier = pltpu.get_barrier_semaphore()
+    for near, there in ((tp - 1, tp > 0), (tp + 1, tp < n_tp - 1)):
+        @pl.when(there)
+        def _():
+            pl.semaphore_signal(barrier, inc=1, device_id={"tp": near}, device_id_type=MESH)
+    pl.semaphore_wait(barrier, jnp.where(tp > 0, 1, 0) + jnp.where(tp < n_tp - 1, 1, 0))
 
 
 def forward_block(keep, tok, valid, gain_ref, w_ref, taps_ref, bias_ref, head_ref, skip_ref,
@@ -389,12 +548,12 @@
 def ahead_kernel(
     open_ref, step_bias, log_rate, direct, tok_ref, cot_ref, pz_ref, px_ref, pbc_ref, pdt_ref, pout_ref, mask_ref,
     norm_gain, conv_chan, bias_chan, conv_shared, bias_shared, gate_gain,
-    tok_out, cot_out, win_out, normed_out, pre_out, y_out, enter_out, dgn_out, gn_out, rows_out, stats_ref,
+    tok_out, cot_out, win_out, normed_out, pre_out, y_out, enter_out, dgn_out, gn_out, rows_out, mixed_out, stats_ref,
     taps_ref, bias_ref, head_ref, skip_ref, gate_ref,
     pin_ref, gain_ref, tok_all, cot_all, w_in, w_out, normed, pre, y, gated, enter, dgn, gnormed, rows, state, xs, squares, crosses,
-    squares_got, crosses_got,
+    squares_got, crosses_got, o_got,
     own_sem, z_send, z_recv, c_send, c_recv, f_send, f_recv, p_send, p_recv, q_send, q_recv, r_send, r_recv,
-    all_sem, out_sem,
+    all_sem, out_sem, o_send, o_recv,
     *, n_tp, n_fs, inner,
 ):
     tp, me = lax.axis_index("tp"), lax.axis_index("fsdp")
@@ -488,10 +647,12 @@
 
     def out(k, block):
         at = span(block)
+        chunk = per // CHUNKS * EARLY
+        kept = pl.ds(pl.multiple_of(block * STRETCH + chunk, chunk), STRETCH - chunk)
         pairs = (
             (normed.at[at], normed_out.at[at]), (pre.at[block % 2], pre_out.at[at]), (y.at[at], y_out.at[at]),
             (enter.at[block], enter_out.at[block]), (gnormed.at[at], gn_out.at[at]),
-            (rows.at[block % 2], rows_out.at[at]), (dgn.at[at], dgn_out.at[at]), (cot_all.at[at], cot_out.at[at]),
+            (rows.at[kept], rows_out.at[kept]), (dgn.at[at], dgn_out.at[at]), (cot_all.at[at], cot_out.at[at]),
         )
         return pltpu.make_async_copy(*pairs[k], out_sem.at[k, block])
 
@@ -539,16 +700,17 @@
     def _(block):
         at = span(block)
 
-        @pl.when(block >= 2)
-        def _():
-            out(5, block - 2).wait()
-
         grstd, _, _ = row_stats(stats_ref.at[:, at], inner)
         value = (gated[at, :] * grstd * gate_ref[...]).astype(BF16)
         gnormed[at, :] = value
-        rows[block % 2] = mm(value, w_out[...], NT).astype(BF16)
+        rows[at, :] = mm(value, w_out[...], NT).astype(BF16)
         out(4, block).start()
         out(5, block).start()
+
+    chunk = per // CHUNKS
+    piece = lambda index, part: chunk_of(rows, index, per, part, chunk)
+    sums = LineSum(tp, n_tp, EARLY, piece, piece, o_got, o_send, o_recv)
+    sums.kick()
 
     def gradient(block):
         at = span(block)
@@ -565,6 +727,7 @@
             gradient(index * ratio + k)
 
     gradients(tp)
+    middle = min(sums.turns, 3)
     for step in range(n_tp - 1):
         for way in range(2):
             if step > 0:
@@ -575,8 +738,14 @@
             @pl.when(late.takes(way, step))
             def _():
                 gradients(tp - step - 1 if way == 0 else tp + step + 1)
+        if step == max(n_tp - 3, 0):
+            pl.loop(0, middle)(sums.advance)
 
     total = swap(crosses, crosses_got, r_send, r_recv)
+    if middle < sums.turns:
+        pl.loop(middle, sums.turns)(sums.advance)
+    sums.settle(lambda part: mixed_out.at[pl.ds(part * chunk, chunk)])
+
     stats_ref[1:2, :] = total[0:1, :]
     stats_ref[2:3, :] = squares[2:3, :]
 
@@ -585,15 +754,15 @@
 
     @pl.loop(0, blocks)
     def _(block):
-        for k in (0, 2, 3, 4, 6, 7):
+        for k in (0, 2, 3, 4, 5, 6, 7):
             out(k, block).wait()
 
     for block in range(max(blocks - 2, 0), blocks):
         out(1, block).wait()
-        out(5, block).wait()
     for step in range(n_tp - 1):
         for way in range(2):
             late.finish(way, step)
+    sums.drain()
     for d in range(1, n_tp):
         remote(squares, squares_got.at[tp], q_send.at[d], q_recv.at[d], tp=(tp + d) % n_tp).wait_send()
         remote(crosses, crosses_got.at[tp], r_send.at[d], r_recv.at[d], tp=(tp + d) % n_tp).wait_send()
@@ -617,12 +786,13 @@
         functools.partial(ahead_kernel, n_tp=n_tp, n_fs=n_fs, inner=chan * n_tp),
         name="ahead",
         in_specs=[pl.BlockSpec(memory_space=pltpu.SMEM)] * 4 + [vmem] * 14,
-        out_specs=[anywhere] * 10 + [vmem] * 6,
+        out_specs=[anywhere] * 10 + [vmem] * 7,
         out_shape=[
             shape((total, width), BF16), shape((total, width), BF16), shape((count * n_fs, cols), BF16),
             shape((total, width), BF16), shape((total, cols), F32), shape((total, chan), F32),
             shape((blocks, STATE, chan), F32), shape((total, chan), F32), shape((total, chan), BF16),
-            shape((total, width), BF16), shape((8, total), F32), shape((4, wide), F32), shape((1, wide), F32),
+            shape((total, width), BF16), shape((per // CHUNKS * EARLY, width), F32), shape((8, total), F32),
+            shape((4, wide), F32), shape((1, wide), F32),
             shape((8, LANES), F32), shape((1, chan), F32), shape((1, chan), F32),
         ],
         scratch_shapes=[
@@ -631,13 +801,15 @@
             pltpu.VMEM((count * n_fs, cols), BF16), pltpu.VMEM((count * n_fs, chan), BF16),
             pltpu.VMEM((total, width), BF16), pltpu.VMEM((2, STRETCH, cols), F32), pltpu.VMEM((total, chan), F32),
             pltpu.VMEM((total, chan), F32), pltpu.VMEM((blocks, STATE, chan), F32), pltpu.VMEM((total, chan), F32),
-            pltpu.VMEM((total, chan), BF16), pltpu.VMEM((2, STRETCH, width), BF16),
+            pltpu.VMEM((total, chan), BF16), pltpu.VMEM((total, width), BF16),
             pltpu.VMEM((STATE, chan), F32), pltpu.VMEM((STRETCH + 8, wide), F32),
             pltpu.VMEM((8, total), F32), pltpu.VMEM((8, total), F32),
             pltpu.VMEM((n_tp, 8, total), F32), pltpu.VMEM((n_tp, 8, total), F32),
+            pltpu.VMEM((2, (n_tp - 1) * EARLY, per // CHUNKS, width), BF16),
             dma((4,)), dma((2, n_tp - 1)), dma((2, n_tp - 1)), dma((2, n_tp - 1)), dma((2, n_tp - 1)),
             dma((2, chips)), dma((2, chips)), dma((2, chips)), dma((2, chips)),
             dma((n_tp,)), dma((n_tp,)), dma((n_tp,)), dma((n_tp,)), dma((2,)), dma((8, blocks)),
+            dma((2, (n_tp - 1) * EARLY)), dma((2, (n_tp - 1) * EARLY)),
         ],
         compiler_params=pltpu.CompilerParams(
             collective_id=TAGS["ahead"], has_side_effects=True, vmem_limit_bytes=63 << 20
@@ -668,24 +840,26 @@
 
 
 def finish_kernel(
-    tok_ref, cot_ref, mixed_ref, gain_ref, dn_ref, own_ref, bc_ref, mine_ref, shared_ref,
+    tok_ref, cot_ref, early_ref, mixed_ref, gain_ref, dn_ref, own_ref, bc_ref, mine_ref, shared_ref,
     output, grad_tokens, g_gain, g_z, g_x, g_bc, g_dt, g_taps, g_bias, g_taps_s, g_bias_s, g_log, g_step, g_skip, g_gate,
     g_out,
 ):
     chan, heads_here = g_z.shape[1], g_log.shape[0]
     resid = tok_ref[...].astype(F32)
-    output[...] = (resid + mixed_ref[...].astype(F32)).astype(BF16)
+    early = early_ref.shape[0]
+    output[0:early, :] = (resid[0:early, :] + early_ref[...]).astype(BF16)
+    output[early:, :] = (resid[early:, :] + mixed_ref[...]).astype(BF16)
     rstd = lax.rsqrt(jnp.mean(resid * resid, axis=1, keepdims=True) + EPSILON)
-    scaled = dn_ref[...] * gain_ref[...].reshape(1, resid.shape[1])
+    scaled = dn_ref[...].astype(F32) * gain_ref[...].reshape(1, resid.shape[1])
     grad_tokens[...] = (
         cot_ref[...].astype(F32) + rstd * scaled
         - resid * (rstd * rstd * rstd) * jnp.mean(scaled * resid, axis=1, keepdims=True)
     ).astype(BF16)
-    g_z[...] = own_ref[:, :chan]
-    g_x[...] = own_ref[:, chan:2 * chan]
-    g_dt[...] = own_ref[:, 2 * chan:2 * chan + LANES].T[0:heads_here, :]
-    g_out[...] = own_ref[:, 2 * chan + LANES:]
-    g_bc[...] = bc_ref[...]
+    g_z[...] = own_ref[:, :chan].astype(F32)
+    g_x[...] = own_ref[:, chan:2 * chan].astype(F32)
+    g_dt[...] = own_ref[:, 2 * chan:2 * chan + LANES].astype(F32).T[0:heads_here, :]
+    g_out[...] = own_ref[:, 2 * chan + LANES:].astype(F32)
+    g_bc[...] = bc_ref[...].astype(F32)
 
     def row(source, at, length):
         return jnp.concatenate([source[at + k:at + k + 1, :] for k in range(length // LANES)], axis=1)
@@ -704,7 +878,7 @@
     g_gain[...] = row(shared_ref, 10, g_gain.shape[0]).reshape(g_gain.shape[0])
 
 
-def finish(tokens, cotangent, mixed, gain, dn, own, bc, mine, shared, heads_here):
+def finish(tokens, cotangent, early, mixed, gain, dn, own, bc, mine, shared, heads_here):
     rows, width = tokens.shape
     count = own.shape[0]
     chan = (own.shape[1] - LANES) // 3
@@ -717,16 +891,17 @@
         shape(chan), shape(count, chan),
     ]
     return pl.pallas_call(
-        finish_kernel, name="finish", in_specs=[vmem] * 9, out_specs=[vmem] * len(outs), out_shape=outs,
+        finish_kernel, name="finish", in_specs=[vmem] * 10, out_specs=[vmem] * len(outs), out_shape=outs,
         compiler_params=pltpu.CompilerParams(vmem_limit_bytes=40 << 20),
-    )(tokens, cotangent, mixed, gain, dn, own, bc, mine, shared)
+    )(tokens, cotangent, early, mixed, gain, dn, own, bc, mine, shared)
 
 
 def exit_kernel(
     dn_ref, normed_ref, dpre_ref, cot_ref, gn_ref, dtaps_ref, dbias_ref, dhead_ref, dchan_ref, dgain_ref,
     dn_out, own_out, bc_out, mine_out, shared_out,
+    dn, normed, dpre, cot, gn, fetch_sem,
     gin_ref, gout_ref, mine_ref, shared_ref,
-    z_held, z_got, near_in, near_out, far_in, far_out, got_in, got_out, mine_got, shared_got, shared_held, shared_z,
+    z_got, near_in, near_out, far_in, far_out, got_in, got_out, mine_got, shared_got, shared_held, shared_z,
     bc_held, bc_got,
     zs, zr, ns, nr, fs, fr, ms, mr, ss, sr, ts, tr, bs, br,
     *, n_tp, n_fs,
@@ -737,6 +912,14 @@
     chan = gout_ref.shape[1]
     cols = gin_ref.shape[1]
     width = gin_ref.shape[0]
+    fetches = [
+        pltpu.make_async_copy(source, target, fetch_sem.at[k])
+        for k, (source, target) in enumerate(
+            [(normed_ref, normed), (dpre_ref, dpre), (cot_ref, cot), (gn_ref, gn), (dn_ref, dn)]
+        )
+    ]
+    for fetch in fetches:
+        fetch.start()
     fill_rows(
         mine_ref, [(dtaps_ref, tap, 0, chan) for tap in range(4)] + [(dbias_ref, 0, 0, chan)]
         + [(dchan_ref, row, 0, chan) for row in range(2)] + [(dhead_ref, row, 0, LANES) for row in range(2)]
@@ -751,51 +934,14 @@
     pl.semaphore_wait(pltpu.get_barrier_semaphore(), n_fs - 1 + n_tp - 1)
 
     chunk = block // CHUNKS
-    steps = (n_tp - 1) * CHUNKS
-
-    def ahead(way, step):
-        return n_tp - 1 - step // CHUNKS if way == 0 else step // CHUNKS
-
-    def passes(way, step):
-        return ahead(way, step) > tp if way == 0 else ahead(way, step) < tp
-
-    def first(way):
-        return tp == 0 if way == 0 else tp == n_tp - 1
-
-    def local(way, step):
-        return dn_ref.at[pl.ds(pl.multiple_of(ahead(way, step) * block + step % CHUNKS * chunk, chunk), chunk)]
-
-    def pass_on(way, step, direct=False):
-        towards = tp + 1 if way == 0 else tp - 1
-        source = local(way, step) if direct else z_held.at[way, step]
-        return remote(source, z_got.at[way, step], zs.at[way, step], zr.at[way, step], tp=towards)
-
-    for way in range(2):
-        @pl.when(first(way))
-        def _():
-            for step in range(2):
-                pass_on(way, step, True).start()
-
-    def advance(turn):
-        for way in range(2):
-            lag = jnp.maximum(tp - 1 if way == 0 else n_tp - 2 - tp, 0)
-            step = turn - lag
-            live = jnp.logical_and(step >= 0, step < steps)
-
-            @pl.when(jnp.logical_and(first(way), live))
-            def _():
-                pass_on(way, step, True).wait_send()
-
-                @pl.when(step + 2 < steps)
-                def _():
-                    pass_on(way, step + 2, True).start()
-
-            @pl.when(jnp.logical_and(jnp.logical_and(passes(way, step), live), jnp.logical_not(first(way))))
-            def _():
-                pass_on(way, step).wait_recv()
-                add_into(z_held.at[way, step], local(way, step), z_got.at[way, step])
-                pass_on(way, step).start()
-
+    sums = LineSum(
+        tp, n_tp, CHUNKS, lambda index, part: chunk_of(dn, index, block, part, chunk),
+        lambda index, part: chunk_of(dn_ref, index, block, part, chunk), z_got, zs, zr,
+    )
+    sums.kick()
+    for k in (0, 1):
+        fetches[k].wait()
+    advance = sums.advance
     parts = (
         (gin_ref, slice(2 * chan, cols), near_in, far_in, got_in),
         (gout_ref, slice(0, chan), near_out, far_out, got_out),
@@ -831,7 +977,7 @@
 
     def differentiate(j):
         _, span, *_ = parts[j]
-        left, right, target = (cot_ref, gn_ref, gout_ref) if j == 1 else (normed_ref, dpre_ref, gin_ref)
+        left, right, target = (cot, gn, gout_ref) if j == 1 else (normed, dpre, gin_ref)
         tile = 256
 
         @pl.loop(0, width // tile)
@@ -852,6 +998,8 @@
         near(j, 0).wait_recv()
 
     differentiate(0)
+    for k in (2, 3, 4):
+        fetches[k].wait()
     advance(0)
     differentiate(1)
     send_sums(0)
@@ -864,7 +1012,7 @@
     advance(3)
     send_sums(3)
     at = 3
-    turns = steps + max(n_tp - 3, 0)
+    turns = sums.turns
     for d in range(1, n_fs):
         for copy in small(d):
             copy.wait_recv()
@@ -876,7 +1024,7 @@
     shared_z[tp] = again
     for d in range(1, n_tp):
         remote(shared_held, shared_z.at[tp], ts.at[d], tr.at[d], tp=(tp + d) % n_tp).start()
-    pl.loop(at + 1, at + 5)(advance)
+    pl.loop(at + 1, turns)(advance)
 
     def settle(j, target, span):
         source, _, held, _, got = parts[j]
@@ -891,7 +1039,6 @@
     bc_got[tp] = bc_held[...]
     for d in range(1, n_tp):
         remote(bc_held, bc_got.at[tp], bs.at[d], br.at[d], tp=(tp + d) % n_tp).start()
-    pl.loop(at + 5, turns)(advance)
     settle(0, own_out.at[:, 2 * chan:2 * chan + LANES], slice(2 * chan + 2 * STATE, cols))
     for j in (1, 2, 3):
         for d in order:
@@ -909,30 +1056,8 @@
     shared_out[...] = total
     add_into(bc_out, *[bc_got.at[peer] for peer in range(n_tp)])
 
-    own = rows_at(dn_ref, tp, block)
-    for way in range(2):
-        for step in range(steps):
-            @pl.when(jnp.logical_and(ahead(way, step) == tp, jnp.logical_not(first(way))))
-            def _():
-                pass_on(way, step).wait_recv()
-
-    for value in range(n_tp):
-        @pl.when(tp == value)
-        def _():
-            for part in range(CHUNKS):
-                span = pl.ds(part * chunk, chunk)
-                incoming = []
-                if value > 0:
-                    incoming.append(z_got.at[0, (n_tp - 1 - value) * CHUNKS + part])
-                if value < n_tp - 1:
-                    incoming.append(z_got.at[1, value * CHUNKS + part])
-                add_into(dn_out.at[span], own.at[span], *incoming)
-
-    for way in range(2):
-        for step in range(steps):
-            @pl.when(jnp.logical_and(passes(way, step), jnp.logical_not(first(way))))
-            def _():
-                pass_on(way, step).wait_send()
+    sums.settle(lambda part: dn_out.at[pl.ds(part * chunk, chunk)])
+    sums.drain()
     for j in range(4):
         for d in range(chips):
             near(j, d).wait_send()
@@ -958,18 +1083,18 @@
     up = lambda n: -(-n // 8) * 8
     mine = (up(7 * chan // LANES + 2), LANES)
     shared = (up((10 * STATE + width) // LANES), LANES)
-    outs = [
-        shape(block, width), shape(count, 3 * chan + LANES), shape(count, 2 * STATE), shape(*mine), shape(*shared),
-    ]
+    low = lambda *extents: jax.ShapeDtypeStruct(extents, BF16)
+    outs = [low(block, width), low(count, 3 * chan + LANES), low(count, 2 * STATE), shape(*mine), shape(*shared)]
     return pl.pallas_call(
         functools.partial(exit_kernel, n_tp=n_tp, n_fs=n_fs),
         name="exit",
-        in_specs=[vmem] * 10,
+        in_specs=[pl.BlockSpec(memory_space=pl.ANY)] * 5 + [vmem] * 5,
         out_specs=[vmem] * len(outs),
         out_shape=outs,
         scratch_shapes=[
+            room(*dn.shape), room(*normed.shape), room(*dpre.shape), room(*cot.shape), room(*gnormed.shape), dma((5,)),
             room(width, cols), room(width, chan), pltpu.VMEM(mine, F32), pltpu.VMEM(shared, F32),
-            room(2, steps, block // CHUNKS, width), room(2, steps, block // CHUNKS, width),
+            room(2, steps, block // CHUNKS, width),
             room(chips, count, cols), room(chips, count, chan), room(chips, count, cols), room(chips, count, chan),
             room(chips, count, cols), room(chips, count, chan),
             pltpu.VMEM((n_fs,) + mine, F32), pltpu.VMEM((n_fs,) + shared, F32),
@@ -991,17 +1116,20 @@
 ):
     chan, heads_here = proj_z.shape[1], proj_dt.shape[1]
     n_tp, n_fs = lax.axis_size("tp"), lax.axis_size("fsdp")
-    tok_all, cot_all, w_in, normed, pre, y, enter, dgn, gnormed, out_rows, stats, taps, bias, heads, skip, gate = ahead(
+    (
+        tok_all, cot_all, w_in, normed, pre, y, enter, dgn, gnormed, out_rows, early, stats, taps, bias, heads, skip,
+        gate,
+    ) = ahead(
         seq_start, (dt_bias, a_log, skip_gain), tokens, cotangent,
         (proj_z, proj_x, proj_bc, proj_dt.T, proj_out.T), token_valid,
         (norm_gain, conv_chan, bias_chan, conv_shared, bias_shared, gate_gain), n_tp, n_fs,
     )
-    mixed = lax.psum_scatter(out_rows, "tp", scatter_dimension=0, tiled=True)
-    dpre, dn_rows, *small = mixer_backward(
-        seq_start, tok_all, w_in, taps, bias, heads, skip, gate, pre, y, enter, dgn, stats, chan * n_tp
+    dpre, dn_rows, *small, mixed = mixer_backward(
+        seq_start, tok_all, w_in, taps, bias, heads, skip, gate, pre, y, enter, dgn, stats, out_rows, chan * n_tp,
+        n_tp,
     )
     sums = leave(dn_rows, normed, dpre, cot_all, gnormed, small, n_tp, n_fs)
-    grads = list(finish(tokens, cotangent, mixed, norm_gain, *sums, heads_here))
+    grads = list(finish(tokens, cotangent, early, mixed, norm_gain, *sums, heads_here))
     grads[6], grads[15] = grads[6].T, grads[15].T
     return tuple(grads)
 

time: 267 us -> 250 us (0.936)
  between operations: 14.1 us -> 0.75 us
    pallas_call x1, Pallas kernels: 85.4 us -> 70.4 us  [leave(): pl.pallas_call(functools.partial(exit_kernel, n_tp=n_tp, n_fs=n_fs), name...]
    pallas_call x2, Pallas kernels: 43.1 us -> 56.2 us  [the longest x1 53.7 us: mixer_backward(): pl.pallas_call(functools.partial(backward_kernel, inner=inner, n_tp=n_tp)...]
    unnamed x18 -> x20, local copies, waits for them, and re-layouts: 6.43 us -> 5.94 us
  transfers between devices with their start and end apart: 1 -> 0, of which waited for: 0 -> 0; matrix products, arithmetic and copies ran while one was open for 0% -> 0% of each run, Pallas kernels for 48% -> 0%
where the time goes in v5:
time: 250 us; the launch traced here: 249 us
  Pallas kernels  243 us (97%)
  local copies, waits for them, and re-layouts  5.94 us (2%)
    pallas_call x1, Pallas kernels, ahead(): pl.pallas_call(functools.partial(ahead_kernel, n_tp=n_tp, n_fs=n_fs, inne...  116 us
    pallas_call x1, Pallas kernels, leave(): pl.pallas_call(functools.partial(exit_kernel, n_tp=n_tp, n_fs=n_fs), name...  70.4 us
    pallas_call x1, Pallas kernels, mixer_backward(): pl.pallas_call(functools.partial(backward_kernel, inner=inner, n_tp=n_tp)...  53.7 us
    unnamed x20, local copies, waits for them, and re-layouts  5.94 us

profile of v5, /device:TPU:9, one launch (start us, length us, event | category | flops | bytes accessed | tf_op | source)
XLA Modules:
  0.0 249.3 jit_solution(10399672180831796004)
XLA Ops:
  0.7 116.0 %ahead.1 = (bf16[1024,1536]{1,0:T(8,128)(2,1)}, bf16[1024,1536]{1,0:T(8,128)(2,1)}, bf16[1536,1920]{1,0:T(8,128)(2,1)}, bf16[1024,1536]{1,0:T(8,128)(2,1)}, f32[...) custom-call(s32[4]{0:T(128)} %open_ref.3, ...), custom_call_target="tpu_custom_call" | custom-call | tf_op jit(solution)/shard_map/ahead/pallas_call | solution.py:785
  116.6 53.7 %mixer_backward.1 = (bf16[1024,1920]{1,0:T(8,128)(2,1)}, bf16[1024,1536]{1,0:T(8,128)(2,1)}, f32[8,1024]{1,0:T(8,128)}, f32[1,1024]{1,0:T(1,128)}, f32[8,128]{1,...) custom-call(s32[4]{0:T(128)} %open_ref.3, bf16[1024,1536]{1,0:T(8,128)(2,1)} %get-tuple-element.63.tok_ref, ...), custom_call_target="tpu_custom_call" | custom-call | flops 12079595520 | bytes 23592960 | tf_op jit(solution)/shard_map/mixer_backward/pallas_call | solution.py:264
  170.4 0.0 copy-start
  170.4 0.0 copy-start.1
  170.4 0.0 copy-start.5
  170.4 0.0 copy-start.7
  170.4 70.4 %exit.1 = (bf16[256,1536]{1,0:T(8,128)(2,1)}, bf16[192,2432]{1,0:T(8,128)(2,1)}, bf16[192,256]{1,0:T(8,128)(2,1)}, f32[48,128]{1,0:T(8,128)}, f32[24,128]{1,0:T(8,128)}) custom-call(bf16[1024,1536]{1,0:T(8,128)(2,1)} %get-tuple-element.77.dn_ref, bf16[1024,1536]{1,0:T(8,128)(2,1)} %get-tuple-element.78.normed_ref, ...), custom_call_target="tpu_custom_call" | custom-call | tf_op jit(solution)/shard_map/exit/pallas_call | solution.py:1088
  240.8 0.0 copy-done
  240.8 0.0 copy-done.1
  240.8 0.0 copy-done.5
  240.9 0.0 copy-done.7
  240.9 0.0 copy-start.2
  240.9 1.3 copy-done.2
  242.1 0.0 copy-start.3
  242.1 1.2 copy-done.3
  243.3 0.0 copy-start.4
  243.3 1.1 copy-done.4
  244.5 0.0 copy-start.6
  244.5 0.9 copy-done.6
  245.3 0.0 copy-start.8
  245.3 0.7 copy-done.8
  246.1 0.0 copy-start.9
  246.1 0.7 copy-done.9
  246.8 2.5 finish.1
Async XLA Ops:
  170.4 70.4 %copy-start = (bf16[256,1536]{1,0:T(8,128)(2,1)S(1)}, bf16[256,1536]{1,0:T(8,128)(2,1)}, u32[]{:S(2)}) copy-start(bf16[256,1536]{1,0:T(8,128)(2,1)} %tok_ref.3) | copy-start | bytes 2359300
  170.4 70.4 %copy-start.1 = (bf16[256,1536]{1,0:T(8,128)(2,1)S(1)}, bf16[256,1536]{1,0:T(8,128)(2,1)}, u32[]{:S(2)}) copy-start(bf16[256,1536]{1,0:T(8,128)(2,1)} %cot_ref.3) | copy-start | bytes 2359300
  170.4 70.4 %copy-start.5 = (f32[64,1536]{1,0:T(8,128)S(1)}, f32[64,1536]{1,0:T(8,128)}, u32[]{:S(2)}) copy-start(f32[64,1536]{1,0:T(8,128)} %get-tuple-element.62.early_ref) | copy-start | bytes 1179652
  170.4 70.4 %copy-start.7 = (f32[1536]{0:T(1024)S(1)}, f32[1536]{0:T(1024)}, u32[]{:S(2)}) copy-start(f32[1536]{0:T(1024)} %gain_ref.1) | copy-start | bytes 18436
  240.9 1.3 copy-start.2
  242.1 1.2 copy-start.3
  243.3 1.1 copy-start.4
  244.5 0.9 copy-start.6
  245.3 0.7 copy-start.8
  246.1 0.7 copy-start.9

commit v6 on v5

--- a/solution.py
+++ b/solution.py
@@ -307,7 +307,7 @@
             jax.ShapeDtypeStruct((8, LANES), F32),
             jax.ShapeDtypeStruct((8, chan), F32),
             jax.ShapeDtypeStruct((1, width), F32),
-            jax.ShapeDtypeStruct((kept, width), F32),
+            jax.ShapeDtypeStruct((kept, width), BF16),
         ],
         cost_estimate=pl.CostEstimate(
             flops=4 * tokens * width * cols, bytes_accessed=tokens * cols * 12, transcendentals=tokens * chan
@@ -623,10 +623,9 @@
                     slot = rows_at(full, ((chip + chips - d) % chips) * 2 + core, count)
                     remote(slot, slot, f_send.at[j, d], f_recv.at[j, d], fsdp=partner).wait_recv()
                     remote(slot, slot, p_send.at[j, d], p_recv.at[j, d], fsdp=partner).start()
-    for step in range(n_tp - 1):
-        for way in range(2):
+    for way in range(2):
+        for step in range(n_tp - 1):
             line.finish(way, step)
-    for way in range(2):
         late.start(way, 0)
     for j, (pack, full) in enumerate(packs):
         for d in range(chips):
@@ -791,7 +790,7 @@
             shape((total, width), BF16), shape((total, width), BF16), shape((count * n_fs, cols), BF16),
             shape((total, width), BF16), shape((total, cols), F32), shape((total, chan), F32),
             shape((blocks, STATE, chan), F32), shape((total, chan), F32), shape((total, chan), BF16),
-            shape((total, width), BF16), shape((per // CHUNKS * EARLY, width), F32), shape((8, total), F32),
+            shape((total, width), BF16), shape((per // CHUNKS * EARLY, width), BF16), shape((8, total), F32),
             shape((4, wide), F32), shape((1, wide), F32),
             shape((8, LANES), F32), shape((1, chan), F32), shape((1, chan), F32),
         ],
@@ -840,6 +839,19 @@
 
 
 def finish_kernel(
+    *refs,
+):
+    sources, refs = refs[:10], refs[10:]
+    results, copies, sem = refs[:16], refs[16:26], refs[26]
+    fetches = [pltpu.make_async_copy(source, copy, sem.at[k]) for k, (source, copy) in enumerate(zip(sources, copies))]
+    for fetch in fetches:
+        fetch.start()
+    for fetch in fetches:
+        fetch.wait()
+    write_results(*copies, *results)
+
+
+def write_results(
     tok_ref, cot_ref, early_ref, mixed_ref, gain_ref, dn_ref, own_ref, bc_ref, mine_ref, shared_ref,
     output, grad_tokens, g_gain, g_z, g_x, g_bc, g_dt, g_taps, g_bias, g_taps_s, g_bias_s, g_log, g_step, g_skip, g_gate,
     g_out,
@@ -847,8 +859,8 @@
     chan, heads_here = g_z.shape[1], g_log.shape[0]
     resid = tok_ref[...].astype(F32)
     early = early_ref.shape[0]
-    output[0:early, :] = (resid[0:early, :] + early_ref[...]).astype(BF16)
-    output[early:, :] = (resid[early:, :] + mixed_ref[...]).astype(BF16)
+    output[0:early, :] = (resid[0:early, :] + early_ref[...].astype(F32)).astype(BF16)
+    output[early:, :] = (resid[early:, :] + mixed_ref[...].astype(F32)).astype(BF16)
     rstd = lax.rsqrt(jnp.mean(resid * resid, axis=1, keepdims=True) + EPSILON)
     scaled = dn_ref[...].astype(F32) * gain_ref[...].reshape(1, resid.shape[1])
     grad_tokens[...] = (
@@ -879,6 +891,7 @@
 
 
 def finish(tokens, cotangent, early, mixed, gain, dn, own, bc, mine, shared, heads_here):
+    operands = (tokens, cotangent, early, mixed, gain, dn, own, bc, mine, shared)
     rows, width = tokens.shape
     count = own.shape[0]
     chan = (own.shape[1] - LANES) // 3
@@ -891,9 +904,11 @@
         shape(chan), shape(count, chan),
     ]
     return pl.pallas_call(
-        finish_kernel, name="finish", in_specs=[vmem] * 10, out_specs=[vmem] * len(outs), out_shape=outs,
-        compiler_params=pltpu.CompilerParams(vmem_limit_bytes=40 << 20),
-    )(tokens, cotangent, early, mixed, gain, dn, own, bc, mine, shared)
+        finish_kernel, name="finish", in_specs=[pl.BlockSpec(memory_space=pltpu.HBM)] * 10,
+        out_specs=[vmem] * len(outs), out_shape=outs,
+        scratch_shapes=[pltpu.VMEM(v.shape, v.dtype) for v in operands] + [pltpu.SemaphoreType.DMA((10,))],
+        compiler_params=pltpu.CompilerParams(vmem_limit_bytes=63 << 20),
+    )(*operands)
 
 
 def exit_kernel(

time: 250 us -> 246 us (0.984)
  local copies, waits for them, and re-layouts: 5.94 us -> 0 us
    unnamed x20 -> x0, local copies, waits for them, and re-layouts: 5.94 us -> none
where the time goes in v6:
time: 246 us
  Pallas kernels  245 us (100%)
    pallas_call x1, Pallas kernels, ahead(): pl.pallas_call(functools.partial(ahead_kernel, n_tp=n_tp, n_fs=n_fs, inne...  116 us
    pallas_call x1, Pallas kernels, leave(): pl.pallas_call(functools.partial(exit_kernel, n_tp=n_tp, n_fs=n_fs), name...  69.9 us
    pallas_call x1, Pallas kernels, mixer_backward(): pl.pallas_call(functools.partial(backward_kernel, inner=inner, n_tp=n_tp)...  53.8 us

profile of v6, /device:TPU:9, one launch (start us, length us, event | category | flops | bytes accessed | tf_op | source)
XLA Modules:
  0.0 245.5 jit_solution(17434473901262105661)
XLA Ops:
  0.7 116.2 %ahead.1 = (bf16[1024,1536]{1,0:T(8,128)(2,1)}, bf16[1024,1536]{1,0:T(8,128)(2,1)}, bf16[1536,1920]{1,0:T(8,128)(2,1)}, bf16[1024,1536]{1,0:T(8,128)(2,1)}, f32[...) custom-call(s32[4]{0:T(128)} %open_ref.3, ...), custom_call_target="tpu_custom_call" | custom-call | tf_op jit(solution)/shard_map/ahead/pallas_call | solution.py:784
  116.9 53.8 %mixer_backward.1 = (bf16[1024,1920]{1,0:T(8,128)(2,1)}, bf16[1024,1536]{1,0:T(8,128)(2,1)}, f32[8,1024]{1,0:T(8,128)}, f32[1,1024]{1,0:T(1,128)}, f32[8,128]{1,...) custom-call(s32[4]{0:T(128)} %open_ref.3, ...), custom_call_target="tpu_custom_call" | custom-call | flops 12079595520 | bytes 23592960 | tf_op jit(solution)/shard_map/mixer_backward/pallas_call | solution.py:264
  170.7 69.9 %exit.1 = (bf16[256,1536]{1,0:T(8,128)(2,1)}, bf16[192,2432]{1,0:T(8,128)(2,1)}, bf16[192,256]{1,0:T(8,128)(2,1)}, f32[48,128]{1,0:T(8,128)}, f32[24,128]{1,0:T(8,128)}) custom-call(bf16[1024,1536]{1,0:T(8,128)(2,1)} %get-tuple-element.77.dn_ref, bf16[1024,1536]{1,0:T(8,128)(2,1)} %get-tuple-element.78.normed_ref, ...), custom_call_target="tpu_custom_call" | custom-call | tf_op jit(solution)/shard_map/exit/pallas_call | solution.py:1103
  240.6 4.7 %finish.1 = (bf16[256,1536]{1,0:T(8,128)(2,1)}, bf16[256,1536]{1,0:T(8,128)(2,1)}, f32[1536]{0:T(1024)}, f32[192,768]{1,0:T(8,128)}, f32[192,768]{1,0:T(8,128)},...) custom-call(bf16[256,1536]{1,0:T(8,128)(2,1)} %refs_0_.1, ...), custom_call_target="tpu_custom_call" | custom-call | tf_op jit(solution)/shard_map/finish/pallas_call | solution.py:906

commit v7 on v6

--- a/solution.py
+++ b/solution.py
@@ -342,36 +342,42 @@
 
 
 class Line:
-    def __init__(self, tp, n_tp, own, whole_ref, send, recv):
+    def __init__(self, tp, n_tp, own, whole_ref, send, recv, split=1):
         self.tp, self.n, self.own, self.whole_ref, self.send, self.recv = tp, n_tp, own, whole_ref, send, recv
         self.count = own.shape[0]
+        self.split, self.part = split, own.shape[0] // split
+
+    def piece(self, index, step):
+        return self.whole_ref.at[
+            pl.ds(pl.multiple_of(index * self.count + step % self.split * self.part, self.part), self.part)
+        ]
 
     def copy(self, way, step, own=False):
         shift = -1 if way == 0 else 1
-        index = self.tp + shift * step
-        slot = rows_at(self.whole_ref, index, self.count)
-        return remote(
-            self.own if own else slot, slot, self.send.at[way, step], self.recv.at[way, step], tp=self.tp - shift
-        )
+        slot = self.piece(self.tp + shift * (step // self.split), step)
+        source = self.own.at[pl.ds(step % self.split * self.part, self.part)] if own else slot
+        return remote(source, slot, self.send.at[way, step], self.recv.at[way, step], tp=self.tp - shift)
 
     def sends(self, way, step):
+        step = step // self.split
         if way == 0:
             return jnp.logical_and(self.tp < self.n - 1, self.tp >= step)
         return jnp.logical_and(self.tp > 0, self.tp + step <= self.n - 1)
 
     def takes(self, way, step):
+        step = step // self.split
         return self.tp >= step + 1 if way == 0 else self.tp + step + 1 <= self.n - 1
 
     def start(self, way, step):
         @pl.when(self.sends(way, step))
         def _():
-            self.copy(way, step, own=step == 0).start()
+            self.copy(way, step, own=step < self.split).start()
 
     def arrive(self, way, step):
         @pl.when(self.takes(way, step))
         def _():
             shift = -1 if way == 0 else 1
-            slot = rows_at(self.whole_ref, self.tp + shift * (step + 1), self.count)
+            slot = self.piece(self.tp + shift * (step // self.split + 1), step)
             remote(
                 slot, slot, self.send.at[way, step], self.recv.at[way, step], tp=self.tp + shift
             ).wait_recv()
@@ -379,7 +385,7 @@
     def finish(self, way, step):
         @pl.when(self.sends(way, step))
         def _():
-            self.copy(way, step, own=step == 0).wait_send()
+            self.copy(way, step, own=step < self.split).wait_send()
 
 
 class LineSum:
@@ -575,7 +581,7 @@
 
     packs = ((pin_ref, w_in), (pout_ref, w_out))
     count = pin_ref.shape[0]
-    line = Line(tp, n_tp, tok_ref, tok_all, z_send, z_recv)
+    line = Line(tp, n_tp, tok_ref, tok_all, z_send, z_recv, split=2)
     late = Line(tp, n_tp, cot_ref, cot_all, c_send, c_recv)
     for way in range(2):
         line.start(way, 0)
@@ -612,21 +618,24 @@
     taps_ref[:, chan:] = conv_shared[...]
     bias_ref[:, :chan] = bias_chan[...].reshape(1, chan)
     bias_ref[:, chan:] = bias_shared[...].reshape(1, 2 * STATE)
-    for step in range(n_tp - 1):
+    last = 2 * (n_tp - 1)
+    for step in range(1, last):
         for way in range(2):
-            line.arrive(way, step)
-            if step + 1 < n_tp - 1:
-                line.start(way, step + 1)
-        if step == n_tp - 3 or n_tp < 3 and step == 0:
-            for j, (pack, full) in enumerate(packs):
-                for d in range(1, chips):
-                    slot = rows_at(full, ((chip + chips - d) % chips) * 2 + core, count)
-                    remote(slot, slot, f_send.at[j, d], f_recv.at[j, d], fsdp=partner).wait_recv()
-                    remote(slot, slot, p_send.at[j, d], p_recv.at[j, d], fsdp=partner).start()
+            if step >= 2:
+                line.arrive(way, step - 2)
+            line.finish(way, step - 1)
+            line.start(way, step)
+    for j, (pack, full) in enumerate(packs):
+        for d in range(1, chips):
+            slot = rows_at(full, ((chip + chips - d) % chips) * 2 + core, count)
+            remote(slot, slot, f_send.at[j, d], f_recv.at[j, d], fsdp=partner).wait_recv()
+            remote(slot, slot, p_send.at[j, d], p_recv.at[j, d], fsdp=partner).start()
     for way in range(2):
-        for step in range(n_tp - 1):
-            line.finish(way, step)
+        line.finish(way, last - 1)
         late.start(way, 0)
+    for way in range(2):
+        line.arrive(way, last - 2)
+        line.arrive(way, last - 1)
     for j, (pack, full) in enumerate(packs):
         for d in range(chips):
             slot = rows_at(full, ((chip + chips - d) % chips) * 2 + 1 - core, count)
@@ -805,7 +814,7 @@
             pltpu.VMEM((8, total), F32), pltpu.VMEM((8, total), F32),
             pltpu.VMEM((n_tp, 8, total), F32), pltpu.VMEM((n_tp, 8, total), F32),
             pltpu.VMEM((2, (n_tp - 1) * EARLY, per // CHUNKS, width), BF16),
-            dma((4,)), dma((2, n_tp - 1)), dma((2, n_tp - 1)), dma((2, n_tp - 1)), dma((2, n_tp - 1)),
+            dma((4,)), dma((2, 2 * (n_tp - 1))), dma((2, 2 * (n_tp - 1))), dma((2, n_tp - 1)), dma((2, n_tp - 1)),
             dma((2, chips)), dma((2, chips)), dma((2, chips)), dma((2, chips)),
             dma((n_tp,)), dma((n_tp,)), dma((n_tp,)), dma((n_tp,)), dma((2,)), dma((8, blocks)),
             dma((2, (n_tp - 1) * EARLY)), dma((2, (n_tp - 1) * EARLY)),

time: 246 us -> 244 us (level)
  Pallas kernels: 245 us -> 241 us
where the time goes in v7:
time: 244 us; the launch traced here: 242 us
  Pallas kernels  241 us (99%)
    pallas_call x1, Pallas kernels, ahead(): pl.pallas_call(functools.partial(ahead_kernel, n_tp=n_tp, n_fs=n_fs, inne...  114 us
    pallas_call x1, Pallas kernels, leave(): pl.pallas_call(functools.partial(exit_kernel, n_tp=n_tp, n_fs=n_fs), name...  68.4 us
    pallas_call x1, Pallas kernels, mixer_backward(): pl.pallas_call(functools.partial(backward_kernel, inner=inner, n_tp=n_tp)...  54.3 us

profile of v7, /device:TPU:9, one launch (start us, length us, event | category | flops | bytes accessed | tf_op | source)
XLA Modules:
  0.0 242.2 jit_solution(10045476707361337345)
XLA Ops:
  0.7 114.0 %ahead.1 = (bf16[1024,1536]{1,0:T(8,128)(2,1)}, bf16[1024,1536]{1,0:T(8,128)(2,1)}, bf16[1536,1920]{1,0:T(8,128)(2,1)}, bf16[1024,1536]{1,0:T(8,128)(2,1)}, f32[...) custom-call(s32[4]{0:T(128)} %open_ref.3, ...), custom_call_target="tpu_custom_call" | custom-call | tf_op jit(solution)/shard_map/ahead/pallas_call | solution.py:793
  114.6 54.3 %mixer_backward.1 = (bf16[1024,1920]{1,0:T(8,128)(2,1)}, bf16[1024,1536]{1,0:T(8,128)(2,1)}, f32[8,1024]{1,0:T(8,128)}, f32[1,1024]{1,0:T(1,128)}, f32[8,128]{1,...) custom-call(s32[4]{0:T(128)} %open_ref.3, ...), custom_call_target="tpu_custom_call" | custom-call | flops 12079595520 | bytes 23592960 | tf_op jit(solution)/shard_map/mixer_backward/pallas_call | solution.py:264
  168.9 68.4 %exit.1 = (bf16[256,1536]{1,0:T(8,128)(2,1)}, bf16[192,2432]{1,0:T(8,128)(2,1)}, bf16[192,256]{1,0:T(8,128)(2,1)}, f32[48,128]{1,0:T(8,128)}, f32[24,128]{1,0:T(8,128)}) custom-call(bf16[1024,1536]{1,0:T(8,128)(2,1)} %get-tuple-element.77.dn_ref, bf16[1024,1536]{1,0:T(8,128)(2,1)} %get-tuple-element.78.normed_ref, ...), custom_call_target="tpu_custom_call" | custom-call | tf_op jit(solution)/shard_map/exit/pallas_call | solution.py:1112
  237.3 4.7 %finish.1 = (bf16[256,1536]{1,0:T(8,128)(2,1)}, bf16[256,1536]{1,0:T(8,128)(2,1)}, f32[1536]{0:T(1024)}, f32[192,768]{1,0:T(8,128)}, f32[192,768]{1,0:T(8,128)},...) custom-call(bf16[256,1536]{1,0:T(8,128)(2,1)} %refs_0_.1, ...), custom_call_target="tpu_custom_call" | custom-call | tf_op jit(solution)/shard_map/finish/pallas_call | solution.py:915

commit v8 on v7

--- a/solution.py
+++ b/solution.py
@@ -322,6 +322,7 @@
 MESH = pl.DeviceIdType.MESH
 CHUNKS = 4
 EARLY = 1
+LARGE = (0, 1, 3, 4, 5, 15)
 TAGS = {"ahead": 1, "backward": 2, "exit": 3}
 
 
@@ -419,7 +420,7 @@
         for way in range(2):
             @pl.when(self.first(way))
             def _():
-                for step in range(min(2, self.steps) if self.paced else self.steps):
+                for step in range(min(3, self.steps) if self.paced else self.steps):
                     self.copy(way, step, True).start()
 
     def advance(self, turn):
@@ -432,13 +433,13 @@
             def _():
                 self.copy(way, step, True).wait_send()
 
-                @pl.when(step + 2 < self.steps)
+                @pl.when(step + 3 < self.steps)
                 def _():
-                    self.copy(way, step + 2, True).start()
+                    self.copy(way, step + 3, True).start()
 
                 @pl.when(step == self.paced - 1)
                 def _():
-                    for rest in range(self.paced + 2, self.steps):
+                    for rest in range(self.paced + 3, self.steps):
                         self.copy(way, rest, True).start()
 
             @pl.when(jnp.logical_and(jnp.logical_and(self.passes(way, step), live), jnp.logical_not(self.first(way))))
@@ -568,6 +569,8 @@
     blocks = tok_all.shape[0] // STRETCH
     per = tok_ref.shape[0]
     chan = pout_ref.shape[1]
+    greet("fsdp", [((chip + d) % chips) * 2 + core for d in range(1, chips)] + [partner])
+    greet("tp", [(tp + d) % n_tp for d in range(1, n_tp)])
     pin_ref[:, :chan] = pz_ref[...]
     pin_ref[:, chan:2 * chan] = px_ref[...]
     pin_ref[:, 2 * chan:2 * chan + 2 * STATE] = pbc_ref[...]
@@ -575,8 +578,6 @@
     pin_ref[:, 2 * chan + 2 * STATE:] = jnp.concatenate(
         [pdt_ref[...].astype(F32), jnp.zeros((LANES - heads_here, rows_dt), F32)], axis=0
     ).T.astype(BF16)
-    greet("fsdp", [((chip + d) % chips) * 2 + core for d in range(1, chips)] + [partner])
-    greet("tp", [(tp + d) % n_tp for d in range(1, n_tp)])
     pl.semaphore_wait(pltpu.get_barrier_semaphore(), chips + n_tp - 1)
 
     packs = ((pin_ref, w_in), (pout_ref, w_out))
@@ -851,31 +852,35 @@
     *refs,
 ):
     sources, refs = refs[:10], refs[10:]
-    results, copies, sem = refs[:16], refs[16:26], refs[26]
+    results, copies, held, sem, out_sem = list(refs[:16]), refs[16:26], refs[26:32], refs[32], refs[33]
     fetches = [pltpu.make_async_copy(source, copy, sem.at[k]) for k, (source, copy) in enumerate(zip(sources, copies))]
-    for fetch in fetches:
-        fetch.start()
-    for fetch in fetches:
-        fetch.wait()
-    write_results(*copies, *results)
-
-
-def write_results(
-    tok_ref, cot_ref, early_ref, mixed_ref, gain_ref, dn_ref, own_ref, bc_ref, mine_ref, shared_ref,
-    output, grad_tokens, g_gain, g_z, g_x, g_bc, g_dt, g_taps, g_bias, g_taps_s, g_bias_s, g_log, g_step, g_skip, g_gate,
-    g_out,
+    for k in (6, 7, 8, 9, 5, 0, 1, 2, 3, 4):
+        fetches[k].start()
+    stores = [pltpu.make_async_copy(held[k], results[n], out_sem.at[k]) for k, n in enumerate(LARGE)]
+    for k, n in enumerate(LARGE):
+        results[n] = held[k]
+    for k in (6, 7, 8, 9):
+        fetches[k].wait()
+    write_grads(*copies[6:], *results[3:])
+    for store in stores[2:]:
+        store.start()
+    for k in range(6):
+        fetches[k].wait()
+    write_tokens(*copies[:6], *results[:2])
+    for store in stores[:2]:
+        store.start()
+    results[2][...] = jnp.concatenate(
+        [copies[9][10 + k:11 + k, :] for k in range(results[2].shape[0] // LANES)], axis=1
+    ).reshape(results[2].shape[0])
+    for store in stores:
+        store.wait()
+
+
+def write_grads(
+    own_ref, bc_ref, mine_ref, shared_ref,
+    g_z, g_x, g_bc, g_dt, g_taps, g_bias, g_taps_s, g_bias_s, g_log, g_step, g_skip, g_gate, g_out,
 ):
     chan, heads_here = g_z.shape[1], g_log.shape[0]
-    resid = tok_ref[...].astype(F32)
-    early = early_ref.shape[0]
-    output[0:early, :] = (resid[0:early, :] + early_ref[...].astype(F32)).astype(BF16)
-    output[early:, :] = (resid[early:, :] + mixed_ref[...].astype(F32)).astype(BF16)
-    rstd = lax.rsqrt(jnp.mean(resid * resid, axis=1, keepdims=True) + EPSILON)
-    scaled = dn_ref[...].astype(F32) * gain_ref[...].reshape(1, resid.shape[1])
-    grad_tokens[...] = (
-        cot_ref[...].astype(F32) + rstd * scaled
-        - resid * (rstd * rstd * rstd) * jnp.mean(scaled * resid, axis=1, keepdims=True)
-    ).astype(BF16)
     g_z[...] = own_ref[:, :chan].astype(F32)
     g_x[...] = own_ref[:, chan:2 * chan].astype(F32)
     g_dt[...] = own_ref[:, 2 * chan:2 * chan + LANES].astype(F32).T[0:heads_here, :]
@@ -896,7 +901,19 @@
     g_log[...] = mine_ref[7 * per:7 * per + 1, :heads_here].reshape(heads_here)
     g_step[...] = mine_ref[7 * per + 1:7 * per + 2, :heads_here].reshape(heads_here)
     g_bias_s[...] = row(shared_ref, 8, 2 * STATE).reshape(2 * STATE)
-    g_gain[...] = row(shared_ref, 10, g_gain.shape[0]).reshape(g_gain.shape[0])
+
+
+def write_tokens(tok_ref, cot_ref, early_ref, mixed_ref, gain_ref, dn_ref, output, grad_tokens):
+    resid = tok_ref[...].astype(F32)
+    early = early_ref.shape[0]
+    output[0:early, :] = (resid[0:early, :] + early_ref[...].astype(F32)).astype(BF16)
+    output[early:, :] = (resid[early:, :] + mixed_ref[...].astype(F32)).astype(BF16)
+    rstd = lax.rsqrt(jnp.mean(resid * resid, axis=1, keepdims=True) + EPSILON)
+    scaled = dn_ref[...].astype(F32) * gain_ref[...].reshape(1, resid.shape[1])
+    grad_tokens[...] = (
+        cot_ref[...].astype(F32) + rstd * scaled
+        - resid * (rstd * rstd * rstd) * jnp.mean(scaled * resid, axis=1, keepdims=True)
+    ).astype(BF16)
 
 
 def finish(tokens, cotangent, early, mixed, gain, dn, own, bc, mine, shared, heads_here):
@@ -914,8 +931,10 @@
     ]
     return pl.pallas_call(
         finish_kernel, name="finish", in_specs=[pl.BlockSpec(memory_space=pltpu.HBM)] * 10,
-        out_specs=[vmem] * len(outs), out_shape=outs,
-        scratch_shapes=[pltpu.VMEM(v.shape, v.dtype) for v in operands] + [pltpu.SemaphoreType.DMA((10,))],
+        out_specs=[pl.BlockSpec(memory_space=pl.ANY) if n in LARGE else vmem for n in range(len(outs))], out_shape=outs,
+        scratch_shapes=[pltpu.VMEM(v.shape, v.dtype) for v in operands]
+        + [pltpu.VMEM(outs[n].shape, outs[n].dtype) for n in LARGE]
+        + [pltpu.SemaphoreType.DMA((10,)), pltpu.SemaphoreType.DMA((6,))],
         compiler_params=pltpu.CompilerParams(vmem_limit_bytes=63 << 20),
     )(*operands)
 
@@ -933,6 +952,8 @@
     tp, me = lax.axis_index("tp"), lax.axis_index("fsdp")
     chip, core, chips = me // 2, me % 2, n_fs // 2
     partner = chip * 2 + 1 - core
+    greet("fsdp", [(me + d) % n_fs for d in range(1, n_fs)])
+    greet("tp", [(tp + d) % n_tp for d in range(1, n_tp)])
     chan = gout_ref.shape[1]
     cols = gin_ref.shape[1]
     width = gin_ref.shape[0]
@@ -953,8 +974,6 @@
         + [(dgain_ref, 0, 0, width)]
     )
     block, count = dn_out.shape[0], own_out.shape[0]
-    greet("fsdp", [(me + d) % n_fs for d in range(1, n_fs)])
-    greet("tp", [(tp + d) % n_tp for d in range(1, n_tp)])
     pl.semaphore_wait(pltpu.get_barrier_semaphore(), n_fs - 1 + n_tp - 1)
 
     chunk = block // CHUNKS

time: 244 us -> 243 us (level)
  no operation moved by 1% of the time
where the time goes in v8:
time: 243 us; the launch traced here: 242 us
  Pallas kernels  241 us (99%)
    pallas_call x1, Pallas kernels, ahead(): pl.pallas_call(functools.partial(ahead_kernel, n_tp=n_tp, n_fs=n_fs, inne...  114 us
    pallas_call x1, Pallas kernels, leave(): pl.pallas_call(functools.partial(exit_kernel, n_tp=n_tp, n_fs=n_fs), name...  68.1 us
    pallas_call x1, Pallas kernels, mixer_backward(): pl.pallas_call(functools.partial(backward_kernel, inner=inner, n_tp=n_tp)...  54.3 us

profile of v8, /device:TPU:9, one launch (start us, length us, event | category | flops | bytes accessed | tf_op | source)
XLA Modules:
  0.0 241.8 jit_solution(17477904652557408330)
XLA Ops:
  0.7 113.9 %ahead.1 = (bf16[1024,1536]{1,0:T(8,128)(2,1)}, bf16[1024,1536]{1,0:T(8,128)(2,1)}, bf16[1536,1920]{1,0:T(8,128)(2,1)}, bf16[1024,1536]{1,0:T(8,128)(2,1)}, f32[...) custom-call(s32[4]{0:T(128)} %open_ref.3, ...), custom_call_target="tpu_custom_call" | custom-call | tf_op jit(solution)/shard_map/ahead/pallas_call | solution.py:794
  114.6 54.3 %mixer_backward.1 = (bf16[1024,1920]{1,0:T(8,128)(2,1)}, bf16[1024,1536]{1,0:T(8,128)(2,1)}, f32[8,1024]{1,0:T(8,128)}, f32[1,1024]{1,0:T(1,128)}, f32[8,128]{1,...) custom-call(s32[4]{0:T(128)} %open_ref.3, ...), custom_call_target="tpu_custom_call" | custom-call | flops 12079595520 | bytes 23592960 | tf_op jit(solution)/shard_map/mixer_backward/pallas_call | solution.py:264
  168.8 68.1 %exit.1 = (bf16[256,1536]{1,0:T(8,128)(2,1)}, bf16[192,2432]{1,0:T(8,128)(2,1)}, bf16[192,256]{1,0:T(8,128)(2,1)}, f32[48,128]{1,0:T(8,128)}, f32[24,128]{1,0:T(8,128)}) custom-call(bf16[1024,1536]{1,0:T(8,128)(2,1)} %get-tuple-element.77.dn_ref, bf16[1024,1536]{1,0:T(8,128)(2,1)} %get-tuple-element.78.normed_ref, ...), custom_call_target="tpu_custom_call" | custom-call | tf_op jit(solution)/shard_map/exit/pallas_call | solution.py:1131
  237.0 4.7 %finish.1 = (bf16[256,1536]{1,0:T(8,128)(2,1)}, bf16[256,1536]{1,0:T(8,128)(2,1)}, f32[1536]{0:T(1024)}, f32[192,768]{1,0:T(8,128)}, f32[192,768]{1,0:T(8,128)},...) custom-call(bf16[256,1536]{1,0:T(8,128)(2,1)} %refs_0_.1, ...), custom_call_target="tpu_custom_call" | custom-call | tf_op jit(solution)/shard_map/finish/pallas_call | solution.py:932
